TPU v7x, 32 devices: a whole 2x2x4 slice. The times are simulated.
32 devices in a mesh: fsdp: 16 (over z, y, x), sp: 2 (over core).
Axes of the slice: x: 2, y: 2, z: 4, core: 2. Of those that a mesh axis runs over, the one named last changes fastest.
Arguments:
- tokens: bfloat16 [4096, 1536], P(('fsdp', 'sp')), may hold values from -6 to 6
- text: bfloat16 [8192, 1536], P(('fsdp', 'sp')), may hold values from -6 to 6
- clip_frames: int32 [16], P('fsdp'), may hold values from 1 to 4, as said below
- timestep: int32 [16, 4], P('fsdp'), may hold values from 0 to 999
- mod_weight: bfloat16 [1, 256, 9216], P(None, 'fsdp'), may hold values from -0.375 to 0.375
- mod_bias: bfloat16 [1, 9216], P(None, 'fsdp'), may hold values from -3 to 3
- qk_gains: bfloat16 [1, 4, 1536], P(None, None, 'fsdp'), may hold values from 0.099609375 to 1.8984375
- self_in: bfloat16 [1, 1536, 4608], P(None, 'fsdp'), may hold values from -0.15625 to 0.15625
- self_out: bfloat16 [1, 1536, 1536], P(None, 'fsdp'), may hold values from -1.25 to 1.25
- cross_q: bfloat16 [1, 1536, 1536], P(None, 'fsdp'), may hold values from -0.15625 to 0.15625
- cross_kv: bfloat16 [1, 1536, 3072], P(None, 'fsdp'), may hold values from -0.15625 to 0.15625
- cross_out: bfloat16 [1, 1536, 1536], P(None, 'fsdp'), may hold values from -1.25 to 1.25
- mlp_in: bfloat16 [1, 1536, 8960], P(None, 'fsdp'), may hold values from -0.15625 to 0.15625
- mlp_out: bfloat16 [1, 8960, 1536], P(None, 'fsdp'), may hold values from -0.0625 to 0.0625
- cotangent: bfloat16 [4096, 1536], P(('fsdp', 'sp')), may hold values from -6 to 6
Outputs:
- output: bfloat16 [4096, 1536], P(('fsdp', 'sp'))
- tokens_grad: float32 [4096, 1536], P(('fsdp', 'sp'))
- mod_weight_grad: float32 [1, 256, 9216], P(None, 'fsdp')
- mod_bias_grad: float32 [1, 9216], P(None, 'fsdp')
- qk_gains_grad: float32 [1, 4, 1536], P(None, None, 'fsdp')
- self_in_grad: float32 [1, 1536, 4608], P(None, 'fsdp')
- self_out_grad: float32 [1, 1536, 1536], P(None, 'fsdp')
- cross_q_grad: float32 [1, 1536, 1536], P(None, 'fsdp')
- cross_kv_grad: float32 [1, 1536, 3072], P(None, 'fsdp')
- cross_out_grad: float32 [1, 1536, 1536], P(None, 'fsdp')
- mlp_in_grad: float32 [1, 1536, 8960], P(None, 'fsdp')
- mlp_out_grad: float32 [1, 8960, 1536], P(None, 'fsdp')
Inputs may be any that keep to these rules, and one draw needn't show every extreme that they name: `clip_frames`: some clip has all 4 frames live in every draw.
All inputs are finite; a program needn't handle non-finite values.
Results may differ from a plain program's by a relative error of at most 0.019.
Values may be sent and summed in bfloat16 or wider, within the bound.
A program may use at most 448 MiB of HBM per device.

v0:
```python
import math

import jax
import jax.numpy as jnp
from jax import lax
from jax.sharding import PartitionSpec as P

D = 1536
HD = 128
TXT = 512
FREQ = 256
LAYERS = 1
WP = 8
FRAME_TOK = 64


EPSILON = 1e-06
NEGATIVE = -1e30


def for_sending(value):

    def short(part):
        return part.astype(jnp.bfloat16) if part.dtype == jnp.float32 else part

    return jax.tree.map(short, value)


def product(left, right):
    return jnp.dot(left, right, preferred_element_type=jnp.float32)


def product_tn(left, right):
    return lax.dot_general(
        left, right, (((0,), (0,)), ((), ())), preferred_element_type=jnp.float32
    )


def product_nt(left, right):
    return lax.dot_general(
        left, right, (((1,), (1,)), ((), ())), preferred_element_type=jnp.float32
    )


def layer_norm(values):
    centred = values - jnp.mean(values, axis=-1, keepdims=True)
    return centred * lax.rsqrt(jnp.mean(centred * centred, axis=-1, keepdims=True) + EPSILON)


def rms_norm(values, gain):
    return values * lax.rsqrt(jnp.mean(values * values, axis=-1, keepdims=True) + EPSILON) * gain


def sinus_features(steps):
    half_dim = FREQ // 2
    rates = jnp.exp(jnp.arange(half_dim).astype(jnp.float32) * (-math.log(10000.0) / half_dim))
    angles = steps.astype(jnp.float32)[:, None] * rates[None, :]
    return jnp.concatenate([jnp.cos(angles), jnp.sin(angles)], axis=1)


def rotary_tables(frame_pos, token_spot):
    half_dim = HD // 2
    side_pairs = HD // 6
    lead_pairs = half_dim - 2 * side_pairs
    pair_index = jnp.arange(half_dim)
    log_base = -math.log(10000.0)
    lead_part = pair_index < lead_pairs
    side_part = jnp.logical_and(pair_index >= lead_pairs, pair_index < lead_pairs + side_pairs)
    last_part = pair_index >= lead_pairs + side_pairs
    frame_rate = jnp.where(
        lead_part, jnp.exp(log_base * pair_index.astype(jnp.float32) / lead_pairs), 0.0
    )
    row_rate = jnp.where(
        side_part,
        jnp.exp(log_base * (pair_index - lead_pairs).astype(jnp.float32) / side_pairs),
        0.0,
    )
    column_rate = jnp.where(
        last_part,
        jnp.exp(log_base * (pair_index - lead_pairs - side_pairs).astype(jnp.float32) / side_pairs),
        0.0,
    )
    patch_row = (token_spot // WP).astype(jnp.float32)
    patch_column = (token_spot % WP).astype(jnp.float32)
    angles = (
        frame_pos.astype(jnp.float32)[:, None] * frame_rate[None, :]
        + patch_row[:, None] * row_rate[None, :]
        + patch_column[:, None] * column_rate[None, :]
    )
    return (jnp.cos(angles), jnp.sin(angles))


def rotate(values, cosine, sine):
    row_count = values.shape[0]
    shaped = values.reshape(row_count, -1, HD)
    half_dim = HD // 2
    first_half = shaped[:, :, :half_dim]
    second_half = shaped[:, :, half_dim:]
    cos_rows = cosine[:, None, :]
    sin_rows = sine[:, None, :]
    turned = jnp.concatenate(
        [
            first_half * cos_rows - second_half * sin_rows,
            second_half * cos_rows + first_half * sin_rows,
        ],
        axis=2,
    )
    return turned.reshape(row_count, -1)


def modulated(residual, shift, scale):
    frames = shift.shape[0]
    normed = layer_norm(residual).reshape(frames, -1, residual.shape[1])
    return (normed * (1.0 + scale[:, None, :]) + shift[:, None, :]).reshape(residual.shape)


def gated_add(residual, branch, gate):
    frames = gate.shape[0]
    return residual + (branch.reshape(frames, -1, branch.shape[1]) * gate[:, None, :]).reshape(
        branch.shape
    )


def gate_scaled(grad_rows, gate):
    frames = gate.shape[0]
    return (grad_rows.reshape(frames, -1, grad_rows.shape[1]) * gate[:, None, :]).reshape(
        grad_rows.shape
    )


def frame_sum(values, frames):
    return jnp.sum(values.reshape(frames, -1, values.shape[1]), axis=1)


def self_prepare(joined, gain_query, gain_key, cosine, sine):
    query_rows = rotate(rms_norm(joined[:, :D], gain_query), cosine, sine)
    key_rows = rotate(rms_norm(joined[:, D : 2 * D], gain_key), cosine, sine)
    return (query_rows, key_rows, joined[:, 2 * D :])


def text_prepare(joined, gain_key):
    return (rms_norm(joined[:, :D], gain_key), joined[:, D:])


def split_heads(rows_in):
    return rows_in.reshape(rows_in.shape[0], -1, HD).transpose(1, 0, 2)


def join_heads(stacked):
    return stacked.transpose(1, 0, 2).reshape(stacked.shape[1], -1)


def head_scores(query_head, key_head, allowed):
    raw_scores = product_nt(query_head, key_head) * (1.0 / math.sqrt(HD))
    return jnp.where(allowed, raw_scores, NEGATIVE)


def attend_forward(query_rows, key_rows, value_rows, key_live):
    allowed = key_live[None, :]

    def one_head(pieces):
        query_head, key_head, value_head = pieces
        scores = head_scores(query_head, key_head, allowed)
        row_max = jnp.max(scores, axis=1, keepdims=True)
        log_total = row_max + jnp.log(jnp.sum(jnp.exp(scores - row_max), axis=1, keepdims=True))
        weights_low = jnp.exp(scores - log_total).astype(jnp.bfloat16)
        return (product(weights_low, value_head), log_total[:, 0])

    mixed_heads, log_totals = lax.map(
        one_head, (split_heads(query_rows), split_heads(key_rows), split_heads(value_rows))
    )
    return (join_heads(mixed_heads).astype(jnp.bfloat16), log_totals)


def attend_backward(query_rows, key_rows, value_rows, log_totals, grad_mixed, key_live):
    allowed = key_live[None, :]
    score_scale = 1.0 / math.sqrt(HD)

    def one_head(pieces):
        query_head, key_head, value_head, log_total, grad_head = pieces
        scores = head_scores(query_head, key_head, allowed)
        weights_full = jnp.exp(scores - log_total[:, None])
        grad_weights = product_nt(grad_head, value_head)
        delta = jnp.sum(weights_full * grad_weights, axis=1, keepdims=True)
        grad_scores = (weights_full * (grad_weights - delta)).astype(jnp.bfloat16)
        grad_query = product(grad_scores, key_head) * score_scale
        grad_key = product_tn(grad_scores, query_head) * score_scale
        grad_value = product_tn(weights_full.astype(jnp.bfloat16), grad_head)
        return (grad_query, grad_key, grad_value)

    grad_query, grad_key, grad_value = lax.map(
        one_head,
        (
            split_heads(query_rows),
            split_heads(key_rows),
            split_heads(value_rows),
            log_totals,
            split_heads(grad_mixed),
        ),
    )
    return (
        join_heads(grad_query).astype(jnp.bfloat16),
        join_heads(grad_key).astype(jnp.bfloat16),
        join_heads(grad_value).astype(jnp.bfloat16),
    )


def to_heads(pieces):
    return jax.tree.map(
        lambda part, own: part.astype(own.dtype),
        lax.all_to_all(for_sending(pieces), "sp", split_axis=1, concat_axis=0, tiled=True),
        pieces,
    )


def to_tokens(pieces):
    return jax.tree.map(
        lambda part, own: part.astype(own.dtype),
        lax.all_to_all(for_sending(pieces), "sp", split_axis=0, concat_axis=1, tiled=True),
        pieces,
    )


def fetch_weights(shards, block_no):
    pieces = [member[block_no] for member in shards]
    return (
        lax.all_gather(pieces[0], "fsdp", axis=0, tiled=True),
        lax.all_gather(pieces[1], "fsdp", axis=0, tiled=True),
        lax.all_gather(pieces[2], "fsdp", axis=1, tiled=True),
        lax.all_gather(pieces[3], "fsdp", axis=0, tiled=True),
        lax.all_gather(pieces[4], "fsdp", axis=0, tiled=True),
        lax.all_gather(pieces[5], "fsdp", axis=0, tiled=True),
        lax.all_gather(pieces[6], "fsdp", axis=0, tiled=True),
        lax.all_gather(pieces[7], "fsdp", axis=0, tiled=True),
        lax.all_gather(pieces[8], "fsdp", axis=0, tiled=True),
        lax.all_gather(pieces[9], "fsdp", axis=0, tiled=True),
    )


def reduce_mlp(grad_up, grad_down):
    owned = (
        lax.psum_scatter(grad_up, "fsdp", scatter_dimension=0, tiled=True),
        lax.psum_scatter(grad_down, "fsdp", scatter_dimension=0, tiled=True),
    )
    return (
        lax.psum(owned[0].astype(jnp.bfloat16), "sp").astype(jnp.float32),
        lax.psum(owned[1].astype(jnp.bfloat16), "sp").astype(jnp.float32),
    )


def reduce_rest(grad_list):
    owned = (
        lax.psum_scatter(grad_list[0], "fsdp", scatter_dimension=0, tiled=True),
        lax.psum_scatter(grad_list[1], "fsdp", scatter_dimension=0, tiled=True),
        lax.psum_scatter(grad_list[2], "fsdp", scatter_dimension=1, tiled=True),
        lax.psum_scatter(grad_list[3], "fsdp", scatter_dimension=0, tiled=True),
        lax.psum_scatter(grad_list[4], "fsdp", scatter_dimension=0, tiled=True),
        lax.psum_scatter(grad_list[5], "fsdp", scatter_dimension=0, tiled=True),
        lax.psum_scatter(grad_list[6], "fsdp", scatter_dimension=0, tiled=True),
        lax.psum_scatter(grad_list[7], "fsdp", scatter_dimension=0, tiled=True),
    )
    return (
        lax.psum(owned[0].astype(jnp.bfloat16), "sp").astype(jnp.float32),
        lax.psum(owned[1].astype(jnp.bfloat16), "sp").astype(jnp.float32),
        lax.psum(owned[2].astype(jnp.bfloat16), "sp").astype(jnp.float32),
        lax.psum(owned[3].astype(jnp.bfloat16), "sp").astype(jnp.float32),
        lax.psum(owned[4].astype(jnp.bfloat16), "sp").astype(jnp.float32),
        lax.psum(owned[5].astype(jnp.bfloat16), "sp").astype(jnp.float32),
        lax.psum(owned[6].astype(jnp.bfloat16), "sp").astype(jnp.float32),
        lax.psum(owned[7].astype(jnp.bfloat16), "sp").astype(jnp.float32),
    )


def body(
    tokens,
    text,
    clip_frames,
    timestep,
    mod_weight,
    mod_bias,
    qk_gains,
    self_in,
    self_out,
    cross_q,
    cross_kv,
    cross_out,
    mlp_in,
    mlp_out,
    cotangent,
):
    row_count = tokens.shape[0]
    frame_count = row_count // FRAME_TOK
    group_frames = timestep.shape[1]
    live_count = clip_frames[0]
    first_frame = lax.axis_index("sp") * frame_count
    own_pos = first_frame + jnp.arange(frame_count, dtype=jnp.int32)
    own_steps = lax.dynamic_slice_in_dim(timestep[0], first_frame, frame_count)
    cosine, sine = rotary_tables(
        jnp.repeat(own_pos, FRAME_TOK),
        jnp.tile(jnp.arange(FRAME_TOK, dtype=jnp.int32), frame_count),
    )
    sinus = sinus_features(own_steps).astype(jnp.bfloat16)
    seq_live = jnp.repeat(jnp.arange(group_frames, dtype=jnp.int32) < live_count, FRAME_TOK)
    text_live = jnp.ones((TXT,), dtype=bool)
    shards = (
        mod_weight,
        mod_bias,
        qk_gains,
        self_in,
        self_out,
        cross_q,
        cross_kv,
        cross_out,
        mlp_in,
        mlp_out,
    )
    residual = tokens.astype(jnp.float32)
    block_no = 0
    weights = fetch_weights(shards, block_no)
    fetched = [weights]
    (
        mod_matrix,
        mod_offset,
        gain_rows,
        self_proj,
        self_back,
        cross_qproj,
        cross_kvproj,
        cross_back,
        up_matrix,
        down_matrix,
    ) = weights
    gain_table = gain_rows.astype(jnp.float32)
    modulation = product(sinus, mod_matrix) + mod_offset.astype(jnp.float32)[None, :]
    shift_one, scale_one, gate_one, shift_two, scale_two, gate_two = jnp.split(
        modulation, 6, axis=1
    )
    attn_float, back_attn_input = jax.vjp(modulated, residual, shift_one, scale_one)
    attn_input = attn_float.astype(jnp.bfloat16)
    joined = product(attn_input, self_proj)
    prepared, back_prepare = jax.vjp(
        lambda joined_rows, gain_query, gain_key: self_prepare(
            joined_rows, gain_query, gain_key, cosine, sine
        ),
        joined,
        gain_table[0],
        gain_table[1],
    )
    query_heads, key_heads, value_heads = to_heads(
        (
            prepared[0].astype(jnp.bfloat16),
            prepared[1].astype(jnp.bfloat16),
            prepared[2].astype(jnp.bfloat16),
        )
    )
    self_heads, self_totals = attend_forward(query_heads, key_heads, value_heads, seq_live)
    self_mixed = to_tokens((self_heads,))[0]
    self_branch = product(self_mixed, self_back)
    residual = gated_add(residual, self_branch, gate_one)
    cross_float, back_cross_norm = jax.vjp(layer_norm, residual)
    cross_input = cross_float.astype(jnp.bfloat16)
    cross_raw = product(cross_input, cross_qproj)
    cross_normed, back_cross_query = jax.vjp(rms_norm, cross_raw, gain_table[2])
    text_raw = product(text, cross_kvproj)
    text_parts, back_text = jax.vjp(text_prepare, text_raw, gain_table[3])
    cross_qheads, cross_kheads, cross_vheads = to_heads(
        (
            cross_normed.astype(jnp.bfloat16),
            text_parts[0].astype(jnp.bfloat16),
            text_parts[1].astype(jnp.bfloat16),
        )
    )
    cross_heads, cross_totals = attend_forward(cross_qheads, cross_kheads, cross_vheads, text_live)
    cross_mixed = to_tokens((cross_heads,))[0]
    residual = residual + product(cross_mixed, cross_back)
    mlp_float, back_mlp_input = jax.vjp(modulated, residual, shift_two, scale_two)
    mlp_input = mlp_float.astype(jnp.bfloat16)
    up_proj = product(mlp_input, up_matrix)
    activated_float, back_gelu = jax.vjp(
        lambda inner: jax.nn.gelu(inner, approximate=True), up_proj
    )
    activated = activated_float.astype(jnp.bfloat16)
    mlp_branch = product(activated, down_matrix)
    residual = gated_add(residual, mlp_branch, gate_two)
    saved = [
        {
            "gate_one": gate_one,
            "gate_two": gate_two,
            "back_attn_input": back_attn_input,
            "attn_input": attn_input,
            "back_prepare": back_prepare,
            "query_heads": query_heads,
            "key_heads": key_heads,
            "value_heads": value_heads,
            "self_totals": self_totals,
            "self_mixed": self_mixed,
            "self_branch": self_branch,
            "back_cross_norm": back_cross_norm,
            "cross_input": cross_input,
            "back_cross_query": back_cross_query,
            "back_text": back_text,
            "cross_qheads": cross_qheads,
            "cross_kheads": cross_kheads,
            "cross_vheads": cross_vheads,
            "cross_totals": cross_totals,
            "cross_mixed": cross_mixed,
            "back_mlp_input": back_mlp_input,
            "mlp_input": mlp_input,
            "back_gelu": back_gelu,
            "activated": activated,
            "mlp_branch": mlp_branch,
        }
    ]
    output = residual.astype(jnp.bfloat16)
    grad_rows = cotangent.astype(jnp.float32)
    reduced = [None] * LAYERS
    for block_no in reversed(range(LAYERS)):
        weights = fetched[block_no]
        (
            mod_matrix,
            mod_offset,
            gain_rows,
            self_proj,
            self_back,
            cross_qproj,
            cross_kvproj,
            cross_back,
            up_matrix,
            down_matrix,
        ) = weights
        kept = saved[block_no]
        grad_branch = gate_scaled(grad_rows, kept["gate_two"]).astype(jnp.bfloat16)
        grad_gate_two = frame_sum(grad_rows * kept["mlp_branch"], frame_count)
        grad_down = product_tn(kept["activated"], grad_branch)
        grad_activated = product_nt(grad_branch, down_matrix)
        grad_up_float = kept["back_gelu"](grad_activated)[0]
        grad_up_low = grad_up_float.astype(jnp.bfloat16)
        grad_up = product_tn(kept["mlp_input"], grad_up_low)
        grad_mlp_input = product_nt(grad_up_low, up_matrix)
        mlp_reduced = reduce_mlp(grad_up, grad_down)
        grad_from_mlp, grad_shift_two, grad_scale_two = kept["back_mlp_input"](grad_mlp_input)
        grad_rows = grad_rows + grad_from_mlp
        grad_low = grad_rows.astype(jnp.bfloat16)
        grad_cross_back = product_tn(kept["cross_mixed"], grad_low)
        grad_cross_mixed = product_nt(grad_low, cross_back).astype(jnp.bfloat16)
        grad_cross_heads = to_heads((grad_cross_mixed,))[0]
        grad_cq_heads, grad_ck_heads, grad_cv_heads = attend_backward(
            kept["cross_qheads"],
            kept["cross_kheads"],
            kept["cross_vheads"],
            kept["cross_totals"],
            grad_cross_heads,
            text_live,
        )
        grad_cross_query, grad_text_keys, grad_text_values = to_tokens(
            (grad_cq_heads, grad_ck_heads, grad_cv_heads)
        )
        grad_cross_raw, grad_gain_two = kept["back_cross_query"](
            grad_cross_query.astype(jnp.float32)
        )
        grad_text_raw, grad_gain_three = kept["back_text"](
            (grad_text_keys.astype(jnp.float32), grad_text_values.astype(jnp.float32))
        )
        grad_cross_low = grad_cross_raw.astype(jnp.bfloat16)
        grad_cross_qproj = product_tn(kept["cross_input"], grad_cross_low)
        grad_cross_kvproj = product_tn(text, grad_text_raw.astype(jnp.bfloat16))
        grad_cross_input = product_nt(grad_cross_low, cross_qproj)
        grad_rows = grad_rows + kept["back_cross_norm"](grad_cross_input)[0]
        grad_self_low = gate_scaled(grad_rows, kept["gate_one"]).astype(jnp.bfloat16)
        grad_gate_one = frame_sum(grad_rows * kept["self_branch"], frame_count)
        grad_self_back = product_tn(kept["self_mixed"], grad_self_low)
        grad_self_mixed = product_nt(grad_self_low, self_back).astype(jnp.bfloat16)
        grad_self_heads = to_heads((grad_self_mixed,))[0]
        grad_q_heads, grad_k_heads, grad_v_heads = attend_backward(
            kept["query_heads"],
            kept["key_heads"],
            kept["value_heads"],
            kept["self_totals"],
            grad_self_heads,
            seq_live,
        )
        grad_query, grad_key, grad_value = to_tokens((grad_q_heads, grad_k_heads, grad_v_heads))
        grad_joined, grad_gain_zero, grad_gain_one = kept["back_prepare"](
            (
                grad_query.astype(jnp.float32),
                grad_key.astype(jnp.float32),
                grad_value.astype(jnp.float32),
            )
        )
        grad_joined_low = grad_joined.astype(jnp.bfloat16)
        grad_self_proj = product_tn(kept["attn_input"], grad_joined_low)
        grad_attn_input = product_nt(grad_joined_low, self_proj)
        grad_from_attn, grad_shift_one, grad_scale_one = kept["back_attn_input"](grad_attn_input)
        grad_rows = grad_rows + grad_from_attn
        grad_modulation = jnp.concatenate(
            [
                grad_shift_one,
                grad_scale_one,
                grad_gate_one,
                grad_shift_two,
                grad_scale_two,
                grad_gate_two,
            ],
            axis=1,
        )
        grad_mod_offset = jnp.sum(grad_modulation, axis=0)
        grad_mod_matrix = product_tn(sinus, grad_modulation.astype(jnp.bfloat16))
        grad_gains = jnp.stack([grad_gain_zero, grad_gain_one, grad_gain_two, grad_gain_three])
        rest_reduced = reduce_rest(
            (
                grad_mod_matrix,
                grad_mod_offset,
                grad_gains,
                grad_self_proj,
                grad_self_back,
                grad_cross_qproj,
                grad_cross_kvproj,
                grad_cross_back,
            )
        )
        reduced[block_no] = [
            rest_reduced[0],
            rest_reduced[1],
            rest_reduced[2],
            rest_reduced[3],
            rest_reduced[4],
            rest_reduced[5],
            rest_reduced[6],
            rest_reduced[7],
            mlp_reduced[0],
            mlp_reduced[1],
        ]
    stacked = [jnp.stack([reduced[0][member]]) for member in range(10)]
    return (
        output,
        grad_rows,
        stacked[0],
        stacked[1],
        stacked[2],
        stacked[3],
        stacked[4],
        stacked[5],
        stacked[6],
        stacked[7],
        stacked[8],
        stacked[9],
    )


def solution(mesh):
    in_specs = (
        P(("fsdp", "sp"), None),
        P(("fsdp", "sp"), None),
        P("fsdp"),
        P("fsdp", None),
        P(None, "fsdp", None),
        P(None, "fsdp"),
        P(None, None, "fsdp"),
        P(None, "fsdp", None),
        P(None, "fsdp", None),
        P(None, "fsdp", None),
        P(None, "fsdp", None),
        P(None, "fsdp", None),
        P(None, "fsdp", None),
        P(None, "fsdp", None),
        P(("fsdp", "sp"), None),
    )
    out_specs = (
        P(("fsdp", "sp"), None),
        P(("fsdp", "sp"), None),
        P(None, "fsdp", None),
        P(None, "fsdp"),
        P(None, None, "fsdp"),
        P(None, "fsdp", None),
        P(None, "fsdp", None),
        P(None, "fsdp", None),
        P(None, "fsdp", None),
        P(None, "fsdp", None),
        P(None, "fsdp", None),
        P(None, "fsdp", None),
    )
    return jax.shard_map(body, mesh=mesh, in_specs=in_specs, out_specs=out_specs, check_vma=False)
```

profile of v0, /device:TPU:0, one launch (start us, length us, event | category | flops | bytes accessed | tf_op | source)
XLA Modules:
  0.0 4543.0 jit_solution(13971809447142004286)
XLA Ops:
  14.3 80.6 %all-reduce.9 = bf16[9216]{0:T(1024)(128)(2,1)S(1)} all-reduce(bf16[9216]{0:T(1024)(128)(2,1)S(1)} %dynamic-update-slice), channel_id=3, replica_groups=mesh['fsdp'=16,'sp'=2] {'fsdp'}, use_global_device_ids=true, to_apply=%add.9 | all-reduce | flops 9216 | bytes 36864
  95.0 44.3 all-gather.3
  142.4 32.3 slice_reduce_fusion
  179.6 43.9 all-gather.27.cloned.1.call-done
  256.5 134.3 %all-gather.21.cloned.1.call-done = bf16[1,1536,4608]{2,1,0:T(8,128)(2,1)} async-done(((bf16[1,96,4608]{2,1,0:T(8,128)(2,1)}), bf16[1,1536,4608]{2,1,0:T(8,128)(2,1)}) %all-gather.21.cloned.1.call-update) | async-done | bytes 14155792 | tf_op jit(solution)/shard_map/all_gather | solution.py:230
  475.7 76.6 %all-gather.25.cloned.1.call-done = bf16[1,1536,1536]{2,1,0:T(8,128)(2,1)} async-done(((bf16[1,96,1536]{2,1,0:T(8,128)(2,1)}), bf16[1,1536,1536]{2,1,0:T(8,128)(2,1)}) %all-gather.25.cloned.1.call-update) | async-done | bytes 4718608 | tf_op jit(solution)/shard_map/all_gather | solution.py:232
  599.9 33.5 all-gather.29.cloned.1.call-done
  638.3 289.5 %all-gather.31.cloned.1.call-done = bf16[1,1536,8960]{2,1,0:T(8,128)(2,1)} async-done(((bf16[1,96,8960]{2,1,0:T(8,128)(2,1)}), bf16[1,1536,8960]{2,1,0:T(8,128)(2,1)}) %all-gather.31.cloned.1.call-update) | async-done | bytes 27525136 | tf_op jit(solution)/shard_map/all_gather | solution.py:235
  942.8 278.7 %all-gather.33.cloned.1.call-done = bf16[1,8960,1536]{2,1,0:T(8,128)(2,1)} async-done(((bf16[1,560,1536]{2,1,0:T(8,128)(2,1)}), bf16[1,8960,1536]{2,1,0:T(8,128)(2,1)}) %all-gather.33.cloned.1.call-update) | async-done | bytes 27525136 | tf_op jit(solution)/shard_map/all_gather | solution.py:236
  1283.2 42.3 while.55
  1361.1 43.3 while.57
  1550.4 23.8 fusion.187
  1575.2 24.9 fusion.175
  1602.2 28.2 reduce-scatter.14.cloned.1.call-done
  1632.1 174.4 %reduce-scatter.20.cloned.1.call-done = f32[96,1536]{1,0:T(8,128)} async-done(((f32[1536,1536]{1,0:T(8,128)}), f32[96,1536]{1,0:T(8,128)}) %reduce-scatter.20.cloned.1.call-update) | async-done | bytes 589840 | tf_op jit(solution)/shard_map/reduce_scatter | solution.py:258
  1808.3 174.3 %reduce-scatter.22.cloned.1.call-done = f32[96,1536]{1,0:T(8,128)} async-done(((f32[1536,1536]{1,0:T(8,128)}), f32[96,1536]{1,0:T(8,128)}) %reduce-scatter.22.cloned.1.call-update) | async-done | bytes 589840 | tf_op jit(solution)/shard_map/reduce_scatter | solution.py:260
  1984.4 173.9 %reduce-scatter.18.cloned.1.call-done = f32[96,1536]{1,0:T(8,128)} async-done(((f32[1536,1536]{1,0:T(8,128)}), f32[96,1536]{1,0:T(8,128)}) %reduce-scatter.18.cloned.1.call-update) | async-done | bytes 589840 | tf_op jit(solution)/shard_map/reduce_scatter | solution.py:257
  2160.1 288.1 %reduce-scatter.30.cloned.1.call-done = f32[96,3072]{1,0:T(8,128)} async-done(((f32[1536,3072]{1,0:T(8,128)}), f32[96,3072]{1,0:T(8,128)}) %reduce-scatter.30.cloned.1.call-update) | async-done | bytes 1179664
  2450.7 397.9 %reduce-scatter.16.cloned.1.call-done = f32[96,4608]{1,0:T(8,128)} async-done(((f32[1536,4608]{1,0:T(8,128)}), f32[96,4608]{1,0:T(8,128)}) %reduce-scatter.16.cloned.1.call-update) | async-done | bytes 1769488 | tf_op jit(solution)/shard_map/reduce_scatter | solution.py:256
  2851.0 753.5 %reduce-scatter.24.cloned.1.call-done = f32[96,8960]{1,0:T(8,128)} async-done(((f32[1536,8960]{1,0:T(8,128)}), f32[96,8960]{1,0:T(8,128)}) %reduce-scatter.24.cloned.1.call-update) | async-done | bytes 3440656 | tf_op jit(solution)/shard_map/reduce_scatter | solution.py:242
  3607.9 752.2 %reduce-scatter.26.cloned.1.call-done = f32[560,1536]{1,0:T(8,128)} async-done(((f32[8960,1536]{1,0:T(8,128)}), f32[560,1536]{1,0:T(8,128)}) %reduce-scatter.26.cloned.1.call-update) | async-done | bytes 3440656 | tf_op jit(solution)/shard_map/reduce_scatter | solution.py:243
  4364.2 74.9 %all-reduce.10 = bf16[9216]{0:T(1024)(128)(2,1)S(1)} all-reduce(f32[9216]{0:T(1024)S(1)} %reduce_sum.354), channel_id=13, replica_groups=mesh['fsdp'=16,'sp'=2] {'fsdp'}, use_global_device_ids=true, to_apply=%region_42.43.clone | all-reduce | flops 9216 | bytes 55296
  4440.8 46.9 %reduce-scatter.28.cloned.1.call-done = f32[96,4]{1,0:T(8,128)} async-done(((f32[1536,4]{1,0:T(8,128)}), f32[96,4]{1,0:T(8,128)}) %reduce-scatter.28.cloned.1.call-update) | async-done | bytes 1552
  4492.2 31.8 all-reduce.15.cloned.1.call-done
  (590 shorter events, 599.4 us)
Async XLA Ops:
  7.2 167.5 %all-gather.19.cloned.1.call-start = ((), (), s32[]{:S(2)}) async-start(), calls=%async_computation.32 | async-start | bytes 5013504 | tf_op jit(solution)/shard_map/all_gather | solution.py:227
  8.0 215.5 %all-gather.27.cloned.1.call-start = ((), (), s32[]{:S(2)}) async-start(), calls=%async_computation.36 | async-start | bytes 10027008 | tf_op jit(solution)/shard_map/all_gather | solution.py:233
  8.7 382.0 %all-gather.21.cloned.1.call-start = ((), (), s32[]{:S(2)}) async-start(), calls=%async_computation.33 | async-start | bytes 15040512 | tf_op jit(solution)/shard_map/all_gather | solution.py:230
  9.5 461.9 %all-gather.23.cloned.1.call-start = ((), (), s32[]{:S(2)}) async-start(), calls=%async_computation.34 | async-start | bytes 5013504 | tf_op jit(solution)/shard_map/all_gather | solution.py:231
  10.0 542.3 %all-gather.25.cloned.1.call-start = ((), (), s32[]{:S(2)}) async-start(), calls=%async_computation.35 | async-start | bytes 5013504 | tf_op jit(solution)/shard_map/all_gather | solution.py:232
  10.6 622.8 %all-gather.29.cloned.1.call-start = ((), (), s32[]{:S(2)}) async-start(), calls=%async_computation.37 | async-start | bytes 5013504 | tf_op jit(solution)/shard_map/all_gather | solution.py:234
  11.2 916.5 %all-gather.31.cloned.1.call-start = ((), (), s32[]{:S(2)}) async-start(), calls=%async_computation.38 | async-start | bytes 29245440 | tf_op jit(solution)/shard_map/all_gather | solution.py:235
  12.0 1209.6 %all-gather.33.cloned.1.call-start = ((), (), s32[]{:S(2)}) async-start(), calls=%async_computation.39 | async-start | bytes 29245440 | tf_op jit(solution)/shard_map/all_gather | solution.py:236
  451.3 20.0 all-to-all-start.3
  475.5 870.6 %copy-start.45 = (f32[128]{0:T(128)}, f32[128]{0:T(128)S(1)}, u32[]{:S(2)}) copy-start(f32[128]{0:T(128)S(1)} %broadcast_multiply_fusion.1) | copy-start | bytes 1540
  475.7 870.3 %copy-start.53 = (f32[128]{0:T(128)}, f32[128]{0:T(128)S(1)}, u32[]{:S(2)}) copy-start(f32[128]{0:T(128)S(1)} %fusion.164) | copy-start | bytes 1540
  595.7 37.7 all-to-all-start.7
  1406.5 6.3 all-to-all-start.12
  1412.7 5.9 all-to-all-start.13
  1416.9 213.4 %reduce-scatter.14.cloned.1.call-start = ((), (), s32[]{:S(2)}) async-start(), calls=%async_computation.25 | async-start | bytes 10027008 | tf_op jit(solution)/shard_map/reduce_scatter | solution.py:253
  1460.8 345.6 %reduce-scatter.20.cloned.1.call-start = ((), (), s32[]{:S(2)}) async-start(), calls=%async_computation.28 | async-start | bytes 10027008 | tf_op jit(solution)/shard_map/reduce_scatter | solution.py:258
  1466.9 515.7 %reduce-scatter.22.cloned.1.call-start = ((), (), s32[]{:S(2)}) async-start(), calls=%async_computation.29 | async-start | bytes 10027008 | tf_op jit(solution)/shard_map/reduce_scatter | solution.py:260
  1473.9 684.4 %reduce-scatter.18.cloned.1.call-start = ((), (), s32[]{:S(2)}) async-start(), calls=%async_computation.27 | async-start | bytes 10027008 | tf_op jit(solution)/shard_map/reduce_scatter | solution.py:257
  1480.9 967.3 %reduce-scatter.30.cloned.1.call-start = ((), (), s32[]{:S(2)}) async-start(), calls=%async_computation.41 | async-start | bytes 20054016
  1535.5 1313.0 %reduce-scatter.16.cloned.1.call-start = ((), (), s32[]{:S(2)}) async-start(), calls=%async_computation.26 | async-start | bytes 30081024 | tf_op jit(solution)/shard_map/reduce_scatter | solution.py:256
  1549.5 2055.1 %reduce-scatter.24.cloned.1.call-start = ((), (), s32[]{:S(2)}) async-start(), calls=%async_computation.30 | async-start | bytes 58490880 | tf_op jit(solution)/shard_map/reduce_scatter | solution.py:242
  1574.3 2785.8 %reduce-scatter.26.cloned.1.call-start = ((), (), s32[]{:S(2)}) async-start(), calls=%async_computation.31 | async-start | bytes 58490880 | tf_op jit(solution)/shard_map/reduce_scatter | solution.py:243
  1600.2 2887.5 %reduce-scatter.28.cloned.1.call-start = ((), (), s32[]{:S(2)}) async-start(), calls=%async_computation.40 | async-start | bytes 835584
  1602.1 2921.9 %all-reduce.15.cloned.1.call-start = ((), (), s32[]{:S(2)}) async-start(), calls=%async_computation.42 | async-start | bytes 12582912 | tf_op jit(solution)/shard_map/psum | solution.py:269
  (75 other events, 2369.0 us)
Sparse Core Ops, SparseCore 0:
  10.9 86.2 all-gather.18
  100.0 123.4 all-gather.26
  226.3 164.4 all-gather.20
  393.4 77.9 all-gather.22
  474.0 78.3 all-gather.24
  555.0 78.3 all-gather.28
  636.2 291.4 all-gather.30
  930.5 290.9 all-gather.32
  1461.0 169.2 reduce-scatter.13
  1635.8 170.5 reduce-scatter.19
  1812.2 170.4 reduce-scatter.21
  1988.2 170.1 reduce-scatter.17
  2164.1 284.1 reduce-scatter.29
  2453.9 394.6 reduce-scatter.15
  2854.6 749.8 reduce-scatter.23
  3610.6 749.4 reduce-scatter.25
  4364.6 123.0 reduce-scatter.27
  4492.0 31.8 all-reduce.14
where the time goes:
time: 4560 us; the launch traced here: 4540 us
  waiting for transfers between devices  3700 us (81%)
  matrix products  310 us (7%)
  blocking collectives  258 us (6%)
  local copies, waits for them, and re-layouts  172 us (4%)
  other arithmetic  68.4 us (2%)
    reduce_scatter x1, waiting for transfers between devices, reduce_mlp(): lax.psum_scatter(grad_up, 'fsdp', scatter_dimension=0, tiled=True)  754 us
    reduce_scatter x1, waiting for transfers between devices, reduce_mlp(): lax.psum_scatter(grad_down, 'fsdp', scatter_dimension=0, tiled=True)  752 us
    reduce_scatter x1, waiting for transfers between devices, reduce_rest(): lax.psum_scatter(grad_list[3], 'fsdp', scatter_dimension=0, tiled=True)  398 us
    unnamed x20, waiting for transfers between devices  340 us
    all_gather x1, waiting for transfers between devices, fetch_weights(): lax.all_gather(pieces[8], 'fsdp', axis=0, tiled=True)  289 us
    all_gather x1, waiting for transfers between devices, fetch_weights(): lax.all_gather(pieces[9], 'fsdp', axis=0, tiled=True)  279 us
    reduce_scatter x1, waiting for transfers between devices, reduce_rest(): lax.psum_scatter(grad_list[5], 'fsdp', scatter_dimension=0, tiled=True)  174 us
    reduce_scatter x1, waiting for transfers between devices, reduce_rest(): lax.psum_scatter(grad_list[7], 'fsdp', scatter_dimension=0, tiled=True)  174 us
  transfers between devices with their start and end apart: 22, of which 18 were waited for; matrix products, arithmetic and copies ran while one was open for 7% of the time, Pallas kernels for 0%

commit v1 on v0

v1 whole, which is shorter than its diff:
```python
import math

import jax
import jax.numpy as jnp
from jax import lax
from jax.experimental import pallas as pl
from jax.experimental.pallas import tpu as pltpu
from jax.sharding import Mesh
from jax.sharding import PartitionSpec as P

D = 1536
HD = 128
TXT = 512
FREQ = 256
WP = 8
FRAME_TOK = 64
PLANE = 4

EPSILON = 1e-06
NEGATIVE = -1e30

FS = ("za", "yb", "xc")
PL = ("yb", "xc")
ALL = ("za", "yb", "xc", "sp")
SCALE = 1.0 / math.sqrt(HD)
BF = jnp.bfloat16
F32 = jnp.float32


def product(left, right):
    return jnp.dot(left, right, preferred_element_type=F32)


def product_tn(left, right):
    return lax.dot_general(left, right, (((0,), (0,)), ((), ())), preferred_element_type=F32)


def product_nt(left, right):
    return lax.dot_general(left, right, (((1,), (1,)), ((), ())), preferred_element_type=F32)


def layer_norm(values):
    centred = values - jnp.mean(values, axis=-1, keepdims=True)
    return centred * lax.rsqrt(jnp.mean(centred * centred, axis=-1, keepdims=True) + EPSILON)


def sinus_features(steps):
    half_dim = FREQ // 2
    rates = jnp.exp(jnp.arange(half_dim).astype(F32) * (-math.log(10000.0) / half_dim))
    angles = steps.astype(F32)[:, None] * rates[None, :]
    return jnp.concatenate([jnp.cos(angles), jnp.sin(angles)], axis=1)


def rotary_tables(frame_pos, token_spot):
    half_dim = HD // 2
    side_pairs = HD // 6
    lead_pairs = half_dim - 2 * side_pairs
    pair_index = jnp.arange(half_dim)
    log_base = -math.log(10000.0)
    lead_part = pair_index < lead_pairs
    side_part = jnp.logical_and(pair_index >= lead_pairs, pair_index < lead_pairs + side_pairs)
    last_part = pair_index >= lead_pairs + side_pairs
    frame_rate = jnp.where(
        lead_part, jnp.exp(log_base * pair_index.astype(F32) / lead_pairs), 0.0
    )
    row_rate = jnp.where(
        side_part, jnp.exp(log_base * (pair_index - lead_pairs).astype(F32) / side_pairs), 0.0
    )
    column_rate = jnp.where(
        last_part,
        jnp.exp(log_base * (pair_index - lead_pairs - side_pairs).astype(F32) / side_pairs),
        0.0,
    )
    patch_row = (token_spot // WP).astype(F32)
    patch_column = (token_spot % WP).astype(F32)
    angles = (
        frame_pos.astype(F32)[:, None] * frame_rate[None, :]
        + patch_row[:, None] * row_rate[None, :]
        + patch_column[:, None] * column_rate[None, :]
    )
    return (jnp.cos(angles), jnp.sin(angles))


def rotate(values, cosine, sine):
    row_count = values.shape[0]
    shaped = values.reshape(row_count, -1, HD)
    half_dim = HD // 2
    first_half = shaped[:, :, :half_dim]
    second_half = shaped[:, :, half_dim:]
    cos_rows = cosine[:, None, :]
    sin_rows = sine[:, None, :]
    turned = jnp.concatenate(
        [
            first_half * cos_rows - second_half * sin_rows,
            second_half * cos_rows + first_half * sin_rows,
        ],
        axis=2,
    )
    return turned.reshape(row_count, -1)


def modulated(residual, shift, scale):
    frames = shift.shape[0]
    normed = layer_norm(residual).reshape(frames, -1, residual.shape[1])
    return (normed * (1.0 + scale[:, None, :]) + shift[:, None, :]).reshape(residual.shape)


def frame_scaled(rows, gate):
    frames = gate.shape[0]
    return (rows.reshape(frames, -1, rows.shape[1]) * gate[:, None, :]).reshape(rows.shape)


def frame_sum(values, frames):
    return jnp.sum(values.reshape(frames, -1, values.shape[1]), axis=1)


def attend_forward_kernel(live_ref, q_ref, k_ref, v_ref, out_ref, lse_ref):
    rows, keys = q_ref.shape[0], k_ref.shape[0]
    spot = lax.broadcasted_iota(jnp.int32, (rows, keys), 1)
    allowed = spot < live_ref[0]
    for head in range(q_ref.shape[1] // HD):
        part = slice(head * HD, (head + 1) * HD)
        scores = jnp.where(allowed, product_nt(q_ref[:, part], k_ref[:, part]) * SCALE, NEGATIVE)
        row_max = jnp.max(scores, axis=1, keepdims=True)
        log_total = row_max + jnp.log(jnp.sum(jnp.exp(scores - row_max), axis=1, keepdims=True))
        weights = jnp.exp(scores - log_total).astype(BF)
        out_ref[:, part] = product(weights, v_ref[:, part]).astype(BF)
        lse_ref[:, part] = jnp.broadcast_to(log_total, (rows, HD))


def attend_backward_kernel(
    live_ref, q_ref, k_ref, v_ref, lse_ref, do_ref, dq_ref, dk_ref, dv_ref
):
    rows, keys = q_ref.shape[0], k_ref.shape[0]
    spot = lax.broadcasted_iota(jnp.int32, (rows, keys), 1)
    allowed = spot < live_ref[0]
    for head in range(q_ref.shape[1] // HD):
        part = slice(head * HD, (head + 1) * HD)
        query, key, value, grad = q_ref[:, part], k_ref[:, part], v_ref[:, part], do_ref[:, part]
        scores = jnp.where(allowed, product_nt(query, key) * SCALE, NEGATIVE)
        weights = jnp.exp(scores - lse_ref[:, head * HD : head * HD + 1])
        grad_weights = product_nt(grad, value)
        delta = jnp.sum(weights * grad_weights, axis=1, keepdims=True)
        grad_scores = (weights * (grad_weights - delta)).astype(BF)
        dq_ref[:, part] = (product(grad_scores, key) * SCALE).astype(BF)
        dk_ref[:, part] = (product_tn(grad_scores, query) * SCALE).astype(BF)
        dv_ref[:, part] = product_tn(weights.astype(BF), grad).astype(BF)


VM = pl.BlockSpec(memory_space=pltpu.VMEM)
SM = pl.BlockSpec(memory_space=pltpu.SMEM)


def attend_forward(live, query, key, value):
    rows, width = query.shape
    keys = key.shape[0]
    heads = width // HD
    return pl.pallas_call(
        attend_forward_kernel,
        out_shape=(
            jax.ShapeDtypeStruct((rows, width), BF),
            jax.ShapeDtypeStruct((rows, width), F32),
        ),
        in_specs=[SM, VM, VM, VM],
        out_specs=(VM, VM),
        cost_estimate=pl.CostEstimate(
            flops=4 * rows * keys * width,
            bytes_accessed=8 * rows * width + 4 * keys * width,
            transcendentals=2 * rows * keys * heads,
        ),
    )(live, query, key, value)


def attend_backward(live, query, key, value, lse, grad):
    rows, width = query.shape
    keys = key.shape[0]
    heads = width // HD
    return pl.pallas_call(
        attend_backward_kernel,
        out_shape=(
            jax.ShapeDtypeStruct((rows, width), BF),
            jax.ShapeDtypeStruct((keys, width), BF),
            jax.ShapeDtypeStruct((keys, width), BF),
        ),
        in_specs=[SM, VM, VM, VM, VM, VM],
        out_specs=(VM, VM, VM),
        cost_estimate=pl.CostEstimate(
            flops=10 * rows * keys * width,
            bytes_accessed=10 * rows * width + 8 * keys * width,
            transcendentals=rows * keys * heads,
        ),
    )(live, query, key, value, lse, grad)


def gather(value, axes, axis=0):
    return lax.all_gather(value, axes, axis=axis, tiled=True)


def scatter(value, axes, axis=0):
    return lax.psum_scatter(value, axes, scatter_dimension=axis, tiled=True)


def swap(value, split_axis, concat_axis):
    return lax.all_to_all(value, "sp", split_axis=split_axis, concat_axis=concat_axis, tiled=True)


def rms_scale(total):
    return lax.rsqrt(total / D + EPSILON)


def square_sum(values):
    return jnp.sum(values * values, axis=1)


def rms_back(values, inverse, gain, grad):
    scaled = grad * gain
    return scaled, jnp.sum(scaled * values, axis=1)


def rms_finish(values, inverse, scaled, total):
    column = inverse[:, None]
    return scaled * column - values * (column * column * column) * (total / D)[:, None]


def body(
    tokens,
    text,
    clip_frames,
    timestep,
    mod_weight,
    mod_bias,
    qk_gains,
    self_in,
    self_out,
    cross_q,
    cross_kv,
    cross_out,
    mlp_in,
    mlp_out,
    cotangent,
):
    half = D // 2
    row_count = tokens.shape[0]
    frame_count = row_count // FRAME_TOK
    group_frames = timestep.shape[1]
    shards = D // self_in.shape[1]
    outer = shards // PLANE
    core = lax.axis_index("sp")
    chip = lax.axis_index(FS)
    own_frame = core * frame_count

    small = jnp.concatenate(
        [mod_bias[0].astype(F32), qk_gains[0].reshape(-1).astype(F32), timestep[0].astype(F32)]
    )
    small_all = gather(small[None], FS)
    bias_len, gain_len = mod_bias.shape[1], qk_gains.shape[2]
    bias_all = small_all[:, :bias_len].reshape(-1)
    gain_all = (
        small_all[:, bias_len : bias_len + 4 * gain_len]
        .reshape(shards, 4, gain_len)
        .transpose(1, 0, 2)
        .reshape(4, 2, half)
    )
    gain_own = lax.dynamic_index_in_dim(gain_all, core, 1, keepdims=False)
    steps_all = small_all[:, bias_len + 4 * gain_len :].reshape(-1)

    def own_half(weight, parts):
        shaped = weight[0].reshape(weight.shape[1], parts, 2, -1)
        return lax.dynamic_index_in_dim(shaped, core, 2, keepdims=False).reshape(
            weight.shape[1], -1
        )

    mod_matrix = gather(own_half(mod_weight, 1), FS)
    self_proj = gather(own_half(self_in, 3), FS)
    self_back = swap(gather(own_half(self_out, 1), FS), 0, 1)
    cross_kvproj = gather(own_half(cross_kv, 2), FS)
    cross_qproj = gather(own_half(cross_q, 1), FS)
    cross_back = swap(gather(own_half(cross_out, 1), FS), 0, 1)

    hid = mlp_out.shape[1] // 2
    in_rows = mlp_in.shape[1]
    up_part = lax.dynamic_index_in_dim(
        mlp_in[0].reshape(in_rows, outer, PLANE, 2, hid), core, 3, keepdims=False
    )
    up_part = up_part.transpose(2, 0, 1, 3).reshape(PLANE * in_rows, outer * hid)
    up_part = lax.all_to_all(up_part, PL, split_axis=0, concat_axis=0, tiled=True)
    up_matrix = gather(up_part, "za")
    down_part = lax.dynamic_slice_in_dim(mlp_out[0], core * hid, hid, 0)
    down_matrix = gather(down_part, "za")

    live_keys = clip_frames * FRAME_TOK
    all_keys = jnp.full((1,), TXT, jnp.int32)
    own_steps = lax.dynamic_slice_in_dim(timestep[0], own_frame, frame_count)
    clip_pos = jnp.arange(group_frames, dtype=jnp.int32)
    cosine, sine = rotary_tables(
        jnp.repeat(clip_pos, FRAME_TOK),
        jnp.tile(jnp.arange(FRAME_TOK, dtype=jnp.int32), group_frames),
    )
    sinus = sinus_features(timestep[0]).astype(BF)

    mod_half = product(sinus, mod_matrix)
    mod_half = mod_half + lax.dynamic_slice_in_dim(bias_all, core * 3 * D, 3 * D)[None]
    modulation = swap(mod_half, 0, 1)
    shift_one, scale_one, gate_one, shift_two, scale_two, gate_two = jnp.split(
        modulation, 6, axis=1
    )

    text_all = gather(text, "sp")

    residual = tokens.astype(F32)
    attn_float, back_attn_input = jax.vjp(modulated, residual, shift_one, scale_one)
    attn_input = gather(attn_float.astype(BF), "sp")
    joined = product(attn_input, self_proj)
    raw_q, raw_k, raw_v = joined[:, :half], joined[:, half : 2 * half], joined[:, 2 * half :]
    totals = lax.psum(jnp.stack([square_sum(raw_q), square_sum(raw_k)]), "sp")
    inv_q, inv_k = rms_scale(totals[0]), rms_scale(totals[1])
    query = rotate(raw_q * inv_q[:, None] * gain_own[0], cosine, sine).astype(BF)
    key = rotate(raw_k * inv_k[:, None] * gain_own[1], cosine, sine).astype(BF)
    value = raw_v.astype(BF)
    self_mixed, self_lse = attend_forward(live_keys, query, key, value)
    self_branch = scatter(product(self_mixed, self_back), "sp")
    residual = residual + frame_scaled(self_branch, gate_one)

    text_raw = product(text_all, cross_kvproj)
    raw_ck, raw_cv = text_raw[:, :half], text_raw[:, half:]
    inv_ck = rms_scale(lax.psum(square_sum(raw_ck)[None], "sp")[0])
    cross_key = (raw_ck * inv_ck[:, None] * gain_own[3]).astype(BF)
    cross_value = raw_cv.astype(BF)

    cross_float, back_cross_norm = jax.vjp(layer_norm, residual)
    cross_input = gather(cross_float.astype(BF), "sp")
    cross_raw = product(cross_input, cross_qproj)
    inv_cq = rms_scale(lax.psum(square_sum(cross_raw)[None], "sp")[0])
    cross_query = (cross_raw * inv_cq[:, None] * gain_own[2]).astype(BF)
    cross_mixed, cross_lse = attend_forward(all_keys, cross_query, cross_key, cross_value)
    residual = residual + scatter(product(cross_mixed, cross_back), "sp")

    mlp_float, back_mlp_input = jax.vjp(modulated, residual, shift_two, scale_two)
    mlp_input = gather(gather(mlp_float.astype(BF), PL), "sp")
    up_proj = product(mlp_input, up_matrix)
    activated_float, back_gelu = jax.vjp(
        lambda inner: jax.nn.gelu(inner, approximate=True), up_proj
    )
    activated = activated_float.astype(BF)

    def plane_sum(partial):
        half_sum = scatter(partial, "sp")
        return scatter(half_sum.astype(BF), PL).astype(F32)

    mlp_branch = plane_sum(product(activated, down_matrix))
    output = (residual + frame_scaled(mlp_branch, gate_two)).astype(BF)

    grad_rows = cotangent.astype(F32)
    grad_branch = frame_scaled(grad_rows, gate_two).astype(BF)
    grad_gate_two = frame_sum(grad_rows * mlp_branch, frame_count)
    grad_branch_all = gather(gather(grad_branch, PL), "sp")
    grad_down = product_tn(activated, grad_branch_all).astype(BF)
    down_owned = scatter(grad_down, "za")
    grad_up_low = back_gelu(product_nt(grad_branch_all, down_matrix))[0].astype(BF)
    grad_up = product_tn(mlp_input, grad_up_low).astype(BF)
    up_owned = scatter(grad_up, "za")
    grad_mlp_input = plane_sum(product_nt(grad_up_low, up_matrix))
    grad_from_mlp, grad_shift_two, grad_scale_two = back_mlp_input(grad_mlp_input)
    grad_rows = grad_rows + grad_from_mlp

    grad_low = gather(grad_rows.astype(BF), "sp")
    grad_cross_back = swap(product_tn(cross_mixed, grad_low).astype(BF), 1, 0)
    cross_back_owned = scatter(grad_cross_back, FS)
    grad_cross_mixed = product_nt(grad_low, cross_back).astype(BF)
    grad_cq, grad_ck, grad_cv = attend_backward(
        all_keys, cross_query, cross_key, cross_value, cross_lse, grad_cross_mixed
    )
    grad_cq, grad_ck = grad_cq.astype(F32), grad_ck.astype(F32)
    grad_gain_two = jnp.sum(grad_cq * cross_raw * inv_cq[:, None], axis=0)
    grad_gain_three = jnp.sum(grad_ck * raw_ck * inv_ck[:, None], axis=0)
    scaled_cq, dots_cq = rms_back(cross_raw, inv_cq, gain_own[2], grad_cq)
    scaled_ck, dots_ck = rms_back(raw_ck, inv_ck, gain_own[3], grad_ck)
    dots_cq = lax.psum(dots_cq[None], "sp")[0]
    dots_ck = lax.psum(dots_ck[None], "sp")[0]
    grad_cross_low = rms_finish(cross_raw, inv_cq, scaled_cq, dots_cq).astype(BF)
    grad_text_low = jnp.concatenate(
        [rms_finish(raw_ck, inv_ck, scaled_ck, dots_ck).astype(BF), grad_cv], axis=1
    )
    cross_q_owned = scatter(product_tn(cross_input, grad_cross_low).astype(BF), FS)
    cross_kv_owned = scatter(product_tn(text_all, grad_text_low).astype(BF), FS)
    grad_cross_input = scatter(product_nt(grad_cross_low, cross_qproj), "sp")
    grad_rows = grad_rows + back_cross_norm(grad_cross_input)[0]

    grad_gate_one = frame_sum(grad_rows * self_branch, frame_count)
    grad_self_low = gather(frame_scaled(grad_rows, gate_one).astype(BF), "sp")
    grad_self_back = swap(product_tn(self_mixed, grad_self_low).astype(BF), 1, 0)
    self_back_owned = scatter(grad_self_back, FS)
    grad_self_mixed = product_nt(grad_self_low, self_back).astype(BF)
    grad_q, grad_k, grad_v = attend_backward(
        live_keys, query, key, value, self_lse, grad_self_mixed
    )
    grad_q = rotate(grad_q.astype(F32), cosine, -sine)
    grad_k = rotate(grad_k.astype(F32), cosine, -sine)
    grad_gain_zero = jnp.sum(grad_q * raw_q * inv_q[:, None], axis=0)
    grad_gain_one = jnp.sum(grad_k * raw_k * inv_k[:, None], axis=0)
    scaled_q, dots_q = rms_back(raw_q, inv_q, gain_own[0], grad_q)
    scaled_k, dots_k = rms_back(raw_k, inv_k, gain_own[1], grad_k)
    dots = lax.psum(jnp.stack([dots_q, dots_k]), "sp")
    grad_joined_low = jnp.concatenate(
        [
            rms_finish(raw_q, inv_q, scaled_q, dots[0]).astype(BF),
            rms_finish(raw_k, inv_k, scaled_k, dots[1]).astype(BF),
            grad_v,
        ],
        axis=1,
    )
    self_in_owned = scatter(product_tn(attn_input, grad_joined_low).astype(BF), FS)
    grad_attn_input = scatter(product_nt(grad_joined_low, self_proj), "sp")
    grad_from_attn, grad_shift_one, grad_scale_one = back_attn_input(grad_attn_input)
    grad_rows = grad_rows + grad_from_attn

    grad_modulation = jnp.concatenate(
        [grad_shift_one, grad_scale_one, grad_gate_one, grad_shift_two, grad_scale_two, grad_gate_two],
        axis=1,
    )
    grad_mod_half = swap(grad_modulation, 1, 0)
    grad_mod_all = gather(grad_mod_half.astype(BF), FS)
    sinus_all = sinus_features(steps_all).astype(BF)
    own_features = mod_weight.shape[1]
    sinus_own = lax.dynamic_slice_in_dim(sinus_all, chip * own_features, own_features, 1)
    mod_weight_grad = gather(product_tn(sinus_own, grad_mod_all), "sp", 1)

    grad_gains = jnp.stack([grad_gain_zero, grad_gain_one, grad_gain_two, grad_gain_three])
    both = jnp.arange(2)[None, :, None] == core
    grad_gains = jnp.where(both, grad_gains[:, None, :], 0.0).reshape(4, shards, gain_len)
    grad_small = jnp.concatenate(
        [
            jnp.sum(grad_modulation, axis=0).reshape(shards, bias_len),
            grad_gains.transpose(1, 0, 2).reshape(shards, 4 * gain_len),
        ],
        axis=1,
    )
    small_owned = lax.psum(scatter(grad_small, FS), "sp")[0]

    def join(owned, parts):
        rows = owned.shape[0]
        pair = gather(owned.reshape(1, rows, parts, -1), "sp").astype(F32)
        return pair.transpose(1, 2, 0, 3).reshape(1, rows, -1)

    up_rows = lax.all_to_all(up_owned, PL, split_axis=0, concat_axis=0, tiled=True)
    up_pair = gather(up_rows.reshape(1, PLANE, in_rows, outer, hid), "sp").astype(F32)
    mlp_in_grad = up_pair.transpose(2, 3, 1, 0, 4).reshape(1, in_rows, -1)
    return (
        output,
        grad_rows,
        mod_weight_grad[None],
        small_owned[None, :bias_len],
        small_owned[bias_len:].reshape(1, 4, gain_len),
        join(self_in_owned, 3),
        join(self_back_owned, 1),
        join(cross_q_owned, 1),
        join(cross_kv_owned, 2),
        join(cross_back_owned, 1),
        mlp_in_grad,
        gather(down_owned, "sp").astype(F32)[None],
    )


def solution(mesh):
    chips, cores = mesh.shape["fsdp"], mesh.shape["sp"]
    grid = mesh.devices.reshape(chips // PLANE, 2, PLANE // 2, cores)
    inner = Mesh(grid, ALL)
    rows, second = P(ALL, None), P(None, FS, None)
    in_specs = (
        rows,
        rows,
        P(FS),
        P(FS, None),
        second,
        P(None, FS),
        P(None, None, FS),
        *([second] * 7),
        rows,
    )
    out_specs = (rows, rows, second, P(None, FS), P(None, None, FS), *([second] * 7))
    return jax.shard_map(body, mesh=inner, in_specs=in_specs, out_specs=out_specs, check_vma=False)
```

time: 4560 us -> 1800 us (0.39)
  waiting for transfers between devices: 3700 us -> 1150 us
  matrix products: 310 us -> 107 us
  blocking collectives: 258 us -> 305 us
    reduce_scatter x7 -> x14, waiting for transfers between devices: 2450 us -> 539 us  [scatter(): return lax.psum_scatter(value, axes, scatter_dimension=axis, tiled=True)]
    all_gather x8 -> x15, waiting for transfers between devices: 872 us -> 469 us  [gather(): return lax.all_gather(value, axes, axis=axis, tiled=True)]
    unnamed x20 -> x31, waiting for transfers between devices: 340 us -> 140 us
    dot_general x32 -> x8, matrix products: 122 us -> 34.5 us  [product_tn(): lax.dot_general(left, right, (((0,), (0,)), ((), ())), preferred_element_...]
    dot_general x42 -> x6, matrix products: 88.9 us -> 30 us  [product_nt(): lax.dot_general(left, right, (((1,), (1,)), ((), ())), preferred_element_...]
    dot_general x32 -> x8, matrix products: 98.8 us -> 42.9 us  [product(): return jnp.dot(left, right, preferred_element_type=F32)]
  transfers between devices with their start and end apart: 22 -> 31, of which waited for: 18 -> 23; matrix products, arithmetic and copies ran while one was open for 7% -> 13% of each run, Pallas kernels for 0% -> 0%
where the time goes in v1:
time: 1800 us; the launch traced here: 1790 us
  waiting for transfers between devices  1150 us (64%)
  blocking collectives  305 us (17%)
  local copies, waits for them, and re-layouts  128 us (7%)
  matrix products  107 us (6%)
  other arithmetic  59.4 us (3%)
  Pallas kernels  20.7 us (1%)
    reduce_scatter x14, waiting for transfers between devices, scatter(): return lax.psum_scatter(value, axes, scatter_dimension=axis, tiled=True)  539 us
    all_gather x15, waiting for transfers between devices, gather(): return lax.all_gather(value, axes, axis=axis, tiled=True)  469 us
    unnamed x2, blocking collectives  155 us
    unnamed x31, waiting for transfers between devices  140 us
    all_gather x11, blocking collectives, gather(): return lax.all_gather(value, axes, axis=axis, tiled=True)  67.1 us
    dot_general x8, matrix products, product(): return jnp.dot(left, right, preferred_element_type=F32)  42.9 us
    all_to_all x5, blocking collectives, swap(): lax.all_to_all(value, 'sp', split_axis=split_axis, concat_axis=concat_axi...  36.1 us
  transfers between devices with their start and end apart: 31, of which 23 were waited for; matrix products, arithmetic and copies ran while one was open for 13% of the time, Pallas kernels for 0%

profile of v1, /device:TPU:0, one launch (start us, length us, event | category | flops | bytes accessed | tf_op | source)
XLA Modules:
  0.0 1792.0 jit_solution(346545224515524044)
XLA Ops:
  24.7 79.5 %all-reduce = f32[15424]{0:T(1024)S(1)} all-reduce(f32[15424]{0:T(1024)S(1)} %maximum_dynamic-update-slice_fusion), channel_id=3, replica_groups=mesh['za'=4,'yb'=2,'xc'=2,'sp'=2] {'za','yb','xc'}, use_global_device_ids=true, to_apply=%add | all-reduce | flops 15424 | bytes 123392
  110.5 30.4 %all-gather.48.cloned.1.call-done = bf16[1536,1,1,768]{3,0,2,1:T(8,128)(2,1)} async-done(((bf16[96,1,1,768]{3,0,2,1:T(8,128)(2,1)}), bf16[1536,1,1,768]{3,0,2,1:T(8,128)(2,1)}) %all-gather.48.cloned.1.call-update) | async-done | bytes 2359312 | tf_op jit(solution)/shard_map/all_gather | solution.py:196
  161.8 81.5 %all-gather.26.cloned.1.call-done = bf16[1536,2304]{1,0:T(8,128)(2,1)} async-done(((bf16[96,2304]{1,0:T(8,128)(2,1)}), bf16[1536,2304]{1,0:T(8,128)(2,1)}) %all-gather.26.cloned.1.call-update) | async-done | bytes 7077904 | tf_op jit(solution)/shard_map/all_gather | solution.py:196
  270.8 36.3 %all-gather.52.cloned.1.call-done = bf16[1536,1,1,768]{3,0,2,1:T(8,128)(2,1)} async-done(((bf16[96,1,1,768]{3,0,2,1:T(8,128)(2,1)}), bf16[1536,1,1,768]{3,0,2,1:T(8,128)(2,1)}) %all-gather.52.cloned.1.call-update) | async-done | bytes 2359312 | tf_op jit(solution)/shard_map/all_gather | solution.py:196
  321.2 79.7 %all-gather.28.cloned.1.call-done = bf16[1536,1536]{1,0:T(8,128)(2,1)} async-done(((bf16[96,1536]{1,0:T(8,128)(2,1)}), bf16[1536,1536]{1,0:T(8,128)(2,1)}) %all-gather.28.cloned.1.call-update) | async-done | bytes 4718608 | tf_op jit(solution)/shard_map/all_gather | solution.py:196
  415.7 62.6 %all-gather.50.cloned.1.call-done = bf16[1536,1,1,768]{3,0,2,1:T(8,128)(2,1)} async-done(((bf16[96,1,1,768]{3,0,2,1:T(8,128)(2,1)}), bf16[1536,1,1,768]{3,0,2,1:T(8,128)(2,1)}) %all-gather.50.cloned.1.call-update) | async-done | bytes 2359312 | tf_op jit(solution)/shard_map/all_gather | solution.py:196
  533.3 17.5 all_to_all.131
  552.7 20.2 %all-gather.38.cloned.1.call-done = bf16[512,1536]{1,0:T(8,128)(2,1)} async-done(((bf16[128,1536]{1,0:T(8,128)(2,1)}), bf16[512,1536]{1,0:T(8,128)(2,1)}) %all-gather.38.cloned.1.call-update) | async-done | bytes 1572880 | tf_op jit(solution)/shard_map/all_gather | solution.py:196
  573.1 71.1 %all-gather.36.cloned.1.call-done = bf16[1536,1120]{1,0:T(8,128)(2,1)} async-done(((bf16[384,1120]{1,0:T(8,128)(2,1)}), bf16[1536,1120]{1,0:T(8,128)(2,1)}) %all-gather.36.cloned.1.call-update) | async-done | bytes 3440656 | tf_op jit(solution)/shard_map/all_gather | solution.py:196
  644.2 12.3 all-gather.34.cloned.1.call-done
  665.4 62.7 %all-gather.54.cloned.1.call-done = bf16[1,1120,1536]{2,1,0:T(8,128)(2,1)} async-done(((bf16[1,280,1536]{2,1,0:T(8,128)(2,1)}), bf16[1,1120,1536]{2,1,0:T(8,128)(2,1)}) %all-gather.54.cloned.1.call-update) | async-done | bytes 3440656 | tf_op jit(solution)/shard_map/all_gather | solution.py:196
  728.1 12.1 all-gather.40.cloned.1.call-done
  777.0 15.0 reduce-scatter.24.cloned.1.call-done
  795.3 33.3 %reduce-scatter.30.cloned.1.call-done = bf16[128,1536]{1,0:T(8,128)(2,1)} async-done(((bf16[512,1536]{1,0:T(8,128)(2,1)}), bf16[128,1536]{1,0:T(8,128)(2,1)}) %reduce-scatter.30.cloned.1.call-update) | async-done | bytes 393232 | tf_op jit(solution)/shard_map/reduce_scatter | solution.py:200
  829.8 33.5 %reduce-scatter.26.cloned.1.call-done = bf16[128,1536]{1,0:T(8,128)(2,1)} async-done(((bf16[512,1536]{1,0:T(8,128)(2,1)}), bf16[128,1536]{1,0:T(8,128)(2,1)}) %reduce-scatter.26.cloned.1.call-update) | async-done | bytes 393232 | tf_op jit(solution)/shard_map/reduce_scatter | solution.py:200
  949.9 13.5 reduce-scatter.44.cloned.1.call-done
  963.5 68.9 %reduce-scatter.48.cloned.1.call-done = bf16[384,1120]{1,0:T(8,128)(2,1)} async-done(((bf16[1536,1120]{1,0:T(8,128)(2,1)}), bf16[384,1120]{1,0:T(8,128)(2,1)}) %reduce-scatter.48.cloned.1.call-update) | async-done | bytes 860176 | tf_op jit(solution)/shard_map/reduce_scatter | solution.py:200
  1032.4 16.8 all_to_all.132
  1079.4 75.3 %all-reduce.1 = f32[16,960]{1,0:T(8,128)S(1)} all-reduce(f32[16,960]{1,0:T(8,128)S(1)} %pad_maximum_fusion.7), channel_id=19, replica_groups=mesh['za'=4,'yb'=2,'xc'=2,'sp'=2] {'za','yb','xc'}, use_global_device_ids=true, to_apply=%region_43.44.clone | all-reduce | flops 15360 | bytes 122880
  1211.7 129.2 %reduce-scatter.42.cloned.1.call-done = bf16[96,768]{1,0:T(8,128)(2,1)} async-done(((bf16[1536,768]{1,0:T(8,128)(2,1)}), bf16[96,768]{1,0:T(8,128)(2,1)}) %reduce-scatter.42.cloned.1.call-update) | async-done | bytes 147472 | tf_op jit(solution)/shard_map/reduce_scatter | solution.py:200
  1350.1 43.3 %all-gather.9 = bf16[16,4,4608]{2,1,0:T(4,128)(2,1)S(1)} all-gather(bf16[1,4,4608]{2,1,0:T(4,128)(2,1)S(1)} %reshape.836), channel_id=1, replica_groups=mesh['za'=4,'yb'=2,'xc'=2,'sp'=2] {'za','yb','xc'}, dimensions={0}, use_global_device_ids=true | all-gather | bytes 626688 | tf_op jit(solution)/shard_map/all_gather | solution.py:196
  1398.0 76.7 %reduce-scatter.38.cloned.1.call-done = bf16[96,768]{1,0:T(8,128)(2,1)} async-done(((bf16[1536,768]{1,0:T(8,128)(2,1)}), bf16[96,768]{1,0:T(8,128)(2,1)}) %reduce-scatter.38.cloned.1.call-update) | async-done | bytes 147472 | tf_op jit(solution)/shard_map/reduce_scatter | solution.py:200
  1478.7 138.3 %reduce-scatter.46.cloned.1.call-done = bf16[96,1536]{1,0:T(8,128)(2,1)} async-done(((bf16[1536,1536]{1,0:T(8,128)(2,1)}), bf16[96,1536]{1,0:T(8,128)(2,1)}) %reduce-scatter.46.cloned.1.call-update) | async-done | bytes 294928
  1623.8 149.6 %reduce-scatter.36.cloned.1.call-done = bf16[96,2304]{1,0:T(8,128)(2,1)} async-done(((bf16[1536,2304]{1,0:T(8,128)(2,1)}), bf16[96,2304]{1,0:T(8,128)(2,1)}) %reduce-scatter.36.cloned.1.call-update) | async-done | bytes 442384 | tf_op jit(solution)/shard_map/reduce_scatter | solution.py:200
  (462 shorter events, 415.3 us)
Async XLA Ops:
  7.2 100.5 %all-gather.46.cloned.1.call-start = ((), (), s32[]{:S(2)}) async-start(), calls=%async_computation.46 | async-start | bytes 2506752 | tf_op jit(solution)/shard_map/all_gather | solution.py:196
  9.6 131.4 %all-gather.48.cloned.1.call-start = ((), (), s32[]{:S(2)}) async-start(), calls=%async_computation.47 | async-start | bytes 2506752 | tf_op jit(solution)/shard_map/all_gather | solution.py:196
  11.7 231.6 %all-gather.26.cloned.1.call-start = ((), (), s32[]{:S(2)}) async-start(), calls=%async_computation.23 | async-start | bytes 7520256 | tf_op jit(solution)/shard_map/all_gather | solution.py:196
  18.0 289.2 %all-gather.52.cloned.1.call-start = ((), (), s32[]{:S(2)}) async-start(), calls=%async_computation.49 | async-start | bytes 2506752 | tf_op jit(solution)/shard_map/all_gather | solution.py:196
  19.2 302.0 %all-gather.30.cloned.1.call-start = ((), (), s32[]{:S(2)}) async-start(), calls=%async_computation.26 | async-start | bytes 2359296 | tf_op jit(solution)/shard_map/all_gather | solution.py:196
  19.8 381.1 %all-gather.28.cloned.1.call-start = ((), (), s32[]{:S(2)}) async-start(), calls=%async_computation.25 | async-start | bytes 5013504 | tf_op jit(solution)/shard_map/all_gather | solution.py:196
  153.3 258.1 %reduce-scatter.20.cloned.1.call-start = ((), (), s32[]{:S(2)}) async-start(), calls=%async_computation.24 | async-start | bytes 2359296 | tf_op jit(solution)/shard_map/reduce_scatter | solution.py:200
  269.6 208.7 %all-gather.50.cloned.1.call-start = ((), (), s32[]{:S(2)}) async-start(), calls=%async_computation.48 | async-start | bytes 2506752 | tf_op jit(solution)/shard_map/all_gather | solution.py:196
  270.8 233.7 %reduce-scatter.22.cloned.1.call-start = ((), (), s32[]{:S(2)}) async-start(), calls=%async_computation.27 | async-start | bytes 2359296 | tf_op jit(solution)/shard_map/reduce_scatter | solution.py:200
  508.8 135.4 %all-gather.36.cloned.1.call-start = ((), (), s32[]{:S(2)}) async-start(), calls=%async_computation.30 | async-start | bytes 4423680 | tf_op jit(solution)/shard_map/all_gather | solution.py:196
  550.8 105.7 %all-gather.34.cloned.1.call-start = ((), (), s32[]{:S(2)}) async-start(), calls=%async_computation.29 | async-start | bytes 4718592 | tf_op jit(solution)/shard_map/all_gather | solution.py:196
  551.6 176.5 %all-gather.54.cloned.1.call-start = ((), (), s32[]{:S(2)}) async-start(), calls=%async_computation.50 | async-start | bytes 4300800 | tf_op jit(solution)/shard_map/all_gather | solution.py:196
  552.6 187.6 %all-gather.40.cloned.1.call-start = ((), (), s32[]{:S(2)}) async-start(), calls=%async_computation.34 | async-start | bytes 4718592 | tf_op jit(solution)/shard_map/all_gather | solution.py:196
  572.9 200.8 %reduce-scatter.28.cloned.1.call-start = ((), (), s32[]{:S(2)}) async-start(), calls=%async_computation.35 | async-start | bytes 9437184 | tf_op jit(solution)/shard_map/reduce_scatter | solution.py:200
  795.2 113.9 %reduce-scatter.32.cloned.1.call-start = ((), (), s32[]{:S(2)}) async-start(), calls=%async_computation.37 | async-start | bytes 2359296 | tf_op jit(solution)/shard_map/reduce_scatter | solution.py:200
  894.6 137.8 %reduce-scatter.48.cloned.1.call-start = ((), (), s32[]{:S(2)}) async-start(), calls=%async_computation.52 | async-start | bytes 4423680 | tf_op jit(solution)/shard_map/reduce_scatter | solution.py:200
  908.4 169.1 %reduce-scatter.34.cloned.1.call-start = ((), (), s32[]{:S(2)}) async-start(), calls=%async_computation.38 | async-start | bytes 2359296 | tf_op jit(solution)/shard_map/reduce_scatter | solution.py:200
  949.8 229.7 %all-gather.44.cloned.1.call-start = ((), (), s32[]{:S(2)}) async-start(), calls=%async_computation.45 | async-start | bytes 2580480 | tf_op jit(solution)/shard_map/all_gather | solution.py:196
  963.4 219.8 %all-gather.42.cloned.1.call-start = ((), (), s32[]{:S(2)}) async-start(), calls=%async_computation.43 | async-start | bytes 3440640 | tf_op jit(solution)/shard_map/all_gather | solution.py:196
  1051.5 156.2 %reduce-scatter.40.cloned.1.call-start = ((), (), s32[]{:S(2)}) async-start(), calls=%async_computation.41 | async-start | bytes 2506752 | tf_op jit(solution)/shard_map/reduce_scatter | solution.py:200
  1055.1 285.8 %reduce-scatter.42.cloned.1.call-start = ((), (), s32[]{:S(2)}) async-start(), calls=%async_computation.42 | async-start | bytes 2506752 | tf_op jit(solution)/shard_map/reduce_scatter | solution.py:200
  1063.9 410.8 %reduce-scatter.38.cloned.1.call-start = ((), (), s32[]{:S(2)}) async-start(), calls=%async_computation.40 | async-start | bytes 2506752 | tf_op jit(solution)/shard_map/reduce_scatter | solution.py:200
  1073.1 544.0 %reduce-scatter.46.cloned.1.call-start = ((), (), s32[]{:S(2)}) async-start(), calls=%async_computation.51 | async-start | bytes 5013504
  1172.3 601.1 %reduce-scatter.36.cloned.1.call-start = ((), (), s32[]{:S(2)}) async-start(), calls=%async_computation.39 | async-start | bytes 7520256 | tf_op jit(solution)/shard_map/reduce_scatter | solution.py:200
  (84 other events, 2509.8 us)
Sparse Core Ops, SparseCore 0:
  11.4 65.3 all-gather.45
  80.1 60.7 all-gather.47
  144.3 98.9 all-gather.25
  246.5 60.5 all-gather.51
  320.5 80.2 all-gather.27
  414.8 63.4 all-gather.49
  508.0 32.1 all-gather.31
  542.0 30.8 all-gather.37
  574.3 69.9 all-gather.35
  658.5 69.4 all-gather.53
  729.4 10.7 all-gather.39
  758.5 15.1 reduce-scatter.27
  775.9 16.0 reduce-scatter.23
  795.4 33.1 reduce-scatter.29
  832.1 31.1 reduce-scatter.25
  897.1 66.2 reduce-scatter.43
  965.7 66.6 reduce-scatter.47
  1045.8 11.2 all-gather.43
  1059.3 12.4 all-gather.41
  1076.6 131.1 reduce-scatter.39
  1212.5 128.3 reduce-scatter.41
  1345.8 128.8 reduce-scatter.37
  1479.9 137.0 reduce-scatter.45
  1622.2 151.1 reduce-scatter.35
  (6 shorter events, 52.5 us)

commit v2 on v1

--- a/solution.py
+++ b/solution.py
@@ -1,3 +1,4 @@
+import functools
 import math
 
 import jax
@@ -23,6 +24,7 @@
 PL = ("yb", "xc")
 ALL = ("za", "yb", "xc", "sp")
 SCALE = 1.0 / math.sqrt(HD)
+MESH = pl.DeviceIdType.MESH
 BF = jnp.bfloat16
 F32 = jnp.float32
 
@@ -149,6 +151,7 @@
 
 VM = pl.BlockSpec(memory_space=pltpu.VMEM)
 SM = pl.BlockSpec(memory_space=pltpu.SMEM)
+ANY = pl.BlockSpec(memory_space=pl.ANY)
 
 
 def attend_forward(live, query, key, value):
@@ -190,6 +193,639 @@
             transcendentals=rows * keys * heads,
         ),
     )(live, query, key, value, lse, grad)
+
+
+def row_add(target, left, right, rows):
+    step = 16 if rows % 16 == 0 else rows
+
+    def chunk(index, carry):
+        at = pl.ds(pl.multiple_of(index * step, step), step)
+        total = left[at, :].astype(F32) + right[at, :].astype(F32)
+        target[at, :] = total.astype(target.dtype)
+        return carry
+
+    lax.fori_loop(0, rows // step, chunk, 0)
+
+
+class Flights:
+    def __init__(self):
+        self.sent = []
+
+    def send(self, source, target, send_sem, recv_sem, device, when=None):
+        copy = pltpu.make_async_remote_copy(
+            src_ref=source,
+            dst_ref=target,
+            send_sem=send_sem,
+            recv_sem=recv_sem,
+            device_id=device,
+            device_id_type=MESH,
+        )
+        if when is None:
+            copy.start()
+        else:
+            pl.when(when)(copy.start)
+        self.sent.append((when, copy))
+
+    def local(self, source, target, sem):
+        copy = pltpu.make_async_copy(source, target, sem)
+        copy.start()
+        return copy
+
+    def drain(self):
+        for when, copy in self.sent:
+            if when is None:
+                copy.wait_send()
+            else:
+                pl.when(when)(copy.wait_send)
+
+
+def landed(target, sem, device):
+    pltpu.make_async_remote_copy(
+        src_ref=target,
+        dst_ref=target,
+        send_sem=sem,
+        recv_sem=sem,
+        device_id=device,
+        device_id_type=MESH,
+    ).wait_recv()
+
+
+def greet(devices, optional=()):
+    barrier = pltpu.get_barrier_semaphore()
+    for device in devices:
+        pl.semaphore_signal(barrier, inc=1, device_id=device, device_id_type=MESH)
+    for when, device in optional:
+
+        @pl.when(when)
+        def _(device=device):
+            pl.semaphore_signal(barrier, inc=1, device_id=device, device_id_type=MESH)
+
+    count = len(devices)
+    for when, _ in optional:
+        count = count + when.astype(jnp.int32)
+    pl.semaphore_wait(barrier, count)
+
+
+def gather_kernel(outer, full, halves, *refs):
+    count = full + 2
+    ins, refs = refs[:count], refs[count:]
+    outs, refs = refs[:count], refs[count:]
+    fins, refs = refs[: len(halves)], refs[len(halves) :]
+    local_sem, zs, zr, s1, r1, s2, r2, a_s, a_r, f_s, f_r, f_l = refs
+    z, y, x = (lax.axis_index(name) for name in FS)
+    core = lax.axis_index("sp")
+    here = 2 * y + x
+    up, down = full, full + 1
+    fly = Flights()
+    x_peer, y_peer = {"xc": 1 - x}, {"yb": 1 - y}
+    diagonal = {"yb": 1 - y, "xc": 1 - x}
+    above, below = {"za": z + 1}, {"za": z - 1}
+    core_peer = {"sp": 1 - core}
+    has_above, has_below = z + 1 < outer, z >= 1
+    greet((x_peer, y_peer, diagonal, core_peer), ((has_above, above), (has_below, below)))
+
+    locals_ = [fly.local(ins[i], outs[i].at[z, y, x], local_sem.at[i]) for i in range(full)]
+    local_up = fly.local(ins[up].at[here], outs[up].at[z, here], local_sem.at[up])
+    local_down = fly.local(ins[down], outs[down].at[z], local_sem.at[down])
+
+    def shard(i, slot):
+        return outs[i].at[slot, y, x] if i < full else outs[i].at[slot]
+
+    def z_send(i, way, hop, source=None):
+        if hop > outer - 2:
+            return
+        slot = z - hop if way == 0 else z + hop
+        when = jnp.logical_and(has_above, slot >= 0) if way == 0 else jnp.logical_and(has_below, slot < outer)
+        fly.send(
+            shard(i, slot) if source is None else source,
+            shard(i, slot),
+            zs.at[i, way, hop],
+            zr.at[i, way, hop],
+            above if way == 0 else below,
+            when,
+        )
+
+    def z_slot(way, hop):
+        slot = z - 1 - hop if way == 0 else z + 1 + hop
+        return slot, (slot >= 0 if way == 0 else slot < outer)
+
+    def z_wait(i, way, hop):
+        slot, when = z_slot(way, hop)
+
+        @pl.when(when)
+        def _():
+            landed(shard(i, slot), zr.at[i, way, hop], below if way == 0 else above)
+
+    def turns(i, slot):
+        turn = (slot + i) % 2
+        first = ((y + turn) % 2, (x + 1 - turn) % 2)
+        second = ((y + 1 - turn) % 2, (x + turn) % 2)
+        return first, second
+
+    def xy_own(i, slot, when=None, source=None):
+        first, second = turns(i, slot)
+        mine = outs[i].at[slot, y, x]
+        source = mine if source is None else source
+        fly.send(source, mine, s1.at[i, slot], r1.at[i, slot], {"yb": first[0], "xc": first[1]}, when)
+        fly.send(source, mine, s2.at[i, slot, 0], r2.at[i, slot, 0], {"yb": second[0], "xc": second[1]}, when)
+
+    def xy_pass(i, slot, when=None):
+        first, second = turns(i, slot)
+        theirs = outs[i].at[slot, first[0], first[1]]
+
+        def wait():
+            landed(theirs, r1.at[i, slot], {"yb": first[0], "xc": first[1]})
+
+        if when is None:
+            wait()
+        else:
+            pl.when(when)(wait)
+        fly.send(theirs, theirs, s2.at[i, slot, 1], r2.at[i, slot, 1], {"yb": second[0], "xc": second[1]}, when)
+
+    def xy_end(i, slot):
+        _, second = turns(i, slot)
+        device = {"yb": second[0], "xc": second[1]}
+        landed(outs[i].at[slot, second[0], second[1]], r2.at[i, slot, 0], device)
+        landed(outs[i].at[slot, 1 - y, 1 - x], r2.at[i, slot, 1], device)
+
+    for i in range(full):
+        for way in range(2):
+            z_send(i, way, 0, ins[i])
+        xy_own(i, z, None, ins[i])
+    for hop in range(outer - 1):
+        for i in range(full):
+            for way in range(2):
+                slot, when = z_slot(way, hop)
+                z_wait(i, way, hop)
+                z_send(i, way, hop + 1)
+                xy_own(i, slot, when)
+        if hop == 0:
+            for turn, device in enumerate((x_peer, y_peer, diagonal)):
+                ty = y if turn == 0 else 1 - y
+                tx = x if turn == 1 else 1 - x
+                fly.send(
+                    ins[up].at[2 * ty + tx],
+                    outs[up].at[z, here],
+                    a_s.at[turn],
+                    a_r.at[turn],
+                    device,
+                )
+    for way in range(2):
+        z_send(down, way, 0, ins[down])
+    local_up.wait()
+    for turn, device in enumerate((x_peer, y_peer, diagonal)):
+        ty = y if turn == 0 else 1 - y
+        tx = x if turn == 1 else 1 - x
+        landed(outs[up].at[z, 2 * ty + tx], a_r.at[turn], device)
+    for way in range(2):
+        z_send(up, way, 0)
+    for i in range(full):
+        xy_pass(i, z)
+    for hop in range(outer - 1):
+        for i in range(full):
+            for way in range(2):
+                slot, when = z_slot(way, hop)
+                xy_pass(i, slot, when)
+        for i in (down, up):
+            for way in range(2):
+                z_wait(i, way, hop)
+                z_send(i, way, hop + 1)
+    for i in range(full):
+        for slot in range(outer):
+            xy_end(i, slot)
+    for copy in locals_:
+        copy.wait()
+    local_down.wait()
+
+    part = outer // 2
+    for j, i in enumerate(halves):
+        width = ins[i].shape[-1]
+        columns = pl.ds(pl.multiple_of(core * width, width), width)
+        theirs = pl.ds((1 - core) * part, part)
+        ours = pl.ds(core * part, part)
+        fly.send(outs[i].at[theirs], fins[j].at[:, :, :, :, columns], f_s.at[j], f_r.at[j], core_peer)
+        fly.local(outs[i].at[ours], fins[j].at[:, :, :, :, columns], f_l.at[j])
+    for j, i in enumerate(halves):
+        width = ins[i].shape[-1]
+        columns = pl.ds(pl.multiple_of(core * width, width), width)
+        others = pl.ds(pl.multiple_of((1 - core) * width, width), width)
+        ours = pl.ds(core * part, part)
+        pltpu.make_async_copy(outs[i].at[ours], fins[j].at[:, :, :, :, columns], f_l.at[j]).wait()
+        landed(fins[j].at[:, :, :, :, others], f_r.at[j], core_peer)
+    fly.drain()
+
+
+def gather_weights(outer, full, halves, up, down):
+    count = len(full) + 2
+    arrays = [*full, up, down]
+    shapes = [jax.ShapeDtypeStruct((outer, 2, 2, *a.shape), a.dtype) for a in full]
+    shapes.append(jax.ShapeDtypeStruct((outer, *up.shape), up.dtype))
+    shapes.append(jax.ShapeDtypeStruct((outer, *down.shape), down.dtype))
+    for i in halves:
+        r, n = full[i].shape
+        shapes.append(jax.ShapeDtypeStruct((outer // 2, 2, 2, r, 2 * n), full[i].dtype))
+    dma = pltpu.SemaphoreType.DMA
+    hops = outer - 1
+    nf, nh = len(full), len(halves)
+    results = pl.pallas_call(
+        functools.partial(gather_kernel, outer, nf, halves),
+        out_shape=shapes,
+        in_specs=[VM] * count,
+        out_specs=[ANY] * len(shapes),
+        scratch_shapes=[
+            dma((count,)),
+            dma((count, 2, hops)),
+            dma((count, 2, hops)),
+            dma((nf, outer)),
+            dma((nf, outer)),
+            dma((nf, outer, 2)),
+            dma((nf, outer, 2)),
+            dma((3,)),
+            dma((3,)),
+            dma((nh,)),
+            dma((nh,)),
+            dma((nh,)),
+        ],
+        compiler_params=pltpu.CompilerParams(collective_id=0, has_side_effects=True),
+        name="gather_weights",
+    )(*arrays)
+    gathered = [v.reshape(-1, v.shape[-1]) for v in results[: nf + 2]]
+    for j, i in enumerate(halves):
+        gathered[i] = results[nf + 2 + j].reshape(-1, results[nf + 2 + j].shape[-1])
+    return gathered, results[: nf + 2]
+
+
+def plane_gather_kernel(own_ref, out_ref, local_sem, send, recv):
+    y, x, core = lax.axis_index("yb"), lax.axis_index("xc"), lax.axis_index("sp")
+    x_peer, y_peer, core_peer = {"xc": 1 - x}, {"yb": 1 - y}, {"sp": 1 - core}
+    fly = Flights()
+    greet((x_peer, y_peer, core_peer))
+    size = own_ref.shape[0] // 2
+    top, low = pl.ds(0, size), pl.ds(size, size)
+    local = fly.local(own_ref, out_ref.at[y, x, core], local_sem.at[0])
+
+    def place(ty, tx, rows):
+        return out_ref.at[ty, tx, core, rows]
+
+    fly.send(own_ref.at[top], place(y, x, top), send.at[0], recv.at[0], x_peer)
+    fly.send(own_ref.at[low], place(y, x, low), send.at[1], recv.at[1], y_peer)
+    fly.send(own_ref.at[low], place(y, x, low), send.at[2], recv.at[2], x_peer)
+    fly.send(own_ref.at[top], place(y, x, top), send.at[3], recv.at[3], y_peer)
+    fly.send(own_ref, out_ref.at[y, x, core], send.at[4], recv.at[4], core_peer)
+
+    def arrive(index, ty, tx, rows, device):
+        landed(place(ty, tx, rows), recv.at[index], device)
+        fly.send(place(ty, tx, rows), place(ty, tx, rows), send.at[index + 5], recv.at[index + 5], core_peer)
+
+    arrive(0, y, 1 - x, top, x_peer)
+    fly.send(place(y, 1 - x, top), place(y, 1 - x, top), send.at[12], recv.at[12], y_peer)
+    arrive(1, 1 - y, x, low, y_peer)
+    fly.send(place(1 - y, x, low), place(1 - y, x, low), send.at[13], recv.at[13], x_peer)
+    arrive(2, y, 1 - x, low, x_peer)
+    arrive(3, 1 - y, x, top, y_peer)
+    for index, rows, device in ((0, top, y_peer), (1, low, x_peer)):
+        landed(place(1 - y, 1 - x, rows), recv.at[12 + index], device)
+        fly.send(
+            place(1 - y, 1 - x, rows), place(1 - y, 1 - x, rows), send.at[10 + index], recv.at[10 + index], core_peer
+        )
+    other = 1 - core
+    landed(out_ref.at[y, x, other], recv.at[4], core_peer)
+    for index, ty, tx, rows in (
+        (5, y, 1 - x, top),
+        (6, 1 - y, x, low),
+        (7, y, 1 - x, low),
+        (8, 1 - y, x, top),
+        (10, 1 - y, 1 - x, top),
+        (11, 1 - y, 1 - x, low),
+    ):
+        landed(out_ref.at[ty, tx, other, rows], recv.at[index], core_peer)
+    local.wait()
+    fly.drain()
+
+
+def plane_gather(own):
+    rows, width = own.shape
+    dma = pltpu.SemaphoreType.DMA
+    out = pl.pallas_call(
+        plane_gather_kernel,
+        out_shape=jax.ShapeDtypeStruct((2, 2, 2, rows, width), own.dtype),
+        in_specs=[VM],
+        out_specs=VM,
+        scratch_shapes=[dma((1,)), dma((14,)), dma((14,))],
+        compiler_params=pltpu.CompilerParams(collective_id=1, has_side_effects=True),
+        name="plane_gather",
+    )(own)
+    return out.reshape(8 * rows, width)
+
+
+def plane_sum_kernel(part_ref, out_ref, core_in, first, second, keep, send, recv):
+    y, x, core = lax.axis_index("yb"), lax.axis_index("xc"), lax.axis_index("sp")
+    x_peer, y_peer, core_peer = {"xc": 1 - x}, {"yb": 1 - y}, {"sp": 1 - core}
+    fly = Flights()
+    greet((x_peer, y_peer, core_peer))
+    rows = part_ref.shape[3]
+    size = rows // 2
+    top, low = pl.ds(0, size), pl.ds(size, size)
+    chips = ((1 - y, 1 - x), (1 - y, x), (y, 1 - x), (y, x))
+    for index, (ty, tx) in enumerate(chips):
+        fly.send(
+            part_ref.at[ty, tx, 1 - core], core_in.at[index], send.at[index], recv.at[index], core_peer
+        )
+
+    def own_part(index):
+        ty, tx = chips[index]
+        return part_ref.at[ty, tx, core]
+
+    def core_sum(index):
+        landed(core_in.at[index], recv.at[index], core_peer)
+        row_add(core_in.at[index], core_in.at[index], own_part(index), rows)
+
+    core_sum(0)
+    fly.send(core_in.at[0, top], first.at[0], send.at[4], recv.at[4], y_peer)
+    fly.send(core_in.at[0, low], first.at[1], send.at[5], recv.at[5], x_peer)
+    core_sum(1)
+    fly.send(core_in.at[1, top], first.at[2], send.at[6], recv.at[6], y_peer)
+    core_sum(2)
+    fly.send(core_in.at[2, low], first.at[3], send.at[7], recv.at[7], x_peer)
+    core_sum(3)
+    landed(first.at[0], recv.at[4], y_peer)
+    row_add(second.at[0], first.at[0], core_in.at[2, top], size)
+    fly.send(second.at[0], second.at[2], send.at[8], recv.at[8], x_peer)
+    landed(first.at[1], recv.at[5], x_peer)
+    row_add(second.at[1], first.at[1], core_in.at[1, low], size)
+    fly.send(second.at[1], second.at[3], send.at[9], recv.at[9], y_peer)
+    landed(first.at[2], recv.at[6], y_peer)
+    row_add(keep.at[top], first.at[2], core_in.at[3, top], size)
+    landed(first.at[3], recv.at[7], x_peer)
+    row_add(keep.at[low], first.at[3], core_in.at[3, low], size)
+    landed(second.at[2], recv.at[8], x_peer)
+    row_add(out_ref.at[top], keep.at[top], second.at[2], size)
+    landed(second.at[3], recv.at[9], y_peer)
+    row_add(out_ref.at[low], keep.at[low], second.at[3], size)
+    fly.drain()
+
+
+def plane_sum(partial):
+    rows, width = partial.shape[0] // 8, partial.shape[1]
+    dma = pltpu.SemaphoreType.DMA
+    return pl.pallas_call(
+        plane_sum_kernel,
+        out_shape=jax.ShapeDtypeStruct((rows, width), F32),
+        in_specs=[VM],
+        out_specs=VM,
+        scratch_shapes=[
+            pltpu.VMEM((4, rows, width), BF),
+            pltpu.VMEM((4, rows // 2, width), BF),
+            pltpu.VMEM((4, rows // 2, width), BF),
+            pltpu.VMEM((rows, width), F32),
+            dma((10,)),
+            dma((10,)),
+        ],
+        compiler_params=pltpu.CompilerParams(collective_id=2, has_side_effects=True),
+        name="plane_sum",
+    )(partial.reshape(2, 2, 2, rows, width))
+
+
+AHEAD, LAG_PLANE, LAG_CHAIN = 6, 2, 4
+
+
+def reduce_kernel(outer, kinds, *refs):
+    count = len(kinds)
+    shards = outer * PLANE
+    gs, refs = refs[:count], refs[count:]
+    frames_ref, small_ref, refs = refs[0], refs[1], refs[2:]
+    outs, refs = refs[:count], refs[count:]
+    frames_out, small_out, refs = refs[0], refs[1], refs[2:]
+    near, refs = refs[:count], refs[count:]
+    plane, refs = refs[:count], refs[count:]
+    chain, refs = refs[:count], refs[count:]
+    split = [i for i, kind in enumerate(kinds) if kind[1]]
+    whole, refs = refs[: len(split)], refs[len(split) :]
+    small_in, small_own, small_peer, refs = refs[0], refs[1], refs[2], refs[3:]
+    e_s, e_r, e_l, s1, r1, s2, r2, zs, zr, o_s, o_r, f_s, f_r, m_s, m_r, l_s = refs
+    z, y, x = (lax.axis_index(name) for name in FS)
+    core = lax.axis_index("sp")
+    here = (z * 2 + y) * 2 + x
+    core_peer = {"sp": 1 - core}
+    above, below = {"za": z + 1}, {"za": z - 1}
+    fly = Flights()
+
+    def chip(index):
+        return {"za": index // 4, "yb": (index // 2) % 2, "xc": index % 2}
+
+    others = [(here + j) % shards for j in range(1, shards)]
+    greet((core_peer, *[chip(index) for index in others]))
+
+    part = outer // 2
+    source = list(gs)
+    for j, i in enumerate(split):
+        width = whole[j].shape[-1]
+        mine = pl.ds(pl.multiple_of(core * width, width), width)
+        theirs = pl.ds(pl.multiple_of((1 - core) * width, width), width)
+        ours = pl.ds(core * part, part)
+        fly.send(gs[i].at[:, :, :, :, theirs], whole[j].at[ours], e_s.at[j], e_r.at[j], core_peer)
+        fly.local(gs[i].at[:, :, :, :, mine], whole[j].at[ours], e_l.at[j])
+        source[i] = whole[j]
+
+    def joined(i):
+        j = split.index(i)
+        width = whole[j].shape[-1]
+        mine = pl.ds(pl.multiple_of(core * width, width), width)
+        ours, other = pl.ds(core * part, part), pl.ds((1 - core) * part, part)
+        pltpu.make_async_copy(gs[i].at[:, :, :, :, mine], whole[j].at[ours], e_l.at[j]).wait()
+        landed(whole[j].at[other], e_r.at[j], core_peer)
+
+    frame_copy = fly.local(frames_ref, frames_out.at[here], l_s.at[0])
+    small_copy = fly.local(small_ref.at[here], small_in.at[here], l_s.at[1])
+    for j, index in enumerate(others):
+        fly.send(frames_ref, frames_out.at[here], f_s.at[j], f_r.at[here], chip(index))
+        fly.send(small_ref.at[index], small_in.at[here], m_s.at[j], m_r.at[here], chip(index))
+
+    def slot_at(step):
+        if step == outer - 1:
+            return z
+        falling = outer - 1 - step
+        falling = jnp.where(falling > z, falling, falling - 1)
+        rising = jnp.where(step < z, step, step + 1)
+        return jnp.where(z < part, falling, rising)
+
+    units = [(slot_at(step), i) for step in range(outer) for i in range(count)]
+
+    def turns(i, slot):
+        turn = (slot + i) % 2
+        first = ((y + 1 - turn) % 2, (x + turn) % 2)
+        second = ((y + turn) % 2, (x + 1 - turn) % 2)
+        return first, second
+
+    def device(place):
+        return {"yb": place[0], "xc": place[1]}
+
+    def start(slot, i):
+        first, _ = turns(i, slot)
+        fly.send(
+            source[i].at[slot, 1 - y, 1 - x], near[i].at[slot, 1], s1.at[i, slot, 1], r1.at[i, slot, 1], device(first)
+        )
+        fly.send(
+            source[i].at[slot, first[0], first[1]], near[i].at[slot, 0], s1.at[i, slot, 0], r1.at[i, slot, 0], device(first)
+        )
+
+    def pass_on(slot, i):
+        first, second = turns(i, slot)
+        rows = near[i].shape[2]
+        landed(near[i].at[slot, 1], r1.at[i, slot, 1], device(first))
+        row_add(near[i].at[slot, 1], near[i].at[slot, 1], source[i].at[slot, second[0], second[1]], rows)
+        fly.send(near[i].at[slot, 1], plane[i].at[slot], s2.at[i, slot], r2.at[i, slot], device(second))
+        landed(near[i].at[slot, 0], r1.at[i, slot, 0], device(first))
+        row_add(near[i].at[slot, 0], near[i].at[slot, 0], source[i].at[slot, y, x], rows)
+
+    def plane_total(slot, i):
+        _, second = turns(i, slot)
+        rows = near[i].shape[2]
+        landed(plane[i].at[slot], r2.at[i, slot], device(second))
+        row_add(plane[i].at[slot], plane[i].at[slot], near[i].at[slot, 0], rows)
+
+    def along(slot, i, last):
+        rows = near[i].shape[2]
+        if not last:
+            for way, when, edge, ahead, behind in (
+                (1, slot < z, z == outer - 1, below, above),
+                (0, slot > z, z == 0, above, below),
+            ):
+
+                @pl.when(jnp.logical_and(when, jnp.logical_not(edge)))
+                def _():
+                    landed(chain[i].at[way, slot], zr.at[i, way, slot], behind)
+                    row_add(plane[i].at[slot], plane[i].at[slot], chain[i].at[way, slot], rows)
+
+                fly.send(
+                    plane[i].at[slot], chain[i].at[way, slot], zs.at[i, way, slot], zr.at[i, way, slot], ahead, when
+                )
+            return
+        parts = kinds[i][0]
+        width = plane[i].shape[-1] // parts
+        for way, when, behind in ((1, z < outer - 1, above), (0, z > 0, below)):
+
+            @pl.when(when)
+            def _():
+                landed(chain[i].at[way, slot], zr.at[i, way, slot], behind)
+
+        step = 16 if rows % 16 == 0 else rows
+        has_above, has_below = z < outer - 1, z > 0
+
+        def chunk(index, carry):
+            at = pl.ds(pl.multiple_of(index * step, step), step)
+            for part_no in range(parts):
+                span = slice(part_no * width, (part_no + 1) * width)
+                total = plane[i][slot, at, span].astype(F32)
+                upper = chain[i][1, slot, at, span].astype(F32)
+                lower = chain[i][0, slot, at, span].astype(F32)
+                total = total + jnp.where(has_above, upper, 0.0) + jnp.where(has_below, lower, 0.0)
+                column = pl.multiple_of((2 * part_no + core) * width, width)
+                outs[i][at, pl.ds(column, width)] = total
+            return carry
+
+        lax.fori_loop(0, rows // step, chunk, 0)
+        for part_no in range(parts):
+            column = pl.multiple_of((2 * part_no + core) * width, width)
+            block = outs[i].at[:, pl.ds(column, width)]
+            fly.send(block, block, o_s.at[i, part_no], o_r.at[i, part_no], core_peer)
+
+    waiting = set(split)
+
+    def begin(unit):
+        slot, i = units[unit]
+        if i in waiting:
+            joined(i)
+            waiting.discard(i)
+        start(slot, i)
+
+    for unit in range(min(AHEAD, len(units))):
+        begin(unit)
+    for tick in range(len(units) + LAG_CHAIN):
+        if tick < len(units):
+            pass_on(*units[tick])
+            if tick + AHEAD < len(units):
+                begin(tick + AHEAD)
+        if 0 <= tick - LAG_PLANE < len(units):
+            plane_total(*units[tick - LAG_PLANE])
+        if 0 <= tick - LAG_CHAIN < len(units):
+            unit = tick - LAG_CHAIN
+            along(*units[unit], unit >= (outer - 1) * count)
+
+    small_copy.wait()
+    frame_copy.wait()
+    for index in others:
+        landed(small_in.at[index], m_r.at[index], chip(index))
+    small_own[...] = jnp.sum(small_in[...], axis=0)
+    fly.send(small_own, small_peer, l_s.at[2], l_s.at[3], core_peer)
+    for index in others:
+        landed(frames_out.at[index], f_r.at[index], chip(index))
+    landed(small_peer, l_s.at[3], core_peer)
+    small_out[...] = small_own[...] + small_peer[...]
+    for i in range(count):
+        parts = kinds[i][0]
+        width = plane[i].shape[-1] // parts
+        for part_no in range(parts):
+            column = pl.multiple_of((2 * part_no + 1 - core) * width, width)
+            landed(outs[i].at[:, pl.ds(column, width)], o_r.at[i, part_no], core_peer)
+    fly.drain()
+
+
+def reduce_weights(outer, kinds, grads, frames, small):
+    shards = outer * PLANE
+    count = len(kinds)
+    shaped, shapes, near, plane, chain, whole = [], [], [], [], [], []
+    for (parts, split), grad in zip(kinds, grads, strict=True):
+        lead = outer // 2 if split else outer
+        rows = grad.shape[0] // (lead * PLANE)
+        width = grad.shape[1] // 2 if split else grad.shape[1]
+        shaped.append(grad.reshape(lead, 2, 2, rows, grad.shape[1]))
+        shapes.append(jax.ShapeDtypeStruct((rows, 2 * width), F32))
+        near.append(pltpu.VMEM((outer, 2, rows, width), BF))
+        plane.append(pltpu.VMEM((outer, rows, width), BF))
+        chain.append(pltpu.VMEM((2, outer, rows, width), BF))
+        if split:
+            whole.append(pltpu.VMEM((outer, 2, 2, rows, width), BF))
+    shapes.append(jax.ShapeDtypeStruct((shards, *frames.shape), frames.dtype))
+    shapes.append(jax.ShapeDtypeStruct(small.shape[1:], F32))
+    dma = pltpu.SemaphoreType.DMA
+    nsplit = len(whole)
+    results = pl.pallas_call(
+        functools.partial(reduce_kernel, outer, kinds),
+        out_shape=shapes,
+        in_specs=[VM] * (count + 2),
+        out_specs=[VM] * count + [VM, VM],
+        scratch_shapes=[
+            *near,
+            *plane,
+            *chain,
+            *whole,
+            pltpu.VMEM(small.shape, F32),
+            pltpu.VMEM(small.shape[1:], F32),
+            pltpu.VMEM(small.shape[1:], F32),
+            dma((nsplit,)),
+            dma((nsplit,)),
+            dma((nsplit,)),
+            dma((count, outer, 2)),
+            dma((count, outer, 2)),
+            dma((count, outer)),
+            dma((count, outer)),
+            dma((count, 2, outer)),
+            dma((count, 2, outer)),
+            dma((count, 3)),
+            dma((count, 3)),
+            dma((shards,)),
+            dma((shards,)),
+            dma((shards,)),
+            dma((shards,)),
+            dma((4,)),
+        ],
+        compiler_params=pltpu.CompilerParams(
+            collective_id=3, has_side_effects=True, vmem_limit_bytes=67043328
+        ),
+        name="reduce_weights",
+    )(*shaped, frames, small)
+    return results[:count], results[count], results[count + 1]
 
 
 def gather(value, axes, axis=0):
@@ -249,20 +885,11 @@
     chip = lax.axis_index(FS)
     own_frame = core * frame_count
 
-    small = jnp.concatenate(
-        [mod_bias[0].astype(F32), qk_gains[0].reshape(-1).astype(F32), timestep[0].astype(F32)]
-    )
-    small_all = gather(small[None], FS)
     bias_len, gain_len = mod_bias.shape[1], qk_gains.shape[2]
-    bias_all = small_all[:, :bias_len].reshape(-1)
-    gain_all = (
-        small_all[:, bias_len : bias_len + 4 * gain_len]
-        .reshape(shards, 4, gain_len)
-        .transpose(1, 0, 2)
-        .reshape(4, 2, half)
-    )
-    gain_own = lax.dynamic_index_in_dim(gain_all, core, 1, keepdims=False)
-    steps_all = small_all[:, bias_len + 4 * gain_len :].reshape(-1)
+    small_len = bias_len + 4 * gain_len
+    small_rows = 8
+    small_width = -(-(small_len + group_frames) // (small_rows * 128)) * 128
+    small_room = small_rows * small_width
 
     def own_half(weight, parts):
         shaped = weight[0].reshape(weight.shape[1], parts, 2, -1)
@@ -270,23 +897,48 @@
             weight.shape[1], -1
         )
 
-    mod_matrix = gather(own_half(mod_weight, 1), FS)
-    self_proj = gather(own_half(self_in, 3), FS)
-    self_back = swap(gather(own_half(self_out, 1), FS), 0, 1)
-    cross_kvproj = gather(own_half(cross_kv, 2), FS)
-    cross_qproj = gather(own_half(cross_q, 1), FS)
-    cross_back = swap(gather(own_half(cross_out, 1), FS), 0, 1)
-
+    small = jnp.concatenate(
+        [
+            mod_bias[0].astype(F32),
+            qk_gains[0].reshape(-1).astype(F32),
+            timestep[0].astype(F32),
+            jnp.zeros((small_room - small_len - group_frames,), F32),
+        ]
+    ).reshape(small_rows, small_width)
     hid = mlp_out.shape[1] // 2
     in_rows = mlp_in.shape[1]
     up_part = lax.dynamic_index_in_dim(
         mlp_in[0].reshape(in_rows, outer, PLANE, 2, hid), core, 3, keepdims=False
     )
-    up_part = up_part.transpose(2, 0, 1, 3).reshape(PLANE * in_rows, outer * hid)
-    up_part = lax.all_to_all(up_part, PL, split_axis=0, concat_axis=0, tiled=True)
-    up_matrix = gather(up_part, "za")
+    up_part = up_part.transpose(2, 0, 1, 3).reshape(PLANE, in_rows, outer * hid)
     down_part = lax.dynamic_slice_in_dim(mlp_out[0], core * hid, hid, 0)
-    down_matrix = gather(down_part, "za")
+    gathered, raw = gather_weights(
+        outer,
+        [
+            small,
+            own_half(mod_weight, 1),
+            own_half(self_in, 3),
+            own_half(self_out, 1),
+            own_half(cross_kv, 2),
+            own_half(cross_q, 1),
+            own_half(cross_out, 1),
+        ],
+        (3, 6),
+        up_part,
+        down_part,
+    )
+    small_all, mod_matrix, self_proj, self_back, cross_kvproj, cross_qproj, cross_back = gathered[:7]
+    up_matrix, down_matrix = gathered[7:]
+    small_all = small_all.reshape(shards, small_room)
+    bias_all = small_all[:, :bias_len].reshape(-1)
+    gain_all = (
+        small_all[:, bias_len:small_len]
+        .reshape(shards, 4, gain_len)
+        .transpose(1, 0, 2)
+        .reshape(4, 2, half)
+    )
+    gain_own = lax.dynamic_index_in_dim(gain_all, core, 1, keepdims=False)
+    steps_all = small_all[:, small_len : small_len + group_frames].reshape(-1)
 
     live_keys = clip_frames * FRAME_TOK
     all_keys = jnp.full((1,), TXT, jnp.int32)
@@ -336,36 +988,31 @@
     residual = residual + scatter(product(cross_mixed, cross_back), "sp")
 
     mlp_float, back_mlp_input = jax.vjp(modulated, residual, shift_two, scale_two)
-    mlp_input = gather(gather(mlp_float.astype(BF), PL), "sp")
+    mlp_input = plane_gather(mlp_float.astype(BF))
     up_proj = product(mlp_input, up_matrix)
     activated_float, back_gelu = jax.vjp(
         lambda inner: jax.nn.gelu(inner, approximate=True), up_proj
     )
     activated = activated_float.astype(BF)
 
-    def plane_sum(partial):
-        half_sum = scatter(partial, "sp")
-        return scatter(half_sum.astype(BF), PL).astype(F32)
-
-    mlp_branch = plane_sum(product(activated, down_matrix))
+    mlp_branch = plane_sum(product(activated, down_matrix).astype(BF))
     output = (residual + frame_scaled(mlp_branch, gate_two)).astype(BF)
 
     grad_rows = cotangent.astype(F32)
     grad_branch = frame_scaled(grad_rows, gate_two).astype(BF)
     grad_gate_two = frame_sum(grad_rows * mlp_branch, frame_count)
-    grad_branch_all = gather(gather(grad_branch, PL), "sp")
+    grad_branch_all = plane_gather(grad_branch)
     grad_down = product_tn(activated, grad_branch_all).astype(BF)
     down_owned = scatter(grad_down, "za")
     grad_up_low = back_gelu(product_nt(grad_branch_all, down_matrix))[0].astype(BF)
     grad_up = product_tn(mlp_input, grad_up_low).astype(BF)
     up_owned = scatter(grad_up, "za")
-    grad_mlp_input = plane_sum(product_nt(grad_up_low, up_matrix))
+    grad_mlp_input = plane_sum(product_nt(grad_up_low, up_matrix).astype(BF))
     grad_from_mlp, grad_shift_two, grad_scale_two = back_mlp_input(grad_mlp_input)
     grad_rows = grad_rows + grad_from_mlp
 
     grad_low = gather(grad_rows.astype(BF), "sp")
-    grad_cross_back = swap(product_tn(cross_mixed, grad_low).astype(BF), 1, 0)
-    cross_back_owned = scatter(grad_cross_back, FS)
+    grad_cross_back = product_tn(cross_mixed, grad_low).astype(BF)
     grad_cross_mixed = product_nt(grad_low, cross_back).astype(BF)
     grad_cq, grad_ck, grad_cv = attend_backward(
         all_keys, cross_query, cross_key, cross_value, cross_lse, grad_cross_mixed
@@ -381,15 +1028,14 @@
     grad_text_low = jnp.concatenate(
         [rms_finish(raw_ck, inv_ck, scaled_ck, dots_ck).astype(BF), grad_cv], axis=1
     )
-    cross_q_owned = scatter(product_tn(cross_input, grad_cross_low).astype(BF), FS)
-    cross_kv_owned = scatter(product_tn(text_all, grad_text_low).astype(BF), FS)
+    grad_cross_qproj = product_tn(cross_input, grad_cross_low).astype(BF)
+    grad_cross_kvproj = product_tn(text_all, grad_text_low).astype(BF)
     grad_cross_input = scatter(product_nt(grad_cross_low, cross_qproj), "sp")
     grad_rows = grad_rows + back_cross_norm(grad_cross_input)[0]
 
     grad_gate_one = frame_sum(grad_rows * self_branch, frame_count)
     grad_self_low = gather(frame_scaled(grad_rows, gate_one).astype(BF), "sp")
-    grad_self_back = swap(product_tn(self_mixed, grad_self_low).astype(BF), 1, 0)
-    self_back_owned = scatter(grad_self_back, FS)
+    grad_self_back = product_tn(self_mixed, grad_self_low).astype(BF)
     grad_self_mixed = product_nt(grad_self_low, self_back).astype(BF)
     grad_q, grad_k, grad_v = attend_backward(
         live_keys, query, key, value, self_lse, grad_self_mixed
@@ -409,7 +1055,7 @@
         ],
         axis=1,
     )
-    self_in_owned = scatter(product_tn(attn_input, grad_joined_low).astype(BF), FS)
+    grad_self_proj = product_tn(attn_input, grad_joined_low).astype(BF)
     grad_attn_input = scatter(product_nt(grad_joined_low, self_proj), "sp")
     grad_from_attn, grad_shift_one, grad_scale_one = back_attn_input(grad_attn_input)
     grad_rows = grad_rows + grad_from_attn
@@ -419,12 +1065,6 @@
         axis=1,
     )
     grad_mod_half = swap(grad_modulation, 1, 0)
-    grad_mod_all = gather(grad_mod_half.astype(BF), FS)
-    sinus_all = sinus_features(steps_all).astype(BF)
-    own_features = mod_weight.shape[1]
-    sinus_own = lax.dynamic_slice_in_dim(sinus_all, chip * own_features, own_features, 1)
-    mod_weight_grad = gather(product_tn(sinus_own, grad_mod_all), "sp", 1)
-
     grad_gains = jnp.stack([grad_gain_zero, grad_gain_one, grad_gain_two, grad_gain_three])
     both = jnp.arange(2)[None, :, None] == core
     grad_gains = jnp.where(both, grad_gains[:, None, :], 0.0).reshape(4, shards, gain_len)
@@ -432,16 +1072,26 @@
         [
             jnp.sum(grad_modulation, axis=0).reshape(shards, bias_len),
             grad_gains.transpose(1, 0, 2).reshape(shards, 4 * gain_len),
+            jnp.zeros((shards, small_room - small_len), F32),
         ],
         axis=1,
-    )
-    small_owned = lax.psum(scatter(grad_small, FS), "sp")[0]
-
-    def join(owned, parts):
-        rows = owned.shape[0]
-        pair = gather(owned.reshape(1, rows, parts, -1), "sp").astype(F32)
-        return pair.transpose(1, 2, 0, 3).reshape(1, rows, -1)
-
+    ).reshape(shards, small_rows, small_width)
+    owned, grad_mod_all, small_owned = reduce_weights(
+        outer,
+        ((1, False), (2, False), (1, True), (1, True), (3, False)),
+        [grad_cross_qproj, grad_cross_kvproj, grad_cross_back, grad_self_back, grad_self_proj],
+        grad_mod_half.astype(BF),
+        grad_small,
+    )
+    cross_q_grad, cross_kv_grad, cross_out_grad, self_out_grad, self_in_grad = owned
+    small_owned = small_owned.reshape(-1)[:small_len]
+    sinus_all = sinus_features(steps_all).astype(BF)
+    own_features = mod_weight.shape[1]
+    sinus_own = lax.dynamic_slice_in_dim(sinus_all, chip * own_features, own_features, 1)
+    grad_mod_all = grad_mod_all.reshape(-1, grad_mod_half.shape[1])
+    mod_weight_grad = gather(product_tn(sinus_own, grad_mod_all), "sp", 1)
+
+    up_owned, down_owned, small_owned = lax.optimization_barrier((up_owned, down_owned, small_owned))
     up_rows = lax.all_to_all(up_owned, PL, split_axis=0, concat_axis=0, tiled=True)
     up_pair = gather(up_rows.reshape(1, PLANE, in_rows, outer, hid), "sp").astype(F32)
     mlp_in_grad = up_pair.transpose(2, 3, 1, 0, 4).reshape(1, in_rows, -1)
@@ -451,11 +1101,11 @@
         mod_weight_grad[None],
         small_owned[None, :bias_len],
         small_owned[bias_len:].reshape(1, 4, gain_len),
-        join(self_in_owned, 3),
-        join(self_back_owned, 1),
-        join(cross_q_owned, 1),
-        join(cross_kv_owned, 2),
-        join(cross_back_owned, 1),
+        self_in_grad[None],
+        self_out_grad[None],
+        cross_q_grad[None],
+        cross_kv_grad[None],
+        cross_out_grad[None],
         mlp_in_grad,
         gather(down_owned, "sp").astype(F32)[None],
     )

time: 1800 us -> 923 us (0.51)
  waiting for transfers between devices: 1150 us -> 5.26 us
  Pallas kernels: 20.7 us -> 593 us
  blocking collectives: 305 us -> 42.6 us
  local copies, waits for them, and re-layouts: 128 us -> 92.5 us
    pallas_call x0 -> x6, Pallas kernels: none -> 573 us  [the longest x1 281 us: gather_weights(): pl.pallas_call(functools.partial(gather_kernel, outer, nf, halves), out_s...]
    reduce_scatter x14 -> x5, waiting for transfers between devices: 539 us -> 4.23 us  [scatter(): return lax.psum_scatter(value, axes, scatter_dimension=axis, tiled=True)]
    all_gather x15 -> x3, waiting for transfers between devices: 469 us -> 0.02 us  [gather(): return lax.all_gather(value, axes, axis=axis, tiled=True)]
    unnamed x2 -> x0, blocking collectives: 155 us -> none
    unnamed x31 -> x10, waiting for transfers between devices: 140 us -> 0.83 us
    all_gather x11 -> x5, blocking collectives: 67.1 us -> 11.9 us  [gather(): return lax.all_gather(value, axes, axis=axis, tiled=True)]
    all_to_all x5 -> x1, blocking collectives: 36.1 us -> 3.75 us  [swap(): lax.all_to_all(value, 'sp', split_axis=split_axis, concat_axis=concat_axi...]
  transfers between devices with their start and end apart: 31 -> 10, of which waited for: 23 -> 2; matrix products, arithmetic and copies ran while one was open for 13% -> 16% of each run, Pallas kernels for 0% -> 56%
where the time goes in v2:
time: 923 us; the launch traced here: 915 us
  Pallas kernels  593 us (64%)
  matrix products  101 us (11%)
  local copies, waits for them, and re-layouts  92.5 us (10%)
  other arithmetic  59.2 us (6%)
  blocking collectives  42.6 us (5%)
  between operations  16.2 us (2%)
    pallas_call x1, Pallas kernels, gather_weights(): pl.pallas_call(functools.partial(gather_kernel, outer, nf, halves), out_s...  281 us
    pallas_call x1, Pallas kernels, reduce_weights(): pl.pallas_call(functools.partial(reduce_kernel, outer, kinds), out_shape=...  211 us
    dot_general x8, matrix products, product(): return jnp.dot(left, right, preferred_element_type=F32)  40.7 us
    pallas_call x2, Pallas kernels, plane_sum(): pl.pallas_call(plane_sum_kernel, out_shape=jax.ShapeDtypeStruct((rows, wi...  40.4 us
    pallas_call x2, Pallas kernels, plane_gather(): pl.pallas_call(plane_gather_kernel, out_shape=jax.ShapeDtypeStruct((2, 2,...  40.2 us
    dot_general x8, matrix products, product_tn(): lax.dot_general(left, right, (((0,), (0,)), ((), ())), preferred_element_...  32.4 us
    dot_general x6, matrix products, product_nt(): lax.dot_general(left, right, (((1,), (1,)), ((), ())), preferred_element_...  28 us
    unnamed x260, local copies, waits for them, and re-layouts  21.2 us
  transfers between devices with their start and end apart: 10, of which 2 were waited for; matrix products, arithmetic and copies ran while one was open for 16% of the time, Pallas kernels for 56%

profile of v2, /device:TPU:0, one launch (start us, length us, event | category | flops | bytes accessed | tf_op | source)
XLA Modules:
  0.0 914.8 jit_solution(13997920757059946743)
XLA Ops:
  23.7 5.8 reshape_squeeze.28
  41.6 281.3 %gather_weights.1 = (f32[4,2,2,8,128]{4,3,2,1,0:T(8,128)}, bf16[4,2,2,16,4608]{4,3,2,1,0:T(8,128)(2,1)}, bf16[4,2,2,96,2304]{4,3,2,1,0:T(8,128)(2,1)}, bf16[4,2,...) custom-call(f32[8,128]{1,0:T(8,128)} %maximum_bitcast_fusion.1.refs_, ...), custom_call_target="tpu_custom_call" | custom-call | tf_op jit(solution)/shard_map/gather_weights/pallas_call | solution.py:430
  334.7 5.3 fusion.89
  363.9 7.1 convolution_bitcast_fusion
  388.0 5.3 shard_map.239
  398.3 20.1 %plane_gather.3 = bf16[2,2,2,128,1536]{4,3,2,1,0:T(8,128)(2,1)} custom-call(bf16[128,1536]{1,0:T(8,128)(2,1)} %fusion.37.own_ref), custom_call_target="tpu_custom_call" | custom-call | tf_op jit(solution)/shard_map/plane_gather/pallas_call | solution.py:509
  418.4 8.8 fusion.92
  430.6 20.1 %plane_gather.2 = bf16[2,2,2,128,1536]{4,3,2,1,0:T(8,128)(2,1)} custom-call(bf16[128,1536]{1,0:T(8,128)(2,1)} %get-tuple-element.100.own_ref), custom_call_target="tpu_custom_call" | custom-call | tf_op jit(solution)/shard_map/plane_gather/pallas_call | solution.py:509
  450.7 10.9 %fusion.6 = (bf16[1024,1120]{0,1:T(8,128)(2,1)S(1)}, f32[1024,1120]{0,1:T(8,128)S(1)}) fusion(f32[1024,1120]{0,1:T(8,128)} %fusion.92, bf16[1024,1536]{1,0:T(8,128)(2,1)} %bitcast.220, bf16[1536,1120]{1,0:T(8,128)(2,1)} %bitcast.295), kind=kOutput, calls=%fused_computation.13 | convolution fusion | flops 3546152960 | bytes 18055168 | tf_op jit(solution)/shard_map/dot_general | solution.py:33
  461.7 5.8 convolution_convert_fusion.5
  467.5 5.9 convolution_convert_fusion.4
  473.5 20.4 %plane_sum.3 = f32[128,1536]{1,0:T(8,128)} custom-call(bf16[2,2,2,128,1536]{4,3,2,1,0:T(8,128)(2,1)} %bitcast.227), custom_call_target="tpu_custom_call" | custom-call | tf_op jit(solution)/shard_map/plane_sum/pallas_call | solution.py:571
  493.9 20.0 %plane_sum.2 = f32[128,1536]{1,0:T(8,128)} custom-call(bf16[2,2,2,128,1536]{4,3,2,1,0:T(8,128)(2,1)} %bitcast.226), custom_call_target="tpu_custom_call" | custom-call | tf_op jit(solution)/shard_map/plane_sum/pallas_call | solution.py:571
  522.9 6.7 shard_map.240
  555.4 5.2 shard_map.241
  579.9 6.3 fusion.41
  586.3 7.0 convolution_convert_fusion.1
  593.3 5.7 copy.138
  599.1 9.1 convolution_convert_fusion.2
  623.5 4.9 convolution_convert_fusion
  639.6 210.8 %reduce_weights.1 = (f32[96,1536]{1,0:T(8,128)}, f32[96,3072]{1,0:T(8,128)}, f32[96,1536]{1,0:T(8,128)}, f32[96,1536]{1,0:T(8,128)}, f32[96,4608]{1,0:T(8,128)},...) custom-call(bf16[4,2,2,96,768]{4,3,2,1,0:T(8,128)(2,1)} %bitcast.209, bf16[4,2,2,96,1536]{4,3,2,1,0:T(8,128)(2,1)} %bitcast.212, ...), custom_call_target="tpu_custom_call" | custom-call | tf_op jit(solution)/shard_map/reduce_weights/pallas_call | solution.py:793
  854.5 16.2 %all_to_all.42 = bf16[4,96,1120]{2,1,0:T(8,128)(2,1)S(1)} all-to-all(bf16[4,96,1120]{2,1,0:T(8,128)(2,1)S(1)} %bitcast.215), channel_id=1, replica_groups=mesh['za'=4,'yb'=2,'xc'=2,'sp'=2] {'yb','xc'}, dimensions={0} | all-to-all | bytes 1720320 | tf_op jit(solution)/shard_map/all_to_all | solution.py:1095
  887.0 7.8 copy.135
  894.8 7.7 reshape.806
  (459 shorter events, 194.4 us)
Async XLA Ops:
  7.2 356.7 %all-gather.4.cloned.1.call-start = ((), (), s32[]{:S(2)}) async-start(), calls=%async_computation.10 | async-start | bytes 2359296 | tf_op jit(solution)/shard_map/all_gather | solution.py:832
  7.9 30.8 %copy-start.102 = (f32[128]{0:T(128)}, f32[128]{0:T(128)S(1)}, u32[]{:S(2)}) copy-start(f32[128]{0:T(128)S(1)} %multiply_exponential_fusion) | copy-start | bytes 1540
  40.9 289.2 %copy-start = (bf16[128,1536]{1,0:T(8,128)(2,1)S(1)}, bf16[128,1536]{1,0:T(8,128)(2,1)}, u32[]{:S(2)}) copy-start(bf16[128,1536]{1,0:T(8,128)(2,1)} %param.15) | copy-start | bytes 1179652
  323.8 16.3 %copy-start.55 = (f32[2,8,8,128]{3,1,2,0:T(8,128)}, f32[2,8,8,128]{3,1,2,0:T(8,128)S(1)}, u32[]{:S(2)}) copy-start(f32[2,8,8,128]{3,1,2,0:T(8,128)S(1)} %copy.160) | copy-start | bytes 196612
  326.7 4.7 all-to-all-start
  330.0 45.0 %reduce-scatter.9.cloned.1.call-start = ((), (), s32[]{:S(2)}) async-start(), calls=%async_computation.9 | async-start | bytes 2359296 | tf_op jit(solution)/shard_map/reduce_scatter | solution.py:836
  363.9 63.9 %reduce-scatter.11.cloned.1.call-start = ((), (), s32[]{:S(2)}) async-start(), calls=%async_computation.11 | async-start | bytes 2359296 | tf_op jit(solution)/shard_map/reduce_scatter | solution.py:836
  382.1 151.8 %copy-start.4 = (f32[256,768]{1,0:T(8,128)}, f32[256,768]{1,0:T(8,128)S(1)}, u32[]{:S(2)}) copy-start(f32[256,768]{1,0:T(8,128)S(1)} %get-tuple-element.143) | copy-start | bytes 2359300
  384.5 42.7 %copy-start.75 = (f32[1,256]{1,0:T(1,128)}, f32[1,256]{1,0:T(1,128)S(1)}, u32[]{:S(2)}) copy-start(f32[1,256]{1,0:T(1,128)S(1)} %add_rsqrt_fusion.1) | copy-start | bytes 3076
  397.0 149.2 %reduce-scatter.13.cloned.1.call-start = ((), (), s32[]{:S(2)}) async-start(), calls=%async_computation.12 | async-start | bytes 2359296 | tf_op jit(solution)/shard_map/reduce_scatter | solution.py:836
  429.0 21.7 %copy-start.97 = (f32[128]{0:T(128)}, f32[128]{0:T(128)S(1)}, u32[]{:S(2)}) copy-start(f32[128]{0:T(128)S(1)} %broadcast_multiply_fusion.2) | copy-start | bytes 1540
  429.3 32.4 %copy-start.112 = (f32[128]{0:T(128)}, f32[128]{0:T(128)S(1)}, u32[]{:S(2)}) copy-start(f32[128]{0:T(128)S(1)} %multiply_reduce_fusion.7) | copy-start | bytes 1540
  429.3 32.4 %copy-start.101 = (f32[128]{0:T(128)}, f32[128]{0:T(128)S(1)}, u32[]{:S(2)}) copy-start(f32[128]{0:T(128)S(1)} %fusion.73) | copy-start | bytes 1540
  450.7 11.0 %copy-start.114 = (bf16[4,280,1536]{2,1,0:T(8,128)(2,1)S(1)}, bf16[4,280,1536]{2,1,0:T(8,128)(2,1)}, u32[]{:S(2)}) copy-start(bf16[4,280,1536]{2,1,0:T(8,128)(2,1)} %get-tuple-element.51) | copy-start | bytes 10321924
  493.9 20.0 %copy-start.7 = (f32[128,1536]{1,0:T(8,128)S(1)}, f32[128,1536]{1,0:T(8,128)}, u32[]{:S(2)}) copy-start(f32[128,1536]{1,0:T(8,128)} %plane_sum.3) | copy-start | bytes 2359300
  522.9 11.0 %copy-start.89 = (f32[256]{0:T(256)S(1)}, f32[256]{0:T(256)}, u32[]{:S(2)}) copy-start(f32[256]{0:T(256)} %multiply_multiply_fusion.7) | copy-start | bytes 3076
  537.8 95.0 %reduce-scatter.15.cloned.1.call-start = ((), (), s32[]{:S(2)}) async-start(), calls=%async_computation.13 | async-start | bytes 2359296 | tf_op jit(solution)/shard_map/reduce_scatter | solution.py:836
  586.2 264.2 %reduce-scatter.19.cloned.1.call-start = ((), (), s32[]{:S(2)}) async-start(), calls=%async_computation.17 | async-start | bytes 4423680
  599.1 253.7 %reduce-scatter.17.cloned.1.call-start = ((), (), s32[]{:S(2)}) async-start(), calls=%async_computation.14 | async-start | bytes 4300800 | tf_op jit(solution)/shard_map/reduce_scatter | solution.py:836
  608.3 270.9 %all-gather.8.cloned.1.call-start = ((), (), s32[]{:S(2)}) async-start(), calls=%async_computation.16 | async-start | bytes 2580480 | tf_op jit(solution)/shard_map/all_gather | solution.py:832
  628.4 10.4 %copy-start.88 = (f32[1024]{0:T(1024)S(1)}, f32[1024]{0:T(1024)}, u32[]{:S(2)}) copy-start(f32[1024]{0:T(1024)} %pad.2.clone) | copy-start | bytes 12292
  852.8 20.2 %copy-start.103 = (f32[128]{0:T(128)S(1)}, f32[128]{0:T(128)}, u32[]{:S(2)}) copy-start(f32[128]{0:T(128)} %copy-done.102) | copy-start | bytes 1540
  852.8 20.4 %copy-start.50 = (bf16[16,4,4608]{2,1,0:T(4,128)(2,1)S(1)}, bf16[16,4,4608]{2,1,0:T(4,128)(2,1)}, u32[]{:S(2)}) copy-start(bf16[16,4,4608]{2,1,0:T(4,128)(2,1)} %get-tuple-element.60) | copy-start | bytes 1769476
  852.8 30.0 %all-gather.6.cloned.1.call-start = ((), (), s32[]{:S(2)}) async-start(), calls=%async_computation.15 | async-start | bytes 3440640 | tf_op jit(solution)/shard_map/all_gather | solution.py:832
  (106 other events, 525.9 us)
Sparse Core Ops, SparseCore 0:
  9.5 12.5 all-gather.3
  364.0 8.2 reduce-scatter.8
  397.1 8.3 reduce-scatter.10
  537.9 8.2 reduce-scatter.12
  586.4 10.3 reduce-scatter.14
  599.2 78.1 reduce-scatter.18
  680.3 97.1 reduce-scatter.16
  852.9 8.7 all-gather.7
  872.2 8.2 all-gather.5

commit v3 on v2

--- a/solution.py
+++ b/solution.py
@@ -196,12 +196,22 @@
 
 
 def row_add(target, left, right, rows):
-    step = 16 if rows % 16 == 0 else rows
+    step = 32 if rows % 32 == 0 else rows
 
     def chunk(index, carry):
         at = pl.ds(pl.multiple_of(index * step, step), step)
-        total = left[at, :].astype(F32) + right[at, :].astype(F32)
-        target[at, :] = total.astype(target.dtype)
+        target[at, :] = left[at, :] + right[at, :]
+        return carry
+
+    lax.fori_loop(0, rows // step, chunk, 0)
+
+
+def row_sum(target, left, right, rows):
+    step = 16 if rows % 16 == 0 else rows
+
+    def chunk(index, carry):
+        at = pl.ds(pl.multiple_of(index * step, step), step)
+        target[at, :] = left[at, :].astype(F32) + right[at, :].astype(F32)
         return carry
 
     lax.fori_loop(0, rows // step, chunk, 0)
@@ -266,30 +276,43 @@
     pl.semaphore_wait(barrier, count)
 
 
-def gather_kernel(outer, full, halves, *refs):
-    count = full + 2
-    ins, refs = refs[:count], refs[count:]
-    outs, refs = refs[:count], refs[count:]
-    fins, refs = refs[: len(halves)], refs[len(halves) :]
-    local_sem, zs, zr, s1, r1, s2, r2, a_s, a_r, f_s, f_r, f_l = refs
+def gather_kernel(outer, kinds, *refs):
+    full = len(kinds)
+    ins, refs = refs[:full], refs[full:]
+    mlp_ref, text_ref, refs = refs[0], refs[1], refs[2:]
+    outs, refs = list(refs[:full]), refs[full:]
+    up_out, text_out, refs = refs[0], refs[1], refs[2:]
+    own, refs = refs[:full], refs[full:]
+    halves = [i for i, kind in enumerate(kinds) if kind[1]]
+    whole, refs = refs[: len(halves)], refs[len(halves) :]
+    up_own, local_sem, zs, zr, s1, r1, s2, r2, a_s, a_r, f_s, f_r, f_l, t_s = refs
     z, y, x = (lax.axis_index(name) for name in FS)
     core = lax.axis_index("sp")
     here = 2 * y + x
-    up, down = full, full + 1
+    up = full
+    fins = {}
+    for j, i in enumerate(halves):
+        fins[i] = outs[i]
+        outs[i] = whole[j]
     fly = Flights()
     x_peer, y_peer = {"xc": 1 - x}, {"yb": 1 - y}
     diagonal = {"yb": 1 - y, "xc": 1 - x}
+    around = ((x_peer, y, 1 - x), (y_peer, 1 - y, x), (diagonal, 1 - y, 1 - x))
     above, below = {"za": z + 1}, {"za": z - 1}
     core_peer = {"sp": 1 - core}
     has_above, has_below = z + 1 < outer, z >= 1
     greet((x_peer, y_peer, diagonal, core_peer), ((has_above, above), (has_below, below)))
 
-    locals_ = [fly.local(ins[i], outs[i].at[z, y, x], local_sem.at[i]) for i in range(full)]
-    local_up = fly.local(ins[up].at[here], outs[up].at[z, here], local_sem.at[up])
-    local_down = fly.local(ins[down], outs[down].at[z], local_sem.at[down])
+    for i, (parts, _) in enumerate(kinds):
+        if parts == 0:
+            own[i][...] = ins[i][...]
+        for part in range(parts):
+            width = ins[i].shape[1] // (2 * parts)
+            column = pl.multiple_of((2 * part + core) * width, width)
+            own[i][:, part * width : (part + 1) * width] = ins[i][:, pl.ds(column, width)]
 
     def shard(i, slot):
-        return outs[i].at[slot, y, x] if i < full else outs[i].at[slot]
+        return outs[i].at[slot, y, x] if i < full else up_out.at[slot]
 
     def z_send(i, way, hop, source=None):
         if hop > outer - 2:
@@ -350,8 +373,22 @@
 
     for i in range(full):
         for way in range(2):
-            z_send(i, way, 0, ins[i])
-        xy_own(i, z, None, ins[i])
+            z_send(i, way, 0, own[i])
+        xy_own(i, z, None, own[i])
+    locals_ = [fly.local(own[i], outs[i].at[z, y, x], local_sem.at[i]) for i in range(full)]
+
+    fly.send(text_ref, text_out.at[core], t_s.at[0], t_s.at[1], core_peer)
+    locals_.append(fly.local(text_ref, text_out.at[core], t_s.at[2]))
+    hid = mlp_ref.shape[1] // (outer * PLANE * 2)
+    for own_core in range(2):
+
+        @pl.when(core == own_core)
+        def _(own_core=own_core):
+            for place in range(PLANE):
+                for slot in range(outer):
+                    column = ((slot * PLANE + place) * 2 + own_core) * hid
+                    up_own[place, :, slot * hid : (slot + 1) * hid] = mlp_ref[:, column : column + hid]
+
     for hop in range(outer - 1):
         for i in range(full):
             for way in range(2):
@@ -360,23 +397,13 @@
                 z_send(i, way, hop + 1)
                 xy_own(i, slot, when)
         if hop == 0:
-            for turn, device in enumerate((x_peer, y_peer, diagonal)):
-                ty = y if turn == 0 else 1 - y
-                tx = x if turn == 1 else 1 - x
-                fly.send(
-                    ins[up].at[2 * ty + tx],
-                    outs[up].at[z, here],
-                    a_s.at[turn],
-                    a_r.at[turn],
-                    device,
-                )
-    for way in range(2):
-        z_send(down, way, 0, ins[down])
-    local_up.wait()
-    for turn, device in enumerate((x_peer, y_peer, diagonal)):
-        ty = y if turn == 0 else 1 - y
-        tx = x if turn == 1 else 1 - x
-        landed(outs[up].at[z, 2 * ty + tx], a_r.at[turn], device)
+            locals_.append(fly.local(up_own.at[here], up_out.at[z, here], local_sem.at[up]))
+            for turn, (device, ty, tx) in enumerate(around):
+                fly.send(up_own.at[2 * ty + tx], up_out.at[z, here], a_s.at[turn], a_r.at[turn], device)
+    for copy in locals_:
+        copy.wait()
+    for turn, (device, ty, tx) in enumerate(around):
+        landed(up_out.at[z, 2 * ty + tx], a_r.at[turn], device)
     for way in range(2):
         z_send(up, way, 0)
     for i in range(full):
@@ -386,56 +413,61 @@
             for way in range(2):
                 slot, when = z_slot(way, hop)
                 xy_pass(i, slot, when)
-        for i in (down, up):
-            for way in range(2):
-                z_wait(i, way, hop)
-                z_send(i, way, hop + 1)
-    for i in range(full):
+        for way in range(2):
+            z_wait(up, way, hop)
+            z_send(up, way, hop + 1)
+    for i in (*halves, *(i for i in range(full) if i not in halves)):
         for slot in range(outer):
             xy_end(i, slot)
-    for copy in locals_:
-        copy.wait()
-    local_down.wait()
-
-    part = outer // 2
+        if i not in halves:
+            continue
+        j, part = halves.index(i), outer // 2
+        width = own[i].shape[-1]
+        columns = pl.ds(pl.multiple_of(core * width, width), width)
+        theirs, ours = pl.ds((1 - core) * part, part), pl.ds(core * part, part)
+        fly.send(outs[i].at[theirs], fins[i].at[:, :, :, :, columns], f_s.at[j], f_r.at[j], core_peer)
+        fly.local(outs[i].at[ours], fins[i].at[:, :, :, :, columns], f_l.at[j])
     for j, i in enumerate(halves):
-        width = ins[i].shape[-1]
-        columns = pl.ds(pl.multiple_of(core * width, width), width)
-        theirs = pl.ds((1 - core) * part, part)
-        ours = pl.ds(core * part, part)
-        fly.send(outs[i].at[theirs], fins[j].at[:, :, :, :, columns], f_s.at[j], f_r.at[j], core_peer)
-        fly.local(outs[i].at[ours], fins[j].at[:, :, :, :, columns], f_l.at[j])
-    for j, i in enumerate(halves):
-        width = ins[i].shape[-1]
+        width = own[i].shape[-1]
         columns = pl.ds(pl.multiple_of(core * width, width), width)
         others = pl.ds(pl.multiple_of((1 - core) * width, width), width)
-        ours = pl.ds(core * part, part)
-        pltpu.make_async_copy(outs[i].at[ours], fins[j].at[:, :, :, :, columns], f_l.at[j]).wait()
-        landed(fins[j].at[:, :, :, :, others], f_r.at[j], core_peer)
+        ours = pl.ds(core * (outer // 2), outer // 2)
+        pltpu.make_async_copy(outs[i].at[ours], fins[i].at[:, :, :, :, columns], f_l.at[j]).wait()
+        landed(fins[i].at[:, :, :, :, others], f_r.at[j], core_peer)
+    landed(text_out.at[1 - core], t_s.at[1], core_peer)
     fly.drain()
 
 
-def gather_weights(outer, full, halves, up, down):
-    count = len(full) + 2
-    arrays = [*full, up, down]
-    shapes = [jax.ShapeDtypeStruct((outer, 2, 2, *a.shape), a.dtype) for a in full]
-    shapes.append(jax.ShapeDtypeStruct((outer, *up.shape), up.dtype))
-    shapes.append(jax.ShapeDtypeStruct((outer, *down.shape), down.dtype))
-    for i in halves:
-        r, n = full[i].shape
-        shapes.append(jax.ShapeDtypeStruct((outer // 2, 2, 2, r, 2 * n), full[i].dtype))
+def gather_weights(outer, kinds, arrays, mlp, text):
+    shapes, own, whole = [], [], []
+    for (parts, keep), array in zip(kinds, arrays, strict=True):
+        rows, width = array.shape
+        half = width // 2 if parts else width
+        own.append(pltpu.VMEM((rows, half), array.dtype))
+        if keep:
+            whole.append(pltpu.VMEM((outer, 2, 2, rows, half), array.dtype))
+            shapes.append(jax.ShapeDtypeStruct((outer // 2, 2, 2, rows, width), array.dtype))
+        else:
+            shapes.append(jax.ShapeDtypeStruct((outer, 2, 2, rows, half), array.dtype))
+    rows, units = mlp.shape
+    mine = units // (2 * PLANE)
+    shapes.append(jax.ShapeDtypeStruct((outer, PLANE, rows, mine), mlp.dtype))
+    shapes.append(jax.ShapeDtypeStruct((2, *text.shape), text.dtype))
     dma = pltpu.SemaphoreType.DMA
     hops = outer - 1
-    nf, nh = len(full), len(halves)
+    nf, nh = len(kinds), len(whole)
     results = pl.pallas_call(
-        functools.partial(gather_kernel, outer, nf, halves),
+        functools.partial(gather_kernel, outer, kinds),
         out_shape=shapes,
-        in_specs=[VM] * count,
+        in_specs=[VM] * (nf + 2),
         out_specs=[ANY] * len(shapes),
         scratch_shapes=[
-            dma((count,)),
-            dma((count, 2, hops)),
-            dma((count, 2, hops)),
+            *own,
+            *whole,
+            pltpu.VMEM((PLANE, rows, mine), mlp.dtype),
+            dma((nf + 1,)),
+            dma((nf + 1, 2, hops)),
+            dma((nf + 1, 2, hops)),
             dma((nf, outer)),
             dma((nf, outer)),
             dma((nf, outer, 2)),
@@ -445,14 +477,15 @@
             dma((nh,)),
             dma((nh,)),
             dma((nh,)),
+            dma((3,)),
         ],
-        compiler_params=pltpu.CompilerParams(collective_id=0, has_side_effects=True),
+        compiler_params=pltpu.CompilerParams(
+            collective_id=0, has_side_effects=True, vmem_limit_bytes=40 * 1024 * 1024
+        ),
+        cost_estimate=pl.CostEstimate(flops=10**11, bytes_accessed=10**8, transcendentals=0),
         name="gather_weights",
-    )(*arrays)
-    gathered = [v.reshape(-1, v.shape[-1]) for v in results[: nf + 2]]
-    for j, i in enumerate(halves):
-        gathered[i] = results[nf + 2 + j].reshape(-1, results[nf + 2 + j].shape[-1])
-    return gathered, results[: nf + 2]
+    )(*arrays, mlp, text)
+    return [value.reshape(-1, value.shape[-1]) for value in results]
 
 
 def plane_gather_kernel(own_ref, out_ref, local_sem, send, recv):
@@ -462,43 +495,32 @@
     greet((x_peer, y_peer, core_peer))
     size = own_ref.shape[0] // 2
     top, low = pl.ds(0, size), pl.ds(size, size)
-    local = fly.local(own_ref, out_ref.at[y, x, core], local_sem.at[0])
-
-    def place(ty, tx, rows):
-        return out_ref.at[ty, tx, core, rows]
-
-    fly.send(own_ref.at[top], place(y, x, top), send.at[0], recv.at[0], x_peer)
-    fly.send(own_ref.at[low], place(y, x, low), send.at[1], recv.at[1], y_peer)
-    fly.send(own_ref.at[low], place(y, x, low), send.at[2], recv.at[2], x_peer)
-    fly.send(own_ref.at[top], place(y, x, top), send.at[3], recv.at[3], y_peer)
-    fly.send(own_ref, out_ref.at[y, x, core], send.at[4], recv.at[4], core_peer)
-
-    def arrive(index, ty, tx, rows, device):
-        landed(place(ty, tx, rows), recv.at[index], device)
-        fly.send(place(ty, tx, rows), place(ty, tx, rows), send.at[index + 5], recv.at[index + 5], core_peer)
-
-    arrive(0, y, 1 - x, top, x_peer)
-    fly.send(place(y, 1 - x, top), place(y, 1 - x, top), send.at[12], recv.at[12], y_peer)
-    arrive(1, 1 - y, x, low, y_peer)
-    fly.send(place(1 - y, x, low), place(1 - y, x, low), send.at[13], recv.at[13], x_peer)
-    arrive(2, y, 1 - x, low, x_peer)
-    arrive(3, 1 - y, x, top, y_peer)
-    for index, rows, device in ((0, top, y_peer), (1, low, x_peer)):
-        landed(place(1 - y, 1 - x, rows), recv.at[12 + index], device)
-        fly.send(
-            place(1 - y, 1 - x, rows), place(1 - y, 1 - x, rows), send.at[10 + index], recv.at[10 + index], core_peer
-        )
-    other = 1 - core
-    landed(out_ref.at[y, x, other], recv.at[4], core_peer)
-    for index, ty, tx, rows in (
-        (5, y, 1 - x, top),
-        (6, 1 - y, x, low),
-        (7, y, 1 - x, low),
-        (8, 1 - y, x, top),
-        (10, 1 - y, 1 - x, top),
-        (11, 1 - y, 1 - x, low),
-    ):
-        landed(out_ref.at[ty, tx, other, rows], recv.at[index], core_peer)
+    fly.send(own_ref.at[top], out_ref.at[0, 1, 0, top], send.at[0], recv.at[0], x_peer)
+    fly.send(own_ref.at[low], out_ref.at[1, 0, 0, low], send.at[1], recv.at[1], y_peer)
+    fly.send(own_ref.at[low], out_ref.at[0, 1, 0, low], send.at[2], recv.at[2], x_peer)
+    fly.send(own_ref.at[top], out_ref.at[1, 0, 0, top], send.at[3], recv.at[3], y_peer)
+    fly.send(own_ref, out_ref.at[0, 0, 1], send.at[4], recv.at[4], core_peer)
+    local = fly.local(own_ref, out_ref.at[0, 0, 0], local_sem.at[0])
+    across = []
+
+    def arrive(index, dy, dx, rows, device, onward=None):
+        block = out_ref.at[dy, dx, 0, rows]
+        landed(block, recv.at[index], device)
+        if onward is not None:
+            to, number = onward
+            fly.send(block, out_ref.at[1, 1, 0, rows], send.at[number], recv.at[number], to)
+        fly.send(block, out_ref.at[dy, dx, 1, rows], send.at[index + 7], recv.at[index + 7], core_peer)
+        across.append((index + 7, dy, dx, rows))
+
+    arrive(0, 0, 1, top, x_peer, (y_peer, 5))
+    arrive(1, 1, 0, low, y_peer, (x_peer, 6))
+    arrive(2, 0, 1, low, x_peer)
+    arrive(3, 1, 0, top, y_peer)
+    arrive(5, 1, 1, top, y_peer)
+    arrive(6, 1, 1, low, x_peer)
+    landed(out_ref.at[0, 0, 1], recv.at[4], core_peer)
+    for index, dy, dx, rows in across:
+        landed(out_ref.at[dy, dx, 1, rows], recv.at[index], core_peer)
     local.wait()
     fly.drain()
 
@@ -513,6 +535,7 @@
         out_specs=VM,
         scratch_shapes=[dma((1,)), dma((14,)), dma((14,))],
         compiler_params=pltpu.CompilerParams(collective_id=1, has_side_effects=True),
+        cost_estimate=pl.CostEstimate(flops=10**10, bytes_accessed=10**7, transcendentals=0),
         name="plane_gather",
     )(own)
     return out.reshape(8 * rows, width)
@@ -526,19 +549,14 @@
     rows = part_ref.shape[3]
     size = rows // 2
     top, low = pl.ds(0, size), pl.ds(size, size)
-    chips = ((1 - y, 1 - x), (1 - y, x), (y, 1 - x), (y, x))
-    for index, (ty, tx) in enumerate(chips):
-        fly.send(
-            part_ref.at[ty, tx, 1 - core], core_in.at[index], send.at[index], recv.at[index], core_peer
-        )
-
-    def own_part(index):
-        ty, tx = chips[index]
-        return part_ref.at[ty, tx, core]
+    chips = ((1, 1), (1, 0), (0, 1), (0, 0))
+    for index, (dy, dx) in enumerate(chips):
+        fly.send(part_ref.at[dy, dx, 1], core_in.at[index], send.at[index], recv.at[index], core_peer)
 
     def core_sum(index):
+        dy, dx = chips[index]
         landed(core_in.at[index], recv.at[index], core_peer)
-        row_add(core_in.at[index], core_in.at[index], own_part(index), rows)
+        row_add(core_in.at[index], core_in.at[index], part_ref.at[dy, dx, 0], rows)
 
     core_sum(0)
     fly.send(core_in.at[0, top], first.at[0], send.at[4], recv.at[4], y_peer)
@@ -555,13 +573,13 @@
     row_add(second.at[1], first.at[1], core_in.at[1, low], size)
     fly.send(second.at[1], second.at[3], send.at[9], recv.at[9], y_peer)
     landed(first.at[2], recv.at[6], y_peer)
-    row_add(keep.at[top], first.at[2], core_in.at[3, top], size)
+    row_sum(keep.at[top], first.at[2], core_in.at[3, top], size)
     landed(first.at[3], recv.at[7], x_peer)
-    row_add(keep.at[low], first.at[3], core_in.at[3, low], size)
+    row_sum(keep.at[low], first.at[3], core_in.at[3, low], size)
     landed(second.at[2], recv.at[8], x_peer)
-    row_add(out_ref.at[top], keep.at[top], second.at[2], size)
+    row_sum(out_ref.at[top], keep.at[top], second.at[2], size)
     landed(second.at[3], recv.at[9], y_peer)
-    row_add(out_ref.at[low], keep.at[low], second.at[3], size)
+    row_sum(out_ref.at[low], keep.at[low], second.at[3], size)
     fly.drain()
 
 
@@ -582,8 +600,40 @@
             dma((10,)),
         ],
         compiler_params=pltpu.CompilerParams(collective_id=2, has_side_effects=True),
+        cost_estimate=pl.CostEstimate(flops=10**10, bytes_accessed=10**7, transcendentals=0),
         name="plane_sum",
     )(partial.reshape(2, 2, 2, rows, width))
+
+
+def pair_sum_kernel(part_ref, out_ref, peer_in, send, recv):
+    core = lax.axis_index("sp")
+    core_peer = {"sp": 1 - core}
+    fly = Flights()
+    greet((core_peer,))
+    size = part_ref.shape[1] // 2
+    for index in range(2):
+        rows = pl.ds(index * size, size)
+        fly.send(part_ref.at[1 - core, rows], peer_in.at[rows], send.at[index], recv.at[index], core_peer)
+    for index in range(2):
+        rows = pl.ds(index * size, size)
+        landed(peer_in.at[rows], recv.at[index], core_peer)
+        row_sum(out_ref.at[rows], part_ref.at[core, rows], peer_in.at[rows], size)
+    fly.drain()
+
+
+def pair_sum(partial):
+    rows, width = partial.shape[0] // 2, partial.shape[1]
+    dma = pltpu.SemaphoreType.DMA
+    return pl.pallas_call(
+        pair_sum_kernel,
+        out_shape=jax.ShapeDtypeStruct((rows, width), F32),
+        in_specs=[VM],
+        out_specs=VM,
+        scratch_shapes=[pltpu.VMEM((rows, width), F32), dma((2,)), dma((2,))],
+        compiler_params=pltpu.CompilerParams(collective_id=4, has_side_effects=True),
+        cost_estimate=pl.CostEstimate(flops=10**9, bytes_accessed=10**7, transcendentals=0),
+        name="pair_sum",
+    )(partial.reshape(2, rows, width))
 
 
 AHEAD, LAG_PLANE, LAG_CHAIN = 6, 2, 4
@@ -593,16 +643,16 @@
     count = len(kinds)
     shards = outer * PLANE
     gs, refs = refs[:count], refs[count:]
-    frames_ref, small_ref, refs = refs[0], refs[1], refs[2:]
+    frames_ref, small_ref, up_ref, down_ref, refs = *refs[:4], refs[4:]
     outs, refs = refs[:count], refs[count:]
-    frames_out, small_out, refs = refs[0], refs[1], refs[2:]
+    frames_out, small_out, up_out, down_out, refs = *refs[:4], refs[4:]
     near, refs = refs[:count], refs[count:]
     plane, refs = refs[:count], refs[count:]
     chain, refs = refs[:count], refs[count:]
     split = [i for i, kind in enumerate(kinds) if kind[1]]
     whole, refs = refs[: len(split)], refs[len(split) :]
-    small_in, small_own, small_peer, refs = refs[0], refs[1], refs[2], refs[3:]
-    e_s, e_r, e_l, s1, r1, s2, r2, zs, zr, o_s, o_r, f_s, f_r, m_s, m_r, l_s = refs
+    small_in, small_own, small_peer, up_in, down_in, refs = *refs[:5], refs[5:]
+    e_s, e_r, e_l, s1, r1, s2, r2, zs, zr, o_s, o_r, f_s, f_r, m_s, m_r, l_s, p_s, p_r = refs
     z, y, x = (lax.axis_index(name) for name in FS)
     core = lax.axis_index("sp")
     here = (z * 2 + y) * 2 + x
@@ -635,11 +685,49 @@
         pltpu.make_async_copy(gs[i].at[:, :, :, :, mine], whole[j].at[ours], e_l.at[j]).wait()
         landed(whole[j].at[other], e_r.at[j], core_peer)
 
-    frame_copy = fly.local(frames_ref, frames_out.at[here], l_s.at[0])
+    frame_width = frames_ref.shape[1]
+    frame_mine = pl.ds(pl.multiple_of(core * frame_width, frame_width), frame_width)
+    frame_other = pl.ds(pl.multiple_of((1 - core) * frame_width, frame_width), frame_width)
+    frame_copy = fly.local(frames_ref, frames_out.at[here, :, frame_mine], l_s.at[0])
     small_copy = fly.local(small_ref.at[here], small_in.at[here], l_s.at[1])
     for j, index in enumerate(others):
-        fly.send(frames_ref, frames_out.at[here], f_s.at[j], f_r.at[here], chip(index))
+        fly.send(frames_ref, frames_out.at[here, :, frame_mine], f_s.at[j], f_r.at[here], chip(index))
         fly.send(small_ref.at[index], small_in.at[here], m_s.at[j], m_r.at[here], chip(index))
+
+    near_by = ((y, 1 - x), (1 - y, x), (1 - y, 1 - x))
+    up_copy = fly.local(up_ref.at[2 * y + x], up_in.at[core, 2 * y + x], p_s.at[0])
+    for j, (ty, tx) in enumerate(near_by):
+        fly.send(
+            up_ref.at[2 * ty + tx],
+            up_in.at[core, 2 * y + x],
+            p_s.at[j + 1],
+            p_r.at[j + 1],
+            {"yb": ty, "xc": tx},
+        )
+    fly.send(down_ref, down_in, p_s.at[4], p_r.at[4], core_peer)
+
+    def feed_forward_landed():
+        up_copy.wait()
+        for j, (ty, tx) in enumerate(near_by):
+            landed(up_in.at[core, 2 * ty + tx], p_r.at[j + 1], {"yb": ty, "xc": tx})
+        fly.send(up_in.at[core], up_in.at[core], p_s.at[5], p_r.at[5], core_peer)
+        hid = down_ref.shape[0]
+        landed(down_in, p_r.at[4], core_peer)
+        for side in range(2):
+
+            @pl.when(core == side)
+            def _(side=side):
+                down_out[side * hid : (side + 1) * hid, :] = down_ref[...].astype(F32)
+                down_out[(1 - side) * hid : (2 - side) * hid, :] = down_in[...].astype(F32)
+
+    def feed_forward_rows():
+        hid = down_ref.shape[0]
+        landed(up_in.at[1 - core], p_r.at[5], core_peer)
+        for slot in range(outer):
+            for place in range(PLANE):
+                for side in range(2):
+                    column = ((slot * PLANE + place) * 2 + side) * hid
+                    up_out[:, column : column + hid] = up_in[side, place, :, slot * hid : (slot + 1) * hid].astype(F32)
 
     def slot_at(step):
         if step == outer - 1:
@@ -694,11 +782,11 @@
 
                 @pl.when(jnp.logical_and(when, jnp.logical_not(edge)))
                 def _():
-                    landed(chain[i].at[way, slot], zr.at[i, way, slot], behind)
-                    row_add(plane[i].at[slot], plane[i].at[slot], chain[i].at[way, slot], rows)
+                    landed(chain[i].at[slot + 1 - way], zr.at[i, way, slot], behind)
+                    row_add(plane[i].at[slot], plane[i].at[slot], chain[i].at[slot + 1 - way], rows)
 
                 fly.send(
-                    plane[i].at[slot], chain[i].at[way, slot], zs.at[i, way, slot], zr.at[i, way, slot], ahead, when
+                    plane[i].at[slot], chain[i].at[slot + 1 - way], zs.at[i, way, slot], zr.at[i, way, slot], ahead, when
                 )
             return
         parts = kinds[i][0]
@@ -707,7 +795,7 @@
 
             @pl.when(when)
             def _():
-                landed(chain[i].at[way, slot], zr.at[i, way, slot], behind)
+                landed(chain[i].at[slot + 1 - way], zr.at[i, way, slot], behind)
 
         step = 16 if rows % 16 == 0 else rows
         has_above, has_below = z < outer - 1, z > 0
@@ -717,8 +805,8 @@
             for part_no in range(parts):
                 span = slice(part_no * width, (part_no + 1) * width)
                 total = plane[i][slot, at, span].astype(F32)
-                upper = chain[i][1, slot, at, span].astype(F32)
-                lower = chain[i][0, slot, at, span].astype(F32)
+                upper = chain[i][slot, at, span].astype(F32)
+                lower = chain[i][slot + 1, at, span].astype(F32)
                 total = total + jnp.where(has_above, upper, 0.0) + jnp.where(has_below, lower, 0.0)
                 column = pl.multiple_of((2 * part_no + core) * width, width)
                 outs[i][at, pl.ds(column, width)] = total
@@ -748,6 +836,10 @@
                 begin(tick + AHEAD)
         if 0 <= tick - LAG_PLANE < len(units):
             plane_total(*units[tick - LAG_PLANE])
+        if tick == 2:
+            feed_forward_landed()
+        if tick == 6:
+            feed_forward_rows()
         if 0 <= tick - LAG_CHAIN < len(units):
             unit = tick - LAG_CHAIN
             along(*units[unit], unit >= (outer - 1) * count)
@@ -759,7 +851,9 @@
     small_own[...] = jnp.sum(small_in[...], axis=0)
     fly.send(small_own, small_peer, l_s.at[2], l_s.at[3], core_peer)
     for index in others:
-        landed(frames_out.at[index], f_r.at[index], chip(index))
+        landed(frames_out.at[index, :, frame_mine], f_r.at[index], chip(index))
+    fly.send(frames_out.at[:, :, frame_mine], frames_out.at[:, :, frame_mine], p_s.at[6], p_r.at[6], core_peer)
+    landed(frames_out.at[:, :, frame_other], p_r.at[6], core_peer)
     landed(small_peer, l_s.at[3], core_peer)
     small_out[...] = small_own[...] + small_peer[...]
     for i in range(count):
@@ -771,7 +865,7 @@
     fly.drain()
 
 
-def reduce_weights(outer, kinds, grads, frames, small):
+def reduce_weights(outer, kinds, grads, frames, small, up, down):
     shards = outer * PLANE
     count = len(kinds)
     shaped, shapes, near, plane, chain, whole = [], [], [], [], [], []
@@ -783,18 +877,20 @@
         shapes.append(jax.ShapeDtypeStruct((rows, 2 * width), F32))
         near.append(pltpu.VMEM((outer, 2, rows, width), BF))
         plane.append(pltpu.VMEM((outer, rows, width), BF))
-        chain.append(pltpu.VMEM((2, outer, rows, width), BF))
+        chain.append(pltpu.VMEM((outer + 1, rows, width), BF))
         if split:
             whole.append(pltpu.VMEM((outer, 2, 2, rows, width), BF))
-    shapes.append(jax.ShapeDtypeStruct((shards, *frames.shape), frames.dtype))
+    shapes.append(jax.ShapeDtypeStruct((shards, frames.shape[0], 2 * frames.shape[1]), frames.dtype))
     shapes.append(jax.ShapeDtypeStruct(small.shape[1:], F32))
+    shapes.append(jax.ShapeDtypeStruct((up.shape[1], 2 * PLANE * up.shape[2]), F32))
+    shapes.append(jax.ShapeDtypeStruct((2 * down.shape[0], down.shape[1]), F32))
     dma = pltpu.SemaphoreType.DMA
     nsplit = len(whole)
     results = pl.pallas_call(
         functools.partial(reduce_kernel, outer, kinds),
         out_shape=shapes,
-        in_specs=[VM] * (count + 2),
-        out_specs=[VM] * count + [VM, VM],
+        in_specs=[VM] * (count + 4),
+        out_specs=[VM] * (count + 4),
         scratch_shapes=[
             *near,
             *plane,
@@ -803,6 +899,8 @@
             pltpu.VMEM(small.shape, F32),
             pltpu.VMEM(small.shape[1:], F32),
             pltpu.VMEM(small.shape[1:], F32),
+            pltpu.VMEM((2, *up.shape), up.dtype),
+            pltpu.VMEM(down.shape, down.dtype),
             dma((nsplit,)),
             dma((nsplit,)),
             dma((nsplit,)),
@@ -819,13 +917,16 @@
             dma((shards,)),
             dma((shards,)),
             dma((4,)),
+            dma((7,)),
+            dma((7,)),
         ],
+        cost_estimate=pl.CostEstimate(flops=10**11, bytes_accessed=10**8, transcendentals=0),
         compiler_params=pltpu.CompilerParams(
             collective_id=3, has_side_effects=True, vmem_limit_bytes=67043328
         ),
         name="reduce_weights",
-    )(*shaped, frames, small)
-    return results[:count], results[count], results[count + 1]
+    )(*shaped, frames, small, up, down)
+    return results[:count], *results[count:]
 
 
 def gather(value, axes, axis=0):
@@ -891,12 +992,6 @@
     small_width = -(-(small_len + group_frames) // (small_rows * 128)) * 128
     small_room = small_rows * small_width
 
-    def own_half(weight, parts):
-        shaped = weight[0].reshape(weight.shape[1], parts, 2, -1)
-        return lax.dynamic_index_in_dim(shaped, core, 2, keepdims=False).reshape(
-            weight.shape[1], -1
-        )
-
     small = jnp.concatenate(
         [
             mod_bias[0].astype(F32),
@@ -905,30 +1000,19 @@
             jnp.zeros((small_room - small_len - group_frames,), F32),
         ]
     ).reshape(small_rows, small_width)
+    gathered = gather_weights(
+        outer,
+        ((0, False), (1, False), (3, False), (1, True), (2, False), (1, False), (1, True)),
+        [small, *(w[0] for w in (mod_weight, self_in, self_out, cross_kv, cross_q, cross_out))],
+        mlp_in[0],
+        text,
+    )
+    small_all, mod_matrix, self_proj, self_back, cross_kvproj, cross_qproj, cross_back = gathered[:7]
+    up_matrix, text_all = gathered[7:]
     hid = mlp_out.shape[1] // 2
-    in_rows = mlp_in.shape[1]
-    up_part = lax.dynamic_index_in_dim(
-        mlp_in[0].reshape(in_rows, outer, PLANE, 2, hid), core, 3, keepdims=False
-    )
-    up_part = up_part.transpose(2, 0, 1, 3).reshape(PLANE, in_rows, outer * hid)
     down_part = lax.dynamic_slice_in_dim(mlp_out[0], core * hid, hid, 0)
-    gathered, raw = gather_weights(
-        outer,
-        [
-            small,
-            own_half(mod_weight, 1),
-            own_half(self_in, 3),
-            own_half(self_out, 1),
-            own_half(cross_kv, 2),
-            own_half(cross_q, 1),
-            own_half(cross_out, 1),
-        ],
-        (3, 6),
-        up_part,
-        down_part,
-    )
-    small_all, mod_matrix, self_proj, self_back, cross_kvproj, cross_qproj, cross_back = gathered[:7]
-    up_matrix, down_matrix = gathered[7:]
+    down_part, small_all = lax.optimization_barrier((down_part, small_all))
+    down_matrix = gather(down_part, "za")
     small_all = small_all.reshape(shards, small_room)
     bias_all = small_all[:, :bias_len].reshape(-1)
     gain_all = (
@@ -957,7 +1041,12 @@
         modulation, 6, axis=1
     )
 
-    text_all = gather(text, "sp")
+    grad_branch = frame_scaled(cotangent.astype(F32), gate_two).astype(BF)
+    exchange = [(0, 1), (1, 0)]
+    beside = jnp.stack([grad_branch, lax.ppermute(grad_branch, "xc", exchange)])
+    beside = jnp.stack([beside, lax.ppermute(beside, "yb", exchange)])
+    beside = jnp.stack([beside, lax.ppermute(beside, "sp", exchange)], axis=2)
+    grad_branch_all = beside.reshape(-1, D)
 
     residual = tokens.astype(F32)
     attn_float, back_attn_input = jax.vjp(modulated, residual, shift_one, scale_one)
@@ -970,7 +1059,7 @@
     key = rotate(raw_k * inv_k[:, None] * gain_own[1], cosine, sine).astype(BF)
     value = raw_v.astype(BF)
     self_mixed, self_lse = attend_forward(live_keys, query, key, value)
-    self_branch = scatter(product(self_mixed, self_back), "sp")
+    self_branch = pair_sum(product(self_mixed, self_back))
     residual = residual + frame_scaled(self_branch, gate_one)
 
     text_raw = product(text_all, cross_kvproj)
@@ -985,7 +1074,7 @@
     inv_cq = rms_scale(lax.psum(square_sum(cross_raw)[None], "sp")[0])
     cross_query = (cross_raw * inv_cq[:, None] * gain_own[2]).astype(BF)
     cross_mixed, cross_lse = attend_forward(all_keys, cross_query, cross_key, cross_value)
-    residual = residual + scatter(product(cross_mixed, cross_back), "sp")
+    residual = residual + pair_sum(product(cross_mixed, cross_back))
 
     mlp_float, back_mlp_input = jax.vjp(modulated, residual, shift_two, scale_two)
     mlp_input = plane_gather(mlp_float.astype(BF))
@@ -999,15 +1088,15 @@
     output = (residual + frame_scaled(mlp_branch, gate_two)).astype(BF)
 
     grad_rows = cotangent.astype(F32)
-    grad_branch = frame_scaled(grad_rows, gate_two).astype(BF)
     grad_gate_two = frame_sum(grad_rows * mlp_branch, frame_count)
-    grad_branch_all = plane_gather(grad_branch)
     grad_down = product_tn(activated, grad_branch_all).astype(BF)
-    down_owned = scatter(grad_down, "za")
     grad_up_low = back_gelu(product_nt(grad_branch_all, down_matrix))[0].astype(BF)
     grad_up = product_tn(mlp_input, grad_up_low).astype(BF)
+    grad_mlp_part = product_nt(grad_up_low, up_matrix).astype(BF)
+    grad_mlp_part, grad_up, grad_down = lax.optimization_barrier((grad_mlp_part, grad_up, grad_down))
+    down_owned = scatter(grad_down, "za")
     up_owned = scatter(grad_up, "za")
-    grad_mlp_input = plane_sum(product_nt(grad_up_low, up_matrix).astype(BF))
+    grad_mlp_input = plane_sum(grad_mlp_part)
     grad_from_mlp, grad_shift_two, grad_scale_two = back_mlp_input(grad_mlp_input)
     grad_rows = grad_rows + grad_from_mlp
 
@@ -1030,7 +1119,7 @@
     )
     grad_cross_qproj = product_tn(cross_input, grad_cross_low).astype(BF)
     grad_cross_kvproj = product_tn(text_all, grad_text_low).astype(BF)
-    grad_cross_input = scatter(product_nt(grad_cross_low, cross_qproj), "sp")
+    grad_cross_input = pair_sum(product_nt(grad_cross_low, cross_qproj))
     grad_rows = grad_rows + back_cross_norm(grad_cross_input)[0]
 
     grad_gate_one = frame_sum(grad_rows * self_branch, frame_count)
@@ -1056,7 +1145,7 @@
         axis=1,
     )
     grad_self_proj = product_tn(attn_input, grad_joined_low).astype(BF)
-    grad_attn_input = scatter(product_nt(grad_joined_low, self_proj), "sp")
+    grad_attn_input = pair_sum(product_nt(grad_joined_low, self_proj))
     grad_from_attn, grad_shift_one, grad_scale_one = back_attn_input(grad_attn_input)
     grad_rows = grad_rows + grad_from_attn
 
@@ -1076,25 +1165,21 @@
         ],
         axis=1,
     ).reshape(shards, small_rows, small_width)
-    owned, grad_mod_all, small_owned = reduce_weights(
+    owned, grad_mod_all, small_owned, mlp_in_grad, mlp_out_grad = reduce_weights(
         outer,
         ((1, False), (2, False), (1, True), (1, True), (3, False)),
         [grad_cross_qproj, grad_cross_kvproj, grad_cross_back, grad_self_back, grad_self_proj],
         grad_mod_half.astype(BF),
         grad_small,
+        up_owned.reshape(PLANE, -1, up_owned.shape[1]),
+        down_owned,
     )
     cross_q_grad, cross_kv_grad, cross_out_grad, self_out_grad, self_in_grad = owned
     small_owned = small_owned.reshape(-1)[:small_len]
     sinus_all = sinus_features(steps_all).astype(BF)
     own_features = mod_weight.shape[1]
     sinus_own = lax.dynamic_slice_in_dim(sinus_all, chip * own_features, own_features, 1)
-    grad_mod_all = grad_mod_all.reshape(-1, grad_mod_half.shape[1])
-    mod_weight_grad = gather(product_tn(sinus_own, grad_mod_all), "sp", 1)
-
-    up_owned, down_owned, small_owned = lax.optimization_barrier((up_owned, down_owned, small_owned))
-    up_rows = lax.all_to_all(up_owned, PL, split_axis=0, concat_axis=0, tiled=True)
-    up_pair = gather(up_rows.reshape(1, PLANE, in_rows, outer, hid), "sp").astype(F32)
-    mlp_in_grad = up_pair.transpose(2, 3, 1, 0, 4).reshape(1, in_rows, -1)
+    mod_weight_grad = product_tn(sinus_own, grad_mod_all.reshape(-1, 6 * D))
     return (
         output,
         grad_rows,
@@ -1106,8 +1191,8 @@
         cross_q_grad[None],
         cross_kv_grad[None],
         cross_out_grad[None],
-        mlp_in_grad,
-        gather(down_owned, "sp").astype(F32)[None],
+        mlp_in_grad[None],
+        mlp_out_grad[None],
     )
 
 

time: 923 us -> 820 us (0.89)
  Pallas kernels: 593 us -> 499 us
  local copies, waits for them, and re-layouts: 92.5 us -> 70.2 us
  other arithmetic: 59.2 us -> 77.3 us
  waiting for transfers between devices: 5.26 us -> 18.9 us
  blocking collectives: 42.6 us -> 30.5 us
    pallas_call x1 -> x5, Pallas kernels: 281 us -> 210 us  [the longest x1 191 us: gather_weights(): pl.pallas_call(functools.partial(gather_kernel, outer, kinds), out_shape=...]
    pallas_call x2 -> x1, Pallas kernels: 40.2 us -> 20.1 us  [plane_gather(): pl.pallas_call(plane_gather_kernel, out_shape=jax.ShapeDtypeStruct((2, 2,...]
    unnamed x260 -> x224, local copies, waits for them, and re-layouts: 21.2 us -> 39.6 us
    reshape x5 -> x2, local copies, waits for them, and re-layouts: 18.7 us -> 1.54 us  [the longest x1 1.52 us: body(): mod_weight_grad = product_tn(sinus_own, grad_mod_all.reshape(-1, 6 * D))]
    ppermute x0 -> x3, waiting for transfers between devices: none -> 16.4 us  [the longest x1 16.4 us: body(): beside = jnp.stack([beside, lax.ppermute(beside, 'yb', exchange)])]
    all_to_all x1 -> x0, blocking collectives: 16.2 us -> none  [body(): lax.all_to_all(up_owned, PL, split_axis=0, concat_axis=0, tiled=True)]
    dynamic_slice x7 -> x0, local copies, waits for them, and re-layouts: 12.4 us -> none  [the longest x2 6.22 us: body(): lax.dynamic_index_in_dim(mlp_in[0].reshape(in_rows, outer, PLANE, 2, hid)...]
  transfers between devices with their start and end apart: 10 -> 6, of which waited for: 2 -> 2; matrix products, arithmetic and copies ran while one was open for 16% -> 22% of each run, Pallas kernels for 56% -> 12%
where the time goes in v3:
time: 820 us; the launch traced here: 808 us
  Pallas kernels  499 us (61%)
  matrix products  93.8 us (11%)
  other arithmetic  77.3 us (9%)
  local copies, waits for them, and re-layouts  70.2 us (9%)
  blocking collectives  30.5 us (4%)
  waiting for transfers between devices  18.9 us (2%)
  between operations  16 us (2%)
    pallas_call x1, Pallas kernels, reduce_weights(): pl.pallas_call(functools.partial(reduce_kernel, outer, kinds), out_shape=...  208 us
    pallas_call x1, Pallas kernels, gather_weights(): pl.pallas_call(functools.partial(gather_kernel, outer, kinds), out_shape=...  191 us
    pallas_call x2, Pallas kernels, plane_sum(): pl.pallas_call(plane_sum_kernel, out_shape=jax.ShapeDtypeStruct((rows, wi...  40.4 us
    unnamed x224, local copies, waits for them, and re-layouts  39.6 us
    dot_general x8, matrix products, product(): return jnp.dot(left, right, preferred_element_type=F32)  35.6 us
    dot_general x6, matrix products, product_nt(): lax.dot_general(left, right, (((1,), (1,)), ((), ())), preferred_element_...  29.2 us
    dot_general x8, matrix products, product_tn(): lax.dot_general(left, right, (((0,), (0,)), ((), ())), preferred_element_...  29 us
    pallas_call x1, Pallas kernels, plane_gather(): pl.pallas_call(plane_gather_kernel, out_shape=jax.ShapeDtypeStruct((2, 2,...  20.1 us
  transfers between devices with their start and end apart: 6, of which 2 were waited for; matrix products, arithmetic and copies ran while one was open for 22% of the time, Pallas kernels for 12%

profile of v3, /device:TPU:0, one launch (start us, length us, event | category | flops | bytes accessed | tf_op | source)
XLA Modules:
  0.0 807.9 jit_solution(11795098982462293771)
XLA Ops:
  20.2 190.9 %gather_weights.1 = (f32[4,2,2,8,128]{4,3,2,1,0:T(8,128)S(1)}, bf16[4,2,2,16,4608]{4,3,2,1,0:T(8,128)(2,1)S(1)}, bf16[4,2,2,96,2304]{4,3,2,1,0:T(8,128)(2,1)}, b...) custom-call(f32[8,128]{1,0:T(8,128)S(1)} %maximum_bitcast_fusion.1.r, ...), custom_call_target="tpu_custom_call" | custom-call | flops 99999997952 | bytes 100000000 | tf_op jit(solution)/shard_map/gather_weights/pallas_call | solution.py:459
  229.5 5.4 fusion.80
  266.6 4.7 pair_sum.4
  287.5 5.3 shard_map.239
  296.5 4.7 pair_sum.5
  319.0 16.4 %collective-permute-done.1 = bf16[2,128,1536]{2,1,0:T(8,128)(2,1)S(1)} collective-permute-done((bf16[2,128,1536]{2,1,0:T(8,128)(2,1)S(1)}, bf16[2,128,1536]{2,1,0:T(8,128)(2,1)S(1)}, u32[]{:S(2)}, u32[]{:S(2)}) %collective-permute-start.1) | collective-permute-done | bytes 786464 | tf_op jit(solution)/shard_map/ppermute | solution.py:1047
  337.2 20.1 %plane_gather.1 = bf16[2,2,2,128,1536]{4,3,2,1,0:T(8,128)(2,1)} custom-call(bf16[128,1536]{1,0:T(8,128)(2,1)} %get-tuple-element.108.own_ref), custom_call_target="tpu_custom_call" | custom-call | flops 10000000000 | bytes 10000000 | tf_op jit(solution)/shard_map/plane_gather/pallas_call | solution.py:531
  357.4 7.0 fusion.84
  369.2 5.8 convolution_convert_fusion.2
  375.0 10.5 %fusion.6 = bf16[1024,1120]{0,1:T(8,128)(2,1)S(1)} fusion(f32[1024,1120]{0,1:T(8,128)} %copy-done.102, bf16[1024,1536]{1,0:T(8,128)(2,1)} %bitcast.229, bf16[1120,1536]{1,0:T(8,128)(2,1)} %all-gather.2.cloned.1.call-done), kind=kOutput, calls=%fused_computation.14 | convolution fusion | flops 3546152960 | bytes 13467648 | tf_op jit(solution)/shard_map/dot_general | solution.py:41
  385.6 5.8 convolution_convert_fusion.4
  391.4 5.1 convolution_convert_fusion.1
  396.7 9.7 %convolution_convert_fusion.5 = bf16[1024,1536]{1,0:T(8,128)(2,1)} fusion(bf16[1120,1536]{1,0:T(8,128)(2,1)} %all-gather.2.cloned.1.call-done, f32[1024,1120]{0,1:T(8,128)} %copy-done.102), kind=kOutput, calls=%fused_computation.17 | convolution fusion | flops 3535110144 | bytes 11173888 | tf_op jit(solution)/shard_map/dot_general | solution.py:33
  406.4 20.4 %plane_sum.3 = f32[128,1536]{1,0:T(8,128)} custom-call(bf16[2,2,2,128,1536]{4,3,2,1,0:T(8,128)(2,1)} %bitcast.295), custom_call_target="tpu_custom_call" | custom-call | flops 10000000000 | bytes 10000000 | tf_op jit(solution)/shard_map/plane_sum/pallas_call | solution.py:589
  429.5 20.0 %plane_sum.2 = f32[128,1536]{1,0:T(8,128)} custom-call(bf16[2,2,2,128,1536]{4,3,2,1,0:T(8,128)(2,1)} %bitcast.296), custom_call_target="tpu_custom_call" | custom-call | flops 10000000000 | bytes 10000000 | tf_op jit(solution)/shard_map/plane_sum/pallas_call | solution.py:589
  458.4 6.7 shard_map.240
  476.9 4.7 pair_sum.6
  490.7 5.1 shard_map.241
  499.9 5.8 copy.92
  518.2 6.2 fusion.86.part_ref
  524.4 4.8 pair_sum.7
  547.2 4.7 all_to_all.33
  565.4 4.9 convolution_convert_fusion
  577.2 207.8 %reduce_weights.1 = (f32[96,1536]{1,0:T(8,128)}, f32[96,3072]{1,0:T(8,128)}, f32[96,1536]{1,0:T(8,128)}, f32[96,1536]{1,0:T(8,128)}, f32[96,4608]{1,0:T(8,128)},...) custom-call(bf16[4,2,2,96,768]{4,3,2,1,0:T(8,128)(2,1)} %bitcast.238, ...), custom_call_target="tpu_custom_call" | custom-call | flops 99999997952 | bytes 100000000 | tf_op jit(solution)/shard_map/reduce_weights/pallas_call | solution.py:889
  (395 shorter events, 209.5 us)
Async XLA Ops:
  7.2 367.8 %all-gather.2.cloned.1.call-start = ((), (), s32[]{:S(2)}) async-start(), calls=%async_computation.4 | async-start | bytes 4300800 | tf_op jit(solution)/shard_map/all_gather | solution.py:933
  215.2 11.0 %copy-start.14 = (bf16[128,1536]{1,0:T(8,128)(2,1)S(1)}, bf16[128,1536]{1,0:T(8,128)(2,1)}, u32[]{:S(2)}) copy-start(bf16[128,1536]{1,0:T(8,128)(2,1)} %param.15) | copy-start | bytes 1179652
  215.2 359.6 %reduce-scatter.5.cloned.1.call-start = ((), (), s32[]{:S(2)}) async-start(), calls=%async_computation.5 | async-start | bytes 4300800 | tf_op jit(solution)/shard_map/reduce_scatter | solution.py:937
  216.0 13.5 %copy-start.58 = (f32[16,1024]{1,0:T(8,128)}, f32[16,1024]{1,0:T(8,128)S(1)}, u32[]{:S(2)}) copy-start(f32[16,1024]{1,0:T(8,128)S(1)} %reshape.729) | copy-start | bytes 196612
  222.8 12.1 %copy-start.61 = (f32[2,1536]{1,0:T(2,128)}, f32[2,1536]{1,0:T(2,128)S(1)}, u32[]{:S(2)}) copy-start(f32[2,1536]{1,0:T(2,128)S(1)} %get-tuple-element.135) | copy-start | bytes 36868
  223.6 90.9 %collective-permute-start = (bf16[128,1536]{1,0:T(8,128)(2,1)}, bf16[128,1536]{1,0:T(8,128)(2,1)}, u32[]{:S(2)}, u32[]{:S(2)}) collective-permute-start(bf16[128,1536]{1,0:T(8,128)(2,1)} %fusion.37), channel_id=1, source_target_pairs={{0,2},{2,0},{1,3},{3,1},{4,6},{6,4},{5,7},{7,5},{8,10},{10,8},{9,1... | collective-permute-start | bytes 1179656 | tf_op jit(solution)/shard_map/ppermute | solution.py:1046
  226.3 8.5 %copy-start.76 = (f32[128]{0:T(128)}, f32[128]{0:T(128)S(1)}, u32[]{:S(2)}) copy-start(f32[128]{0:T(128)S(1)} %broadcast_multiply_fusion.4) | copy-start | bytes 1540
  226.9 9.2 %slice-start = ((s8[4718592]{0:T(1024)(128)(4,1)}), s8[4194304]{0:T(1024)(128)(4,1)S(1)}, s32[]{:S(2)}) async-start(s8[4718592]{0:T(1024)(128)(4,1)} %bitcast.287), calls=%async_computation.7 | async-start | bytes 8388608
  309.5 8.7 %copy-start.90 = (f32[64]{0:T(128)S(1)}, f32[64]{0:T(128)}, u32[]{:S(2)}) copy-start(f32[64]{0:T(128)} %mul.1215) | copy-start | bytes 772
  309.5 8.7 %copy-start.92 = (f32[128]{0:T(128)S(1)}, f32[128]{0:T(128)}, u32[]{:S(2)}) copy-start(f32[128]{0:T(128)} %copy-done.91) | copy-start | bytes 1540
  315.7 19.7 %collective-permute-start.1 = (bf16[2,128,1536]{2,1,0:T(8,128)(2,1)S(1)}, bf16[2,128,1536]{2,1,0:T(8,128)(2,1)S(1)}, u32[]{:S(2)}, u32[]{:S(2)}) collective-permute-start(bf16[2,128,1536]{2,1,0:T(8,128)(2,1)S(1)} %get-tuple-element.130), channel_id=1, source_target_pairs={{0,4},{4,0},{1,5},{5,1},{2,6},{6,2},{3,7},{7,3},{8,12},{12,8},{9,1... | collective-permute-start | bytes 2359304 | tf_op jit(solution)/shard_map/ppermute | solution.py:1047
  337.2 27.1 %collective-permute-start.2 = (bf16[2,2,128,1536]{3,2,1,0:T(8,128)(2,1)}, bf16[2,2,128,1536]{3,2,1,0:T(8,128)(2,1)}, u32[]{:S(2)}, u32[]{:S(2)}) collective-permute-start(bf16[2,2,128,1536]{3,2,1,0:T(8,128)(2,1)} %get-tuple-element.119), channel_id=1, source_target_pairs={{0,1},{1,0},{2,3},{3,2},{4,5},{5,4},{6,7},{7,6},{8,9},{9,8},{10,11... | collective-permute-start | bytes 4718600 | tf_op jit(solution)/shard_map/ppermute | solution.py:1048
  375.0 10.5 %copy-start.99 = (bf16[4,4,96,1120]{3,2,1,0:T(8,128)(2,1)S(1)}, bf16[4,4,96,1120]{3,2,1,0:T(8,128)(2,1)}, u32[]{:S(2)}) copy-start(bf16[4,4,96,1120]{3,2,1,0:T(8,128)(2,1)} %get-tuple-element.56) | copy-start | bytes 10321924
  396.5 180.7 %reduce-scatter.7.cloned.1.call-start = ((), (), s32[]{:S(2)}) async-start(), calls=%async_computation.6 | async-start | bytes 4423680 | tf_op jit(solution)/shard_map/reduce_scatter | solution.py:937
  524.4 8.4 %copy-start.81 = (f32[768]{0:T(1024)S(1)}, f32[768]{0:T(1024)}, u32[]{:S(2)}) copy-start(f32[768]{0:T(1024)} %get-tuple-element.78) | copy-start | bytes 9220
  524.4 8.4 %copy-start.80 = (f32[768]{0:T(1024)S(1)}, f32[768]{0:T(1024)}, u32[]{:S(2)}) copy-start(f32[768]{0:T(1024)} %get-tuple-element.80) | copy-start | bytes 9220
  524.4 8.4 %copy-start.79 = (f32[768]{0:T(1024)S(1)}, f32[768]{0:T(1024)}, u32[]{:S(2)}) copy-start(f32[768]{0:T(1024)} %get-tuple-element.85) | copy-start | bytes 9220
  524.4 8.6 %copy-start.96 = (pred[16]{0:T(512)(128)(4,1)S(1)}, pred[16]{0:T(512)(128)(4,1)}, u32[]{:S(2)}) copy-start(pred[16]{0:T(512)(128)(4,1)} %broadcast_in_dim.192) | copy-start | bytes 52
  524.4 9.3 %copy-start.95 = (f32[128]{0:T(128)S(1)}, f32[128]{0:T(128)}, u32[]{:S(2)}) copy-start(f32[128]{0:T(128)} %copy-done.94) | copy-start | bytes 1540
  534.1 22.8 %copy-start.19 = (f32[512,1536]{1,0:T(8,128)S(1)}, f32[512,1536]{1,0:T(8,128)}, u32[]{:S(2)}) copy-start(f32[512,1536]{1,0:T(8,128)} %copy-done.17) | copy-start | bytes 9437188
  536.9 17.8 %copy-start.82 = (f32[1024]{0:T(1024)S(1)}, f32[1024]{0:T(1024)}, u32[]{:S(2)}) copy-start(f32[1024]{0:T(1024)} %pad.2.clone) | copy-start | bytes 12292
  536.9 20.1 %copy-start.67 = (f32[1,512]{1,0:T(1,128)S(1)}, f32[1,512]{1,0:T(1,128)}, u32[]{:S(2)}) copy-start(f32[1,512]{1,0:T(1,128)} %copy-done.64) | copy-start | bytes 6148
  536.9 20.1 %copy-start.85 = (f32[512]{0:T(512)S(1)}, f32[512]{0:T(512)}, u32[]{:S(2)}) copy-start(f32[512]{0:T(512)} %multiply_multiply_fusion.4) | copy-start | bytes 6148
  538.1 20.5 %copy-start.50 = (bf16[256,768]{1,0:T(8,128)(2,1)S(1)}, bf16[256,768]{1,0:T(8,128)(2,1)}, u32[]{:S(2)}) copy-start(bf16[256,768]{1,0:T(8,128)(2,1)} %get-tuple-element.49) | copy-start | bytes 1179652
  (87 other events, 325.9 us)
Sparse Core Ops, SparseCore 0:
  215.4 68.7 all-gather.1
  396.6 65.1 reduce-scatter.4
  510.6 66.6 reduce-scatter.6

commit v4 on v3

--- a/solution.py
+++ b/solution.py
@@ -8,6 +8,7 @@
 from jax.experimental.pallas import tpu as pltpu
 from jax.sharding import Mesh
 from jax.sharding import PartitionSpec as P
+
 
 D = 1536
 HD = 128
@@ -541,68 +542,69 @@
     return out.reshape(8 * rows, width)
 
 
-def plane_sum_kernel(part_ref, out_ref, core_in, first, second, keep, send, recv):
+def plane_sum_kernel(part_a, part_b, out_a, out_b, core_in, first, second, keep, send, recv):
     y, x, core = lax.axis_index("yb"), lax.axis_index("xc"), lax.axis_index("sp")
     x_peer, y_peer, core_peer = {"xc": 1 - x}, {"yb": 1 - y}, {"sp": 1 - core}
     fly = Flights()
     greet((x_peer, y_peer, core_peer))
-    rows = part_ref.shape[3]
-    size = rows // 2
-    top, low = pl.ds(0, size), pl.ds(size, size)
-    chips = ((1, 1), (1, 0), (0, 1), (0, 0))
-    for index, (dy, dx) in enumerate(chips):
-        fly.send(part_ref.at[dy, dx, 1], core_in.at[index], send.at[index], recv.at[index], core_peer)
-
-    def core_sum(index):
-        dy, dx = chips[index]
-        landed(core_in.at[index], recv.at[index], core_peer)
-        row_add(core_in.at[index], core_in.at[index], part_ref.at[dy, dx, 0], rows)
-
-    core_sum(0)
-    fly.send(core_in.at[0, top], first.at[0], send.at[4], recv.at[4], y_peer)
-    fly.send(core_in.at[0, low], first.at[1], send.at[5], recv.at[5], x_peer)
-    core_sum(1)
-    fly.send(core_in.at[1, top], first.at[2], send.at[6], recv.at[6], y_peer)
-    core_sum(2)
-    fly.send(core_in.at[2, low], first.at[3], send.at[7], recv.at[7], x_peer)
-    core_sum(3)
-    landed(first.at[0], recv.at[4], y_peer)
-    row_add(second.at[0], first.at[0], core_in.at[2, top], size)
-    fly.send(second.at[0], second.at[2], send.at[8], recv.at[8], x_peer)
-    landed(first.at[1], recv.at[5], x_peer)
-    row_add(second.at[1], first.at[1], core_in.at[1, low], size)
-    fly.send(second.at[1], second.at[3], send.at[9], recv.at[9], y_peer)
-    landed(first.at[2], recv.at[6], y_peer)
-    row_sum(keep.at[top], first.at[2], core_in.at[3, top], size)
-    landed(first.at[3], recv.at[7], x_peer)
-    row_sum(keep.at[low], first.at[3], core_in.at[3, low], size)
-    landed(second.at[2], recv.at[8], x_peer)
-    row_sum(out_ref.at[top], keep.at[top], second.at[2], size)
-    landed(second.at[3], recv.at[9], y_peer)
-    row_sum(out_ref.at[low], keep.at[low], second.at[3], size)
+    rows = part_a.shape[3]
+    chips = (((1, 1), (1, 0), (0, 1), (0, 0)), ((1, 1), (0, 1), (1, 0), (0, 0)))
+    parts, outs, peers = (part_a, part_b), (out_a, out_b), ((y_peer, x_peer), (x_peer, y_peer))
+    for index in range(4):
+        for n in range(2):
+            dy, dx = chips[n][index]
+            fly.send(
+                parts[n].at[dy, dx, 1], core_in.at[n, index], send.at[n, index], recv.at[n, index], core_peer
+            )
+
+    def core_sum(n, index):
+        dy, dx = chips[n][index]
+        landed(core_in.at[n, index], recv.at[n, index], core_peer)
+        row_add(core_in.at[n, index], core_in.at[n, index], parts[n].at[dy, dx, 0], rows)
+
+    for index in range(2):
+        for n in range(2):
+            core_sum(n, index)
+            fly.send(
+                core_in.at[n, index], first.at[n, index], send.at[n, index + 4], recv.at[n, index + 4], peers[n][0]
+            )
+    for index in (2, 3):
+        for n in range(2):
+            core_sum(n, index)
+    for n in range(2):
+        landed(first.at[n, 0], recv.at[n, 4], peers[n][0])
+        row_add(second.at[n, 0], first.at[n, 0], core_in.at[n, 2], rows)
+        fly.send(second.at[n, 0], second.at[n, 1], send.at[n, 6], recv.at[n, 6], peers[n][1])
+    for n in range(2):
+        landed(first.at[n, 1], recv.at[n, 5], peers[n][0])
+        row_sum(keep.at[n], first.at[n, 1], core_in.at[n, 3], rows)
+    for n in range(2):
+        landed(second.at[n, 1], recv.at[n, 6], peers[n][1])
+        row_sum(outs[n], keep.at[n], second.at[n, 1], rows)
     fly.drain()
 
 
-def plane_sum(partial):
-    rows, width = partial.shape[0] // 8, partial.shape[1]
+def plane_sum(one, other):
+    rows, width = one.shape[0] // 8, one.shape[1]
     dma = pltpu.SemaphoreType.DMA
+    shape = jax.ShapeDtypeStruct((rows, width), F32)
     return pl.pallas_call(
         plane_sum_kernel,
-        out_shape=jax.ShapeDtypeStruct((rows, width), F32),
-        in_specs=[VM],
-        out_specs=VM,
+        out_shape=(shape, shape),
+        in_specs=[VM, VM],
+        out_specs=(VM, VM),
         scratch_shapes=[
-            pltpu.VMEM((4, rows, width), BF),
-            pltpu.VMEM((4, rows // 2, width), BF),
-            pltpu.VMEM((4, rows // 2, width), BF),
-            pltpu.VMEM((rows, width), F32),
-            dma((10,)),
-            dma((10,)),
+            pltpu.VMEM((2, 4, rows, width), BF),
+            pltpu.VMEM((2, 2, rows, width), BF),
+            pltpu.VMEM((2, 2, rows, width), BF),
+            pltpu.VMEM((2, rows, width), F32),
+            dma((2, 7)),
+            dma((2, 7)),
         ],
         compiler_params=pltpu.CompilerParams(collective_id=2, has_side_effects=True),
         cost_estimate=pl.CostEstimate(flops=10**10, bytes_accessed=10**7, transcendentals=0),
         name="plane_sum",
-    )(partial.reshape(2, 2, 2, rows, width))
+    )(one.reshape(2, 2, 2, rows, width), other.reshape(2, 2, 2, rows, width))
 
 
 def pair_sum_kernel(part_ref, out_ref, peer_in, send, recv):
@@ -637,6 +639,7 @@
 
 
 AHEAD, LAG_PLANE, LAG_CHAIN = 6, 2, 4
+PLAIN, SPLIT, OVER_X, OVER_Y = range(4)
 
 
 def reduce_kernel(outer, kinds, *refs):
@@ -646,10 +649,17 @@
     frames_ref, small_ref, up_ref, down_ref, refs = *refs[:4], refs[4:]
     outs, refs = refs[:count], refs[count:]
     frames_out, small_out, up_out, down_out, refs = *refs[:4], refs[4:]
-    near, refs = refs[:count], refs[count:]
-    plane, refs = refs[:count], refs[count:]
-    chain, refs = refs[:count], refs[count:]
-    split = [i for i, kind in enumerate(kinds) if kind[1]]
+    pieces = [(i, part) for i, (parts, _) in enumerate(kinds) for part in range(parts)]
+    total = len(pieces)
+    forms = [kinds[i][1] for i, _ in pieces]
+    near_refs, near = list(refs), {}
+    for p in range(total):
+        if forms[p] in (PLAIN, SPLIT):
+            near[p] = near_refs.pop(0)
+    refs = near_refs
+    plane, refs = refs[:total], refs[total:]
+    chain, refs = refs[:total], refs[total:]
+    split = [i for i, kind in enumerate(kinds) if kind[1] == SPLIT]
     whole, refs = refs[: len(split)], refs[len(split) :]
     small_in, small_own, small_peer, up_in, down_in, refs = *refs[:5], refs[5:]
     e_s, e_r, e_l, s1, r1, s2, r2, zs, zr, o_s, o_r, f_s, f_r, m_s, m_r, l_s, p_s, p_r = refs
@@ -666,24 +676,30 @@
     others = [(here + j) % shards for j in range(1, shards)]
     greet((core_peer, *[chip(index) for index in others]))
 
-    part = outer // 2
-    source = list(gs)
+    part_slots = outer // 2
+    ours, other_slots = pl.ds(core * part_slots, part_slots), pl.ds((1 - core) * part_slots, part_slots)
     for j, i in enumerate(split):
         width = whole[j].shape[-1]
         mine = pl.ds(pl.multiple_of(core * width, width), width)
         theirs = pl.ds(pl.multiple_of((1 - core) * width, width), width)
-        ours = pl.ds(core * part, part)
         fly.send(gs[i].at[:, :, :, :, theirs], whole[j].at[ours], e_s.at[j], e_r.at[j], core_peer)
         fly.local(gs[i].at[:, :, :, :, mine], whole[j].at[ours], e_l.at[j])
-        source[i] = whole[j]
 
     def joined(i):
         j = split.index(i)
         width = whole[j].shape[-1]
         mine = pl.ds(pl.multiple_of(core * width, width), width)
-        ours, other = pl.ds(core * part, part), pl.ds((1 - core) * part, part)
         pltpu.make_async_copy(gs[i].at[:, :, :, :, mine], whole[j].at[ours], e_l.at[j]).wait()
-        landed(whole[j].at[other], e_r.at[j], core_peer)
+        landed(whole[j].at[other_slots], e_r.at[j], core_peer)
+
+    def width_of(p):
+        return plane[p].shape[-1]
+
+    def source(p, *place):
+        i, part = pieces[p]
+        held = whole[split.index(i)] if forms[p] == SPLIT else gs[i]
+        width = width_of(p)
+        return held.at[(*place, slice(None), pl.ds(part * width, width))]
 
     frame_width = frames_ref.shape[1]
     frame_mine = pl.ds(pl.multiple_of(core * frame_width, frame_width), frame_width)
@@ -735,12 +751,12 @@
         falling = outer - 1 - step
         falling = jnp.where(falling > z, falling, falling - 1)
         rising = jnp.where(step < z, step, step + 1)
-        return jnp.where(z < part, falling, rising)
-
-    units = [(slot_at(step), i) for step in range(outer) for i in range(count)]
-
-    def turns(i, slot):
-        turn = (slot + i) % 2
+        return jnp.where(z < part_slots, falling, rising)
+
+    units = [(slot_at(step), p) for step in range(outer) for p in range(total)]
+
+    def turns(p, slot):
+        turn = (slot + p) % 2
         first = ((y + 1 - turn) % 2, (x + turn) % 2)
         second = ((y + turn) % 2, (x + 1 - turn) % 2)
         return first, second
@@ -748,84 +764,90 @@
     def device(place):
         return {"yb": place[0], "xc": place[1]}
 
-    def start(slot, i):
-        first, _ = turns(i, slot)
+    def start(slot, p):
+        first, _ = turns(p, slot)
         fly.send(
-            source[i].at[slot, 1 - y, 1 - x], near[i].at[slot, 1], s1.at[i, slot, 1], r1.at[i, slot, 1], device(first)
+            source(p, slot, 1 - y, 1 - x), near[p].at[slot, 1], s1.at[p, slot, 1], r1.at[p, slot, 1], device(first)
         )
         fly.send(
-            source[i].at[slot, first[0], first[1]], near[i].at[slot, 0], s1.at[i, slot, 0], r1.at[i, slot, 0], device(first)
+            source(p, slot, first[0], first[1]), near[p].at[slot, 0], s1.at[p, slot, 0], r1.at[p, slot, 0], device(first)
         )
 
-    def pass_on(slot, i):
-        first, second = turns(i, slot)
-        rows = near[i].shape[2]
-        landed(near[i].at[slot, 1], r1.at[i, slot, 1], device(first))
-        row_add(near[i].at[slot, 1], near[i].at[slot, 1], source[i].at[slot, second[0], second[1]], rows)
-        fly.send(near[i].at[slot, 1], plane[i].at[slot], s2.at[i, slot], r2.at[i, slot], device(second))
-        landed(near[i].at[slot, 0], r1.at[i, slot, 0], device(first))
-        row_add(near[i].at[slot, 0], near[i].at[slot, 0], source[i].at[slot, y, x], rows)
-
-    def plane_total(slot, i):
-        _, second = turns(i, slot)
-        rows = near[i].shape[2]
-        landed(plane[i].at[slot], r2.at[i, slot], device(second))
-        row_add(plane[i].at[slot], plane[i].at[slot], near[i].at[slot, 0], rows)
-
-    def along(slot, i, last):
-        rows = near[i].shape[2]
+    def summed_over(p):
+        return (x, {"xc": 1 - x}) if forms[p] == OVER_X else (y, {"yb": 1 - y})
+
+    def pass_on(slot, p):
+        rows = plane[p].shape[1]
+        if p not in near:
+            index, peer = summed_over(p)
+            fly.send(source(p, slot, 1 - index), plane[p].at[slot], s2.at[p, slot], r2.at[p, slot], peer)
+            return
+        first, second = turns(p, slot)
+        landed(near[p].at[slot, 1], r1.at[p, slot, 1], device(first))
+        row_add(near[p].at[slot, 1], near[p].at[slot, 1], source(p, slot, second[0], second[1]), rows)
+        fly.send(near[p].at[slot, 1], plane[p].at[slot], s2.at[p, slot], r2.at[p, slot], device(second))
+        landed(near[p].at[slot, 0], r1.at[p, slot, 0], device(first))
+        row_add(near[p].at[slot, 0], near[p].at[slot, 0], source(p, slot, y, x), rows)
+
+    def plane_total(slot, p):
+        rows = plane[p].shape[1]
+        if p not in near:
+            index, peer = summed_over(p)
+            landed(plane[p].at[slot], r2.at[p, slot], peer)
+            row_add(plane[p].at[slot], plane[p].at[slot], source(p, slot, index), rows)
+            return
+        _, second = turns(p, slot)
+        landed(plane[p].at[slot], r2.at[p, slot], device(second))
+        row_add(plane[p].at[slot], plane[p].at[slot], near[p].at[slot, 0], rows)
+
+    def along(slot, p, last):
+        rows, width = plane[p].shape[1:]
         if not last:
             for way, when, edge, ahead, behind in (
                 (1, slot < z, z == outer - 1, below, above),
                 (0, slot > z, z == 0, above, below),
             ):
+                link = chain[p].at[slot + 1 - way]
 
                 @pl.when(jnp.logical_and(when, jnp.logical_not(edge)))
-                def _():
-                    landed(chain[i].at[slot + 1 - way], zr.at[i, way, slot], behind)
-                    row_add(plane[i].at[slot], plane[i].at[slot], chain[i].at[slot + 1 - way], rows)
-
-                fly.send(
-                    plane[i].at[slot], chain[i].at[slot + 1 - way], zs.at[i, way, slot], zr.at[i, way, slot], ahead, when
-                )
+                def _(way=way, link=link, behind=behind):
+                    landed(link, zr.at[p, way, slot], behind)
+                    row_add(plane[p].at[slot], plane[p].at[slot], link, rows)
+
+                fly.send(plane[p].at[slot], link, zs.at[p, way, slot], zr.at[p, way, slot], ahead, when)
             return
-        parts = kinds[i][0]
-        width = plane[i].shape[-1] // parts
-        for way, when, behind in ((1, z < outer - 1, above), (0, z > 0, below)):
+        has_above, has_below = z < outer - 1, z > 0
+        for way, when, behind in ((1, has_above, above), (0, has_below, below)):
 
             @pl.when(when)
-            def _():
-                landed(chain[i].at[slot + 1 - way], zr.at[i, way, slot], behind)
+            def _(way=way, behind=behind):
+                landed(chain[p].at[slot + 1 - way], zr.at[p, way, slot], behind)
 
         step = 16 if rows % 16 == 0 else rows
-        has_above, has_below = z < outer - 1, z > 0
+        i, part = pieces[p]
+        column = pl.multiple_of((2 * part + core) * width, width)
 
         def chunk(index, carry):
             at = pl.ds(pl.multiple_of(index * step, step), step)
-            for part_no in range(parts):
-                span = slice(part_no * width, (part_no + 1) * width)
-                total = plane[i][slot, at, span].astype(F32)
-                upper = chain[i][slot, at, span].astype(F32)
-                lower = chain[i][slot + 1, at, span].astype(F32)
-                total = total + jnp.where(has_above, upper, 0.0) + jnp.where(has_below, lower, 0.0)
-                column = pl.multiple_of((2 * part_no + core) * width, width)
-                outs[i][at, pl.ds(column, width)] = total
+            upper = jnp.where(has_above, chain[p][slot, at, :].astype(F32), 0.0)
+            lower = jnp.where(has_below, chain[p][slot + 1, at, :].astype(F32), 0.0)
+            outs[i][at, pl.ds(column, width)] = plane[p][slot, at, :].astype(F32) + upper + lower
             return carry
 
         lax.fori_loop(0, rows // step, chunk, 0)
-        for part_no in range(parts):
-            column = pl.multiple_of((2 * part_no + core) * width, width)
-            block = outs[i].at[:, pl.ds(column, width)]
-            fly.send(block, block, o_s.at[i, part_no], o_r.at[i, part_no], core_peer)
+        block = outs[i].at[:, pl.ds(column, width)]
+        fly.send(block, block, o_s.at[p], o_r.at[p], core_peer)
 
     waiting = set(split)
 
     def begin(unit):
-        slot, i = units[unit]
-        if i in waiting:
-            joined(i)
-            waiting.discard(i)
-        start(slot, i)
+        slot, p = units[unit]
+        if p not in near:
+            return
+        if pieces[p][0] in waiting:
+            joined(pieces[p][0])
+            waiting.discard(pieces[p][0])
+        start(slot, p)
 
     for unit in range(min(AHEAD, len(units))):
         begin(unit)
@@ -836,56 +858,58 @@
                 begin(tick + AHEAD)
         if 0 <= tick - LAG_PLANE < len(units):
             plane_total(*units[tick - LAG_PLANE])
-        if tick == 2:
+        if tick == 4:
             feed_forward_landed()
-        if tick == 6:
+        if tick == 10:
             feed_forward_rows()
         if 0 <= tick - LAG_CHAIN < len(units):
             unit = tick - LAG_CHAIN
-            along(*units[unit], unit >= (outer - 1) * count)
-
-    small_copy.wait()
-    frame_copy.wait()
-    for index in others:
-        landed(small_in.at[index], m_r.at[index], chip(index))
-    small_own[...] = jnp.sum(small_in[...], axis=0)
-    fly.send(small_own, small_peer, l_s.at[2], l_s.at[3], core_peer)
-    for index in others:
-        landed(frames_out.at[index, :, frame_mine], f_r.at[index], chip(index))
-    fly.send(frames_out.at[:, :, frame_mine], frames_out.at[:, :, frame_mine], p_s.at[6], p_r.at[6], core_peer)
+            along(*units[unit], unit >= (outer - 1) * total)
+        if tick == total:
+            frame_copy.wait()
+            for index in others:
+                landed(frames_out.at[index, :, frame_mine], f_r.at[index], chip(index))
+            fly.send(frames_out.at[:, :, frame_mine], frames_out.at[:, :, frame_mine], p_s.at[6], p_r.at[6], core_peer)
+            small_copy.wait()
+            for index in others:
+                landed(small_in.at[index], m_r.at[index], chip(index))
+            small_own[...] = jnp.sum(small_in[...], axis=0)
+            fly.send(small_own, small_peer, l_s.at[2], l_s.at[3], core_peer)
+
     landed(frames_out.at[:, :, frame_other], p_r.at[6], core_peer)
     landed(small_peer, l_s.at[3], core_peer)
     small_out[...] = small_own[...] + small_peer[...]
-    for i in range(count):
-        parts = kinds[i][0]
-        width = plane[i].shape[-1] // parts
-        for part_no in range(parts):
-            column = pl.multiple_of((2 * part_no + 1 - core) * width, width)
-            landed(outs[i].at[:, pl.ds(column, width)], o_r.at[i, part_no], core_peer)
+    for p, (i, part) in enumerate(pieces):
+        width = width_of(p)
+        column = pl.multiple_of((2 * part + 1 - core) * width, width)
+        landed(outs[i].at[:, pl.ds(column, width)], o_r.at[p], core_peer)
     fly.drain()
 
 
 def reduce_weights(outer, kinds, grads, frames, small, up, down):
     shards = outer * PLANE
-    count = len(kinds)
     shaped, shapes, near, plane, chain, whole = [], [], [], [], [], []
-    for (parts, split), grad in zip(kinds, grads, strict=True):
-        lead = outer // 2 if split else outer
-        rows = grad.shape[0] // (lead * PLANE)
-        width = grad.shape[1] // 2 if split else grad.shape[1]
-        shaped.append(grad.reshape(lead, 2, 2, rows, grad.shape[1]))
-        shapes.append(jax.ShapeDtypeStruct((rows, 2 * width), F32))
-        near.append(pltpu.VMEM((outer, 2, rows, width), BF))
-        plane.append(pltpu.VMEM((outer, rows, width), BF))
-        chain.append(pltpu.VMEM((outer + 1, rows, width), BF))
-        if split:
-            whole.append(pltpu.VMEM((outer, 2, 2, rows, width), BF))
+    for (parts, form), grad in zip(kinds, grads, strict=True):
+        full_width = grad.shape[-1] // 2 if form == SPLIT else grad.shape[-1]
+        if form in (PLAIN, SPLIT):
+            lead = outer // 2 if form == SPLIT else outer
+            grad = grad.reshape(lead, 2, 2, -1, grad.shape[-1])
+        rows, width = grad.shape[-2], full_width // parts
+        shaped.append(grad)
+        shapes.append(jax.ShapeDtypeStruct((rows, 2 * full_width), F32))
+        for _ in range(parts):
+            if form in (PLAIN, SPLIT):
+                near.append(pltpu.VMEM((outer, 2, rows, width), BF))
+            plane.append(pltpu.VMEM((outer, rows, width), BF))
+            chain.append(pltpu.VMEM((outer + 1, rows, width), BF))
+        if form == SPLIT:
+            whole.append(pltpu.VMEM((outer, 2, 2, rows, full_width), BF))
     shapes.append(jax.ShapeDtypeStruct((shards, frames.shape[0], 2 * frames.shape[1]), frames.dtype))
     shapes.append(jax.ShapeDtypeStruct(small.shape[1:], F32))
     shapes.append(jax.ShapeDtypeStruct((up.shape[1], 2 * PLANE * up.shape[2]), F32))
     shapes.append(jax.ShapeDtypeStruct((2 * down.shape[0], down.shape[1]), F32))
     dma = pltpu.SemaphoreType.DMA
-    nsplit = len(whole)
+    count, total, nsplit = len(kinds), len(plane), len(whole)
     results = pl.pallas_call(
         functools.partial(reduce_kernel, outer, kinds),
         out_shape=shapes,
@@ -904,14 +928,14 @@
             dma((nsplit,)),
             dma((nsplit,)),
             dma((nsplit,)),
-            dma((count, outer, 2)),
-            dma((count, outer, 2)),
-            dma((count, outer)),
-            dma((count, outer)),
-            dma((count, 2, outer)),
-            dma((count, 2, outer)),
-            dma((count, 3)),
-            dma((count, 3)),
+            dma((total, outer, 2)),
+            dma((total, outer, 2)),
+            dma((total, outer)),
+            dma((total, outer)),
+            dma((total, 2, outer)),
+            dma((total, 2, outer)),
+            dma((total,)),
+            dma((total,)),
             dma((shards,)),
             dma((shards,)),
             dma((shards,)),
@@ -949,7 +973,7 @@
     return jnp.sum(values * values, axis=1)
 
 
-def rms_back(values, inverse, gain, grad):
+def rms_back(values, gain, grad):
     scaled = grad * gain
     return scaled, jnp.sum(scaled * values, axis=1)
 
@@ -984,6 +1008,7 @@
     outer = shards // PLANE
     core = lax.axis_index("sp")
     chip = lax.axis_index(FS)
+    in_rows = self_in.shape[1]
     own_frame = core * frame_count
 
     bias_len, gain_len = mod_bias.shape[1], qk_gains.shape[2]
@@ -1043,10 +1068,12 @@
 
     grad_branch = frame_scaled(cotangent.astype(F32), gate_two).astype(BF)
     exchange = [(0, 1), (1, 0)]
-    beside = jnp.stack([grad_branch, lax.ppermute(grad_branch, "xc", exchange)])
-    beside = jnp.stack([beside, lax.ppermute(beside, "yb", exchange)])
-    beside = jnp.stack([beside, lax.ppermute(beside, "sp", exchange)], axis=2)
-    grad_branch_all = beside.reshape(-1, D)
+    beside = [
+        grad_branch,
+        lax.ppermute(grad_branch, "xc", exchange),
+        lax.ppermute(grad_branch, "yb", exchange),
+        lax.ppermute(grad_branch, PL, [(0, 3), (1, 2), (2, 1), (3, 0)]),
+    ]
 
     residual = tokens.astype(F32)
     attn_float, back_attn_input = jax.vjp(modulated, residual, shift_one, scale_one)
@@ -1061,6 +1088,9 @@
     self_mixed, self_lse = attend_forward(live_keys, query, key, value)
     self_branch = pair_sum(product(self_mixed, self_back))
     residual = residual + frame_scaled(self_branch, gate_one)
+    residual, *beside = lax.optimization_barrier((residual, *beside))
+    beside = jnp.stack(beside)
+    grad_branch_all = jnp.stack([beside, lax.ppermute(beside, "sp", exchange)], axis=1).reshape(-1, D)
 
     text_raw = product(text_all, cross_kvproj)
     raw_ck, raw_cv = text_raw[:, :half], text_raw[:, half:]
@@ -1084,11 +1114,9 @@
     )
     activated = activated_float.astype(BF)
 
-    mlp_branch = plane_sum(product(activated, down_matrix).astype(BF))
-    output = (residual + frame_scaled(mlp_branch, gate_two)).astype(BF)
+    mlp_part = product(activated, down_matrix).astype(BF)
 
     grad_rows = cotangent.astype(F32)
-    grad_gate_two = frame_sum(grad_rows * mlp_branch, frame_count)
     grad_down = product_tn(activated, grad_branch_all).astype(BF)
     grad_up_low = back_gelu(product_nt(grad_branch_all, down_matrix))[0].astype(BF)
     grad_up = product_tn(mlp_input, grad_up_low).astype(BF)
@@ -1096,7 +1124,9 @@
     grad_mlp_part, grad_up, grad_down = lax.optimization_barrier((grad_mlp_part, grad_up, grad_down))
     down_owned = scatter(grad_down, "za")
     up_owned = scatter(grad_up, "za")
-    grad_mlp_input = plane_sum(grad_mlp_part)
+    mlp_branch, grad_mlp_input = plane_sum(mlp_part, grad_mlp_part)
+    output = (residual + frame_scaled(mlp_branch, gate_two)).astype(BF)
+    grad_gate_two = frame_sum(grad_rows * mlp_branch, frame_count)
     grad_from_mlp, grad_shift_two, grad_scale_two = back_mlp_input(grad_mlp_input)
     grad_rows = grad_rows + grad_from_mlp
 
@@ -1109,16 +1139,21 @@
     grad_cq, grad_ck = grad_cq.astype(F32), grad_ck.astype(F32)
     grad_gain_two = jnp.sum(grad_cq * cross_raw * inv_cq[:, None], axis=0)
     grad_gain_three = jnp.sum(grad_ck * raw_ck * inv_ck[:, None], axis=0)
-    scaled_cq, dots_cq = rms_back(cross_raw, inv_cq, gain_own[2], grad_cq)
-    scaled_ck, dots_ck = rms_back(raw_ck, inv_ck, gain_own[3], grad_ck)
-    dots_cq = lax.psum(dots_cq[None], "sp")[0]
-    dots_ck = lax.psum(dots_ck[None], "sp")[0]
+    scaled_cq, dots_cq = rms_back(cross_raw, gain_own[2], grad_cq)
+    scaled_ck, dots_ck = rms_back(raw_ck, gain_own[3], grad_ck)
+    dots = lax.psum(jnp.concatenate([dots_cq, dots_ck])[None], "sp")[0]
+    dots_cq, dots_ck = dots[: dots_cq.shape[0]], dots[dots_cq.shape[0] :]
     grad_cross_low = rms_finish(cross_raw, inv_cq, scaled_cq, dots_cq).astype(BF)
     grad_text_low = jnp.concatenate(
         [rms_finish(raw_ck, inv_ck, scaled_ck, dots_ck).astype(BF), grad_cv], axis=1
     )
     grad_cross_qproj = product_tn(cross_input, grad_cross_low).astype(BF)
     grad_cross_kvproj = product_tn(text_all, grad_text_low).astype(BF)
+    place_y, place_x = lax.axis_index("yb"), lax.axis_index("xc")
+    kv_parts = grad_cross_kvproj.reshape(outer, 2, 2, in_rows, -1)
+    q_parts = grad_cross_qproj.reshape(outer, 2, 2, in_rows, -1)
+    kv_sent = lax.ppermute(lax.dynamic_index_in_dim(kv_parts, 1 - place_y, 1, False), "yb", exchange)
+    q_sent = lax.ppermute(lax.dynamic_index_in_dim(q_parts, 1 - place_x, 2, False), "xc", exchange)
     grad_cross_input = pair_sum(product_nt(grad_cross_low, cross_qproj))
     grad_rows = grad_rows + back_cross_norm(grad_cross_input)[0]
 
@@ -1133,8 +1168,8 @@
     grad_k = rotate(grad_k.astype(F32), cosine, -sine)
     grad_gain_zero = jnp.sum(grad_q * raw_q * inv_q[:, None], axis=0)
     grad_gain_one = jnp.sum(grad_k * raw_k * inv_k[:, None], axis=0)
-    scaled_q, dots_q = rms_back(raw_q, inv_q, gain_own[0], grad_q)
-    scaled_k, dots_k = rms_back(raw_k, inv_k, gain_own[1], grad_k)
+    scaled_q, dots_q = rms_back(raw_q, gain_own[0], grad_q)
+    scaled_k, dots_k = rms_back(raw_k, gain_own[1], grad_k)
     dots = lax.psum(jnp.stack([dots_q, dots_k]), "sp")
     grad_joined_low = jnp.concatenate(
         [
@@ -1165,10 +1200,12 @@
         ],
         axis=1,
     ).reshape(shards, small_rows, small_width)
+    kv_near = lax.dynamic_index_in_dim(kv_parts, place_y, 1, False) + kv_sent
+    q_near = lax.dynamic_index_in_dim(q_parts, place_x, 2, False) + q_sent
     owned, grad_mod_all, small_owned, mlp_in_grad, mlp_out_grad = reduce_weights(
         outer,
-        ((1, False), (2, False), (1, True), (1, True), (3, False)),
-        [grad_cross_qproj, grad_cross_kvproj, grad_cross_back, grad_self_back, grad_self_proj],
+        ((1, OVER_Y), (2, OVER_X), (1, SPLIT), (1, SPLIT), (3, PLAIN)),
+        [q_near, kv_near, grad_cross_back, grad_self_back, grad_self_proj],
         grad_mod_half.astype(BF),
         grad_small,
         up_owned.reshape(PLANE, -1, up_owned.shape[1]),
@@ -1213,4 +1250,5 @@
         rows,
     )
     out_specs = (rows, rows, second, P(None, FS), P(None, None, FS), *([second] * 7))
+
     return jax.shard_map(body, mesh=inner, in_specs=in_specs, out_specs=out_specs, check_vma=False)

time: 820 us -> 783 us (0.955)
  Pallas kernels: 499 us -> 447 us
    pallas_call x1, Pallas kernels: 208 us -> 162 us  [reduce_weights(): pl.pallas_call(functools.partial(reduce_kernel, outer, kinds), out_shape=...]
    ppermute x3 -> x6, waiting for transfers between devices: 16.4 us -> 25.3 us  [the longest x1 17.1 us: body(): lax.ppermute(lax.dynamic_index_in_dim(q_parts, 1 - place_x, 2, False), 'x...]
    pallas_call x2 -> x1, Pallas kernels: 40.4 us -> 35 us  [plane_sum(): pl.pallas_call(plane_sum_kernel, out_shape=(shape, shape), in_specs=[VM,...]
    unnamed x224 -> x236, local copies, waits for them, and re-layouts: 39.6 us -> 43.2 us
  transfers between devices with their start and end apart: 6 -> 9, of which waited for: 2 -> 2; matrix products, arithmetic and copies ran while one was open for 22% -> 23% of each run, Pallas kernels for 12% -> 12%
where the time goes in v4:
time: 783 us; the launch traced here: 773 us
  Pallas kernels  447 us (57%)
  matrix products  93 us (12%)
  local copies, waits for them, and re-layouts  77.5 us (10%)
  other arithmetic  77.4 us (10%)
  blocking collectives  30.8 us (4%)
  waiting for transfers between devices  25.3 us (3%)
  between operations  15.8 us (2%)
    pallas_call x1, Pallas kernels, gather_weights(): pl.pallas_call(functools.partial(gather_kernel, outer, kinds), out_shape=...  191 us
    pallas_call x1, Pallas kernels, reduce_weights(): pl.pallas_call(functools.partial(reduce_kernel, outer, kinds), out_shape=...  162 us
    unnamed x236, local copies, waits for them, and re-layouts  43.2 us
    dot_general x8, matrix products, product(): return jnp.dot(left, right, preferred_element_type=F32)  38.4 us
    pallas_call x1, Pallas kernels, plane_sum(): pl.pallas_call(plane_sum_kernel, out_shape=(shape, shape), in_specs=[VM,...  35 us
    dot_general x6, matrix products, product_nt(): lax.dot_general(left, right, (((1,), (1,)), ((), ())), preferred_element_...  29.5 us
    dot_general x8, matrix products, product_tn(): lax.dot_general(left, right, (((0,), (0,)), ((), ())), preferred_element_...  25 us
    pallas_call x1, Pallas kernels, plane_gather(): pl.pallas_call(plane_gather_kernel, out_shape=jax.ShapeDtypeStruct((2, 2,...  19.9 us
  transfers between devices with their start and end apart: 9, of which 2 were waited for; matrix products, arithmetic and copies ran while one was open for 23% of the time, Pallas kernels for 12%

profile of v4, /device:TPU:0, one launch (start us, length us, event | category | flops | bytes accessed | tf_op | source)
XLA Modules:
  0.0 772.9 jit_solution(7684896242510713337)
XLA Ops:
  20.4 190.9 %gather_weights.1 = (f32[4,2,2,8,128]{4,3,2,1,0:T(8,128)S(1)}, bf16[4,2,2,16,4608]{4,3,2,1,0:T(8,128)(2,1)S(1)}, bf16[4,2,2,96,2304]{4,3,2,1,0:T(8,128)(2,1)}, b...) custom-call(f32[8,128]{1,0:T(8,128)S(1)} %maximum_bitcast_fusion.1.r, ...), custom_call_target="tpu_custom_call" | custom-call | flops 99999997952 | bytes 100000000 | tf_op jit(solution)/shard_map/gather_weights/pallas_call | solution.py:460
  233.4 5.8 fusion.77
  271.5 4.7 pair_sum.4
  276.2 4.9 fusion.79
  308.5 5.3 shard_map.239
  317.6 4.7 pair_sum.5
  326.8 19.9 %plane_gather.1 = bf16[2,2,2,128,1536]{4,3,2,1,0:T(8,128)(2,1)} custom-call(bf16[128,1536]{1,0:T(8,128)(2,1)} %get-tuple-element.120.own_ref), custom_call_target="tpu_custom_call" | custom-call | flops 10000000000 | bytes 10000000 | tf_op jit(solution)/shard_map/plane_gather/pallas_call | solution.py:532
  346.8 7.0 fusion.81
  358.5 5.5 convolution_convert_fusion.2
  364.0 10.5 %fusion.6 = bf16[1024,1120]{0,1:T(8,128)(2,1)S(1)} fusion(f32[1024,1120]{0,1:T(8,128)} %copy-done.108, bf16[1024,1536]{1,0:T(8,128)(2,1)} %bitcast.247, bf16[1120,1536]{1,0:T(8,128)(2,1)} %all-gather.2.cloned.1.call-done), kind=kOutput, calls=%fused_computation.14 | convolution fusion | flops 3546152960 | bytes 13467648 | tf_op jit(solution)/shard_map/dot_general | solution.py:42
  374.5 6.1 convolution_convert_fusion.4
  380.6 5.1 convolution_convert_fusion.1
  385.8 9.7 %convolution_convert_fusion.5 = bf16[1024,1536]{1,0:T(8,128)(2,1)} fusion(bf16[1120,1536]{1,0:T(8,128)(2,1)} %all-gather.2.cloned.1.call-done, f32[1024,1120]{0,1:T(8,128)} %copy-done.108), kind=kOutput, calls=%fused_computation.17 | convolution fusion | flops 3535110144 | bytes 11173888 | tf_op jit(solution)/shard_map/dot_general | solution.py:34
  395.5 35.0 %plane_sum.1 = (f32[128,1536]{1,0:T(8,128)}, f32[128,1536]{1,0:T(8,128)}) custom-call(bf16[2,2,2,128,1536]{4,3,2,1,0:T(8,128)(2,1)} %bitcast.307, bf16[2,2,2,128,1536]{4,3,2,1,0:T(8,128)(2,1)} %bitcast.306), custom_call_target="tpu_custom_call" | custom-call | flops 10000000000 | bytes 10000000 | tf_op jit(solution)/shard_map/plane_sum/pallas_call | solution.py:591
  441.9 6.7 shard_map.240
  463.8 4.7 pair_sum.6
  477.5 5.1 shard_map.241
  487.7 5.8 copy.112
  503.3 6.2 fusion.83.part_ref
  509.5 4.7 pair_sum.7
  557.5 4.9 convolution_convert_fusion
  562.5 17.1 %collective-permute-done.4 = bf16[4,2,96,768]{3,2,1,0:T(8,128)(2,1)S(1)} collective-permute-done((bf16[4,2,96,768]{3,2,1,0:T(8,128)(2,1)S(1)}, bf16[4,2,96,768]{3,2,1,0:T(8,128)(2,1)S(1)}, u32[]{:S(2)}, u32[]{:S(2)}) %collective-permute-start.4) | collective-permute-done | bytes 1179680 | tf_op jit(solution)/shard_map/ppermute | solution.py:1156
  580.7 8.1 %collective-permute-done.5 = bf16[4,2,96,1536]{3,2,1,0:T(8,128)(2,1)S(1)} collective-permute-done((bf16[4,2,96,1536]{3,2,1,0:T(8,128)(2,1)}, bf16[4,2,96,1536]{3,2,1,0:T(8,128)(2,1)S(1)}, u32[]{:S(2)}, u32[]{:S(2)}) %collective-permute-start.5) | collective-permute-done | bytes 2359328 | tf_op jit(solution)/shard_map/ppermute | solution.py:1155
  590.5 161.8 %reduce_weights.1 = (f32[96,1536]{1,0:T(8,128)}, f32[96,3072]{1,0:T(8,128)}, f32[96,1536]{1,0:T(8,128)}, f32[96,1536]{1,0:T(8,128)}, f32[96,4608]{1,0:T(8,128)},...) custom-call(bf16[4,2,96,768]{3,2,1,0:T(8,128)(2,1)} %bitcast_add_fusion.1.refs_0_, ...), custom_call_target="tpu_custom_call" | custom-call | flops 99999997952 | bytes 100000000 | tf_op jit(solution)/shard_map/reduce_weights/pallas_call | solution.py:913
  (418 shorter events, 216.8 us)
Async XLA Ops:
  7.2 356.8 %all-gather.2.cloned.1.call-start = ((), (), s32[]{:S(2)}) async-start(), calls=%async_computation.4 | async-start | bytes 4300800 | tf_op jit(solution)/shard_map/all_gather | solution.py:957
  214.2 8.0 %copy-start.24 = (bf16[128,1536]{1,0:T(8,128)(2,1)S(1)}, bf16[128,1536]{1,0:T(8,128)(2,1)}, u32[]{:S(2)}) copy-start(bf16[128,1536]{1,0:T(8,128)(2,1)} %param.29) | copy-start | bytes 1179652
  215.5 14.2 %copy-start.13 = (bf16[128,1536]{1,0:T(8,128)(2,1)S(1)}, bf16[128,1536]{1,0:T(8,128)(2,1)}, u32[]{:S(2)}) copy-start(bf16[128,1536]{1,0:T(8,128)(2,1)} %param.15) | copy-start | bytes 1179652
  222.2 7.9 %copy-start.66 = (f32[2,1536]{1,0:T(2,128)}, f32[2,1536]{1,0:T(2,128)S(1)}, u32[]{:S(2)}) copy-start(f32[2,1536]{1,0:T(2,128)S(1)} %get-tuple-element.145) | copy-start | bytes 36868
  223.1 66.2 %collective-permute-start.2 = (bf16[128,1536]{1,0:T(8,128)(2,1)}, bf16[128,1536]{1,0:T(8,128)(2,1)}, u32[]{:S(2)}, u32[]{:S(2)}) collective-permute-start(bf16[128,1536]{1,0:T(8,128)(2,1)} %fusion.33), channel_id=1, source_target_pairs={{0,6},{2,4},{4,2},{6,0},{1,7},{3,5},{5,3},{7,1},{8,14},{10,12},{12... | collective-permute-start | bytes 1179656 | tf_op jit(solution)/shard_map/ppermute | solution.py:1075
  224.6 64.7 %collective-permute-start.1 = (bf16[128,1536]{1,0:T(8,128)(2,1)}, bf16[128,1536]{1,0:T(8,128)(2,1)}, u32[]{:S(2)}, u32[]{:S(2)}) collective-permute-start(bf16[128,1536]{1,0:T(8,128)(2,1)} %fusion.33), channel_id=1, source_target_pairs={{0,4},{4,0},{1,5},{5,1},{2,6},{6,2},{3,7},{7,3},{8,12},{12,8},{9,1... | collective-permute-start | bytes 1179656 | tf_op jit(solution)/shard_map/ppermute | solution.py:1074
  225.9 63.3 %collective-permute-start = (bf16[128,1536]{1,0:T(8,128)(2,1)}, bf16[128,1536]{1,0:T(8,128)(2,1)}, u32[]{:S(2)}, u32[]{:S(2)}) collective-permute-start(bf16[128,1536]{1,0:T(8,128)(2,1)} %fusion.33), channel_id=1, source_target_pairs={{0,2},{2,0},{1,3},{3,1},{4,6},{6,4},{5,7},{7,5},{8,10},{10,8},{9,1... | collective-permute-start | bytes 1179656 | tf_op jit(solution)/shard_map/ppermute | solution.py:1073
  226.6 363.9 %reduce-scatter.5.cloned.1.call-start = ((), (), s32[]{:S(2)}) async-start(), calls=%async_computation.5 | async-start | bytes 4300800 | tf_op jit(solution)/shard_map/reduce_scatter | solution.py:961
  297.5 56.3 %collective-permute-start.3 = (bf16[4,128,1536]{2,1,0:T(8,128)(2,1)}, bf16[4,128,1536]{2,1,0:T(8,128)(2,1)}, u32[]{:S(2)}, u32[]{:S(2)}) collective-permute-start(bf16[4,128,1536]{2,1,0:T(8,128)(2,1)} %get-tuple-element.129), channel_id=1, source_target_pairs={{0,1},{1,0},{2,3},{3,2},{4,5},{5,4},{6,7},{7,6},{8,9},{9,8},{10,11... | collective-permute-start | bytes 4718600 | tf_op jit(solution)/shard_map/ppermute | solution.py:1093
  346.8 7.0 copy-start.28
  364.0 10.5 %copy-start.105 = (bf16[4,4,96,1120]{3,2,1,0:T(8,128)(2,1)S(1)}, bf16[4,4,96,1120]{3,2,1,0:T(8,128)(2,1)}, u32[]{:S(2)}) copy-start(bf16[4,4,96,1120]{3,2,1,0:T(8,128)(2,1)} %get-tuple-element.64) | copy-start | bytes 10321924
  374.5 6.1 copy-start.106
  385.8 204.7 %reduce-scatter.7.cloned.1.call-start = ((), (), s32[]{:S(2)}) async-start(), calls=%async_computation.6 | async-start | bytes 4423680 | tf_op jit(solution)/shard_map/reduce_scatter | solution.py:961
  430.5 6.0 copy-start.25
  432.8 7.6 copy-start.52
  487.7 5.8 copy-start.16
  509.5 6.7 copy-start.93
  518.2 10.3 %copy-start.18 = (f32[512,1536]{1,0:T(8,128)S(1)}, f32[512,1536]{1,0:T(8,128)}, u32[]{:S(2)}) copy-start(f32[512,1536]{1,0:T(8,128)} %copy-done.17) | copy-start | bytes 9437188
  535.2 15.3 %copy-start.37 = (bf16[256,768]{1,0:T(8,128)(2,1)S(1)}, bf16[256,768]{1,0:T(8,128)(2,1)}, u32[]{:S(2)}) copy-start(bf16[256,768]{1,0:T(8,128)(2,1)} %copy-done.36) | copy-start | bytes 1179652
  535.2 15.3 %copy-start.41 = (bf16[256,1536]{1,0:T(8,128)(2,1)S(1)}, bf16[256,1536]{1,0:T(8,128)(2,1)}, u32[]{:S(2)}) copy-start(bf16[256,1536]{1,0:T(8,128)(2,1)} %copy-done.40) | copy-start | bytes 2359300
  535.2 53.7 %collective-permute-start.5 = (bf16[4,2,96,1536]{3,2,1,0:T(8,128)(2,1)}, bf16[4,2,96,1536]{3,2,1,0:T(8,128)(2,1)S(1)}, u32[]{:S(2)}, u32[]{:S(2)}) collective-permute-start(bf16[4,2,96,1536]{3,2,1,0:T(8,128)(2,1)} %dynamic-slice_bitcast_fusion), channel_id=1, source_target_pairs={{0,4},{4,0},{1,5},{5,1},{2,6},{6,2},{3,7},{7,3},{8,12},{12,8},{9,1... | collective-permute-start | bytes 7077896 | tf_op jit(solution)/shard_map/ppermute | solution.py:1155
  551.5 28.1 %collective-permute-start.4 = (bf16[4,2,96,768]{3,2,1,0:T(8,128)(2,1)S(1)}, bf16[4,2,96,768]{3,2,1,0:T(8,128)(2,1)S(1)}, u32[]{:S(2)}, u32[]{:S(2)}) collective-permute-start(bf16[4,2,96,768]{3,2,1,0:T(8,128)(2,1)S(1)} %dynamic-slice_bitcast_fusion.1), channel_id=1, source_target_pairs={{0,2},{2,0},{1,3},{3,1},{4,6},{6,4},{5,7},{7,5},{8,10},{10,8},{9,1... | collective-permute-start | bytes 3538952 | tf_op jit(solution)/shard_map/ppermute | solution.py:1156
  555.3 33.6 %slice-start = ((s8[4718592]{0:T(1024)(128)(4,1)}), s8[4194304]{0:T(1024)(128)(4,1)S(1)}, s32[]{:S(2)}) async-start(s8[4718592]{0:T(1024)(128)(4,1)} %bitcast.238), calls=%async_computation.7 | async-start | bytes 8388608
  557.5 31.4 %slice-start.1 = ((s8[4718592]{0:T(1024)(128)(4,1)}), s8[524288]{0:T(1024)(128)(4,1)S(1)}, s32[]{:S(2)}) async-start(s8[4718592]{0:T(1024)(128)(4,1)} %bitcast.238), calls=%async_computation.8 | async-start | bytes 1048576
  (96 other events, 270.2 us)
Sparse Core Ops, SparseCore 0:
  226.7 68.4 all-gather.1
  385.9 65.1 reduce-scatter.4
  501.0 66.6 reduce-scatter.6

commit v5 on v4

--- a/solution.py
+++ b/solution.py
@@ -84,24 +84,6 @@
     return (jnp.cos(angles), jnp.sin(angles))
 
 
-def rotate(values, cosine, sine):
-    row_count = values.shape[0]
-    shaped = values.reshape(row_count, -1, HD)
-    half_dim = HD // 2
-    first_half = shaped[:, :, :half_dim]
-    second_half = shaped[:, :, half_dim:]
-    cos_rows = cosine[:, None, :]
-    sin_rows = sine[:, None, :]
-    turned = jnp.concatenate(
-        [
-            first_half * cos_rows - second_half * sin_rows,
-            second_half * cos_rows + first_half * sin_rows,
-        ],
-        axis=2,
-    )
-    return turned.reshape(row_count, -1)
-
-
 def modulated(residual, shift, scale):
     frames = shift.shape[0]
     normed = layer_norm(residual).reshape(frames, -1, residual.shape[1])
@@ -117,83 +99,9 @@
     return jnp.sum(values.reshape(frames, -1, values.shape[1]), axis=1)
 
 
-def attend_forward_kernel(live_ref, q_ref, k_ref, v_ref, out_ref, lse_ref):
-    rows, keys = q_ref.shape[0], k_ref.shape[0]
-    spot = lax.broadcasted_iota(jnp.int32, (rows, keys), 1)
-    allowed = spot < live_ref[0]
-    for head in range(q_ref.shape[1] // HD):
-        part = slice(head * HD, (head + 1) * HD)
-        scores = jnp.where(allowed, product_nt(q_ref[:, part], k_ref[:, part]) * SCALE, NEGATIVE)
-        row_max = jnp.max(scores, axis=1, keepdims=True)
-        log_total = row_max + jnp.log(jnp.sum(jnp.exp(scores - row_max), axis=1, keepdims=True))
-        weights = jnp.exp(scores - log_total).astype(BF)
-        out_ref[:, part] = product(weights, v_ref[:, part]).astype(BF)
-        lse_ref[:, part] = jnp.broadcast_to(log_total, (rows, HD))
-
-
-def attend_backward_kernel(
-    live_ref, q_ref, k_ref, v_ref, lse_ref, do_ref, dq_ref, dk_ref, dv_ref
-):
-    rows, keys = q_ref.shape[0], k_ref.shape[0]
-    spot = lax.broadcasted_iota(jnp.int32, (rows, keys), 1)
-    allowed = spot < live_ref[0]
-    for head in range(q_ref.shape[1] // HD):
-        part = slice(head * HD, (head + 1) * HD)
-        query, key, value, grad = q_ref[:, part], k_ref[:, part], v_ref[:, part], do_ref[:, part]
-        scores = jnp.where(allowed, product_nt(query, key) * SCALE, NEGATIVE)
-        weights = jnp.exp(scores - lse_ref[:, head * HD : head * HD + 1])
-        grad_weights = product_nt(grad, value)
-        delta = jnp.sum(weights * grad_weights, axis=1, keepdims=True)
-        grad_scores = (weights * (grad_weights - delta)).astype(BF)
-        dq_ref[:, part] = (product(grad_scores, key) * SCALE).astype(BF)
-        dk_ref[:, part] = (product_tn(grad_scores, query) * SCALE).astype(BF)
-        dv_ref[:, part] = product_tn(weights.astype(BF), grad).astype(BF)
-
-
 VM = pl.BlockSpec(memory_space=pltpu.VMEM)
 SM = pl.BlockSpec(memory_space=pltpu.SMEM)
 ANY = pl.BlockSpec(memory_space=pl.ANY)
-
-
-def attend_forward(live, query, key, value):
-    rows, width = query.shape
-    keys = key.shape[0]
-    heads = width // HD
-    return pl.pallas_call(
-        attend_forward_kernel,
-        out_shape=(
-            jax.ShapeDtypeStruct((rows, width), BF),
-            jax.ShapeDtypeStruct((rows, width), F32),
-        ),
-        in_specs=[SM, VM, VM, VM],
-        out_specs=(VM, VM),
-        cost_estimate=pl.CostEstimate(
-            flops=4 * rows * keys * width,
-            bytes_accessed=8 * rows * width + 4 * keys * width,
-            transcendentals=2 * rows * keys * heads,
-        ),
-    )(live, query, key, value)
-
-
-def attend_backward(live, query, key, value, lse, grad):
-    rows, width = query.shape
-    keys = key.shape[0]
-    heads = width // HD
-    return pl.pallas_call(
-        attend_backward_kernel,
-        out_shape=(
-            jax.ShapeDtypeStruct((rows, width), BF),
-            jax.ShapeDtypeStruct((keys, width), BF),
-            jax.ShapeDtypeStruct((keys, width), BF),
-        ),
-        in_specs=[SM, VM, VM, VM, VM, VM],
-        out_specs=(VM, VM, VM),
-        cost_estimate=pl.CostEstimate(
-            flops=10 * rows * keys * width,
-            bytes_accessed=10 * rows * width + 8 * keys * width,
-            transcendentals=rows * keys * heads,
-        ),
-    )(live, query, key, value, lse, grad)
 
 
 def row_add(target, left, right, rows):
@@ -277,6 +185,179 @@
     pl.semaphore_wait(barrier, count)
 
 
+def raw_views(joint, refs):
+    if joint:
+        rows_ref, rest = refs[0], refs[1:]
+        width = rows_ref.shape[1] // 3
+        spans = ((rows_ref, 0), (rows_ref, width), (rows_ref, 2 * width))
+    else:
+        rows_ref, keys_ref, rest = refs[0], refs[1], refs[2:]
+        width = rows_ref.shape[1]
+        spans = ((rows_ref, 0), (keys_ref, 0), (keys_ref, width))
+
+    def view(which, head):
+        ref, base = spans[which]
+        return ref[:, base + head * HD : base + (head + 1) * HD]
+
+    return view, width, rest
+
+
+def turned(values, cos_ref, sin_ref, sign):
+    return values * cos_ref[...] + sign * (pltpu.roll(values, HD // 2, 1) * sin_ref[...])
+
+
+def attend_forward_kernel(joint, rotary, live_ref, *refs):
+    view, width, refs = raw_views(joint, refs)
+    gain_ref, cos_ref, sin_ref, refs = *refs[:3], refs[3:]
+    out_ref, lse_ref, query_ref, key_ref, inv_q_ref, inv_k_ref, refs = *refs[:6], refs[6:]
+    q_sum, k_sum, q_peer, k_peer, send, recv = refs
+    heads = width // HD
+    core_peer = {"sp": 1 - lax.axis_index("sp")}
+    fly = Flights()
+    greet((core_peer,))
+    for which, own, peer in ((0, q_sum, q_peer), (1, k_sum, k_peer)):
+        total = view(which, 0) * view(which, 0)
+        for head in range(1, heads):
+            total = total + view(which, head) * view(which, head)
+        own[...] = jnp.broadcast_to(jnp.sum(total, axis=1, keepdims=True), own.shape)
+        fly.send(own, peer, send.at[which], recv.at[which], core_peer)
+    for which, own, peer, kept in ((0, q_sum, q_peer, inv_q_ref), (1, k_sum, k_peer, inv_k_ref)):
+        landed(peer, recv.at[which], core_peer)
+        kept[...] = lax.rsqrt((own[...] + peer[...]) / D + EPSILON)
+    rows, keys = query_ref.shape[0], key_ref.shape[0]
+    spot = lax.broadcasted_iota(jnp.int32, (rows, keys), 1)
+    allowed = spot < live_ref[0]
+    for head in range(heads):
+        part = slice(head * HD, (head + 1) * HD)
+        query = view(0, head) * inv_q_ref[...] * gain_ref[0:1, part]
+        key = view(1, head) * inv_k_ref[...] * gain_ref[1:2, part]
+        if rotary:
+            query, key = turned(query, cos_ref, sin_ref, 1.0), turned(key, cos_ref, sin_ref, 1.0)
+        query, key, value = query.astype(BF), key.astype(BF), view(2, head).astype(BF)
+        query_ref[:, part], key_ref[:, part] = query, key
+        scores = jnp.where(allowed, product_nt(query, key) * SCALE, NEGATIVE)
+        row_max = jnp.max(scores, axis=1, keepdims=True)
+        log_total = row_max + jnp.log(jnp.sum(jnp.exp(scores - row_max), axis=1, keepdims=True))
+        weights = jnp.exp(scores - log_total).astype(BF)
+        out_ref[:, part] = product(weights, value).astype(BF)
+        lse_ref[:, part] = jnp.broadcast_to(log_total, (rows, HD))
+    fly.drain()
+
+
+def attend_backward_kernel(joint, rotary, live_ref, *refs):
+    view, width, refs = raw_views(joint, refs)
+    gain_ref, cos_ref, sin_ref, refs = *refs[:3], refs[3:]
+    query_ref, key_ref, lse_ref, inv_q_ref, inv_k_ref, do_ref, refs = *refs[:6], refs[6:]
+    if joint:
+        grad_refs, refs = ((refs[0], 0), (refs[0], width), (refs[0], 2 * width)), refs[1:]
+    else:
+        grad_refs, refs = ((refs[0], 0), (refs[1], 0), (refs[1], width)), refs[2:]
+    gain_out, scaled_q, scaled_k, q_dot, k_dot, q_peer, k_peer, send, recv = refs
+    heads = width // HD
+    core_peer = {"sp": 1 - lax.axis_index("sp")}
+    fly = Flights()
+    greet((core_peer,))
+    rows, keys = query_ref.shape[0], key_ref.shape[0]
+    spot = lax.broadcasted_iota(jnp.int32, (rows, keys), 1)
+    allowed = spot < live_ref[0]
+    dots = [None, None]
+    gain_out[...] = jnp.zeros_like(gain_out)
+    for head in range(heads):
+        part = slice(head * HD, (head + 1) * HD)
+        query, key, grad = query_ref[:, part], key_ref[:, part], do_ref[:, part]
+        value = view(2, head).astype(BF)
+        scores = jnp.where(allowed, product_nt(query, key) * SCALE, NEGATIVE)
+        weights = jnp.exp(scores - lse_ref[:, head * HD : head * HD + 1])
+        grad_weights = product_nt(grad, value)
+        delta = jnp.sum(weights * grad_weights, axis=1, keepdims=True)
+        grad_scores = (weights * (grad_weights - delta)).astype(BF)
+        grad_query = (product(grad_scores, key) * SCALE).astype(BF).astype(F32)
+        grad_key = (product_tn(grad_scores, query) * SCALE).astype(BF).astype(F32)
+        grad_value = product_tn(weights.astype(BF), grad).astype(BF)
+        ref, base = grad_refs[2]
+        ref[:, base + head * HD : base + (head + 1) * HD] = grad_value
+        for which, grad_rows, inverse, held in ((0, grad_query, inv_q_ref, scaled_q), (1, grad_key, inv_k_ref, scaled_k)):
+            if rotary:
+                grad_rows = turned(grad_rows, cos_ref, sin_ref, -1.0)
+            raw = view(which, head)
+            gain_out[which : which + 1, part] = jnp.sum(grad_rows * raw * inverse[...], axis=0, keepdims=True)
+            scaled = grad_rows * gain_ref[which : which + 1, part]
+            held[:, part] = scaled
+            dots[which] = scaled * raw if head == 0 else dots[which] + scaled * raw
+    for which, own, peer in ((0, q_dot, q_peer), (1, k_dot, k_peer)):
+        own[...] = jnp.broadcast_to(jnp.sum(dots[which], axis=1, keepdims=True), own.shape)
+        fly.send(own, peer, send.at[which], recv.at[which], core_peer)
+    for which, own, peer, inverse, held in (
+        (0, q_dot, q_peer, inv_q_ref, scaled_q),
+        (1, k_dot, k_peer, inv_k_ref, scaled_k),
+    ):
+        landed(peer, recv.at[which], core_peer)
+        column = inverse[...]
+        slope = column * column * column * ((own[...] + peer[...]) / D)
+        ref, base = grad_refs[which]
+        for head in range(heads):
+            part = slice(head * HD, (head + 1) * HD)
+            out = held[:, part] * column - view(which, head) * slope
+            ref[:, base + head * HD : base + (head + 1) * HD] = out.astype(BF)
+    fly.drain()
+
+
+def attend_call(kernel, joint, rotary, number, live, raws, others, shapes, scratch, flops, exps):
+    dma = pltpu.SemaphoreType.DMA
+    arrays = [*raws, *others]
+    moved = sum(v.size * v.dtype.itemsize for v in [*arrays, *shapes])
+    return pl.pallas_call(
+        functools.partial(kernel, joint, rotary),
+        out_shape=shapes,
+        in_specs=[SM] + [VM] * len(arrays),
+        out_specs=[VM] * len(shapes),
+        scratch_shapes=[*scratch, dma((2,)), dma((2,))],
+        compiler_params=pltpu.CompilerParams(collective_id=number, has_side_effects=True),
+        cost_estimate=pl.CostEstimate(flops=flops, bytes_accessed=moved, transcendentals=exps),
+    )(live, *arrays)
+
+
+def attend_sizes(raws):
+    joint = len(raws) == 1
+    rows, keys = raws[0].shape[0], raws[-1].shape[0]
+    return joint, rows, keys, raws[0].shape[1] // 3 if joint else raws[0].shape[1]
+
+
+def attend_forward(live, raws, gains, cosine, sine, rotary, number):
+    joint, rows, keys, width = attend_sizes(raws)
+    shape = jax.ShapeDtypeStruct
+    shapes = [
+        shape((rows, width), BF),
+        shape((rows, width), F32),
+        shape((rows, width), BF),
+        shape((keys, width), BF),
+        shape((rows, HD), F32),
+        shape((keys, HD), F32),
+    ]
+    scratch = [pltpu.VMEM((n, HD), F32) for n in (rows, keys, rows, keys)]
+    work = rows * keys * width
+    return attend_call(
+        attend_forward_kernel, joint, rotary, number, live, raws, [gains, cosine, sine],
+        shapes, scratch, 4 * work, 2 * work // HD,
+    )
+
+
+def attend_backward(live, raws, gains, cosine, sine, rotary, number, saved, grad):
+    joint, rows, keys, width = attend_sizes(raws)
+    shape = jax.ShapeDtypeStruct
+    shapes = [shape(raw.shape, BF) for raw in raws] + [shape((8, width), F32)]
+    scratch = [pltpu.VMEM((rows, width), F32), pltpu.VMEM((keys, width), F32)]
+    scratch += [pltpu.VMEM((n, HD), F32) for n in (rows, keys, rows, keys)]
+    work = rows * keys * width
+    return attend_call(
+        attend_backward_kernel, joint, rotary, number, live, raws,
+        [gains, cosine, sine, *saved, grad], shapes, scratch, 10 * work, work // HD,
+    )
+
+
+ALL_CHIPS, KEEP, HALF_X, HALF_Y = range(4)
+
+
 def gather_kernel(outer, kinds, *refs):
     full = len(kinds)
     ins, refs = refs[:full], refs[full:]
@@ -284,7 +365,8 @@
     outs, refs = list(refs[:full]), refs[full:]
     up_out, text_out, refs = refs[0], refs[1], refs[2:]
     own, refs = refs[:full], refs[full:]
-    halves = [i for i, kind in enumerate(kinds) if kind[1]]
+    halves = [i for i, kind in enumerate(kinds) if kind[1] == KEEP]
+    form = [kind[1] for kind in kinds]
     whole, refs = refs[: len(halves)], refs[len(halves) :]
     up_own, local_sem, zs, zr, s1, r1, s2, r2, a_s, a_r, f_s, f_r, f_l, t_s = refs
     z, y, x = (lax.axis_index(name) for name in FS)
@@ -312,8 +394,15 @@
             column = pl.multiple_of((2 * part + core) * width, width)
             own[i][:, part * width : (part + 1) * width] = ins[i][:, pl.ds(column, width)]
 
+    def spot(i, slot, ty, tx):
+        if form[i] == HALF_X:
+            return outs[i].at[slot, tx]
+        if form[i] == HALF_Y:
+            return outs[i].at[slot, ty]
+        return outs[i].at[slot, ty, tx]
+
     def shard(i, slot):
-        return outs[i].at[slot, y, x] if i < full else up_out.at[slot]
+        return spot(i, slot, y, x) if i < full else up_out.at[slot]
 
     def z_send(i, way, hop, source=None):
         if hop > outer - 2:
@@ -347,13 +436,19 @@
         return first, second
 
     def xy_own(i, slot, when=None, source=None):
+        mine = spot(i, slot, y, x)
+        source = mine if source is None else source
+        if form[i] in (HALF_X, HALF_Y):
+            peer = x_peer if form[i] == HALF_X else y_peer
+            fly.send(source, mine, s1.at[i, slot], r1.at[i, slot], peer, when)
+            return
         first, second = turns(i, slot)
-        mine = outs[i].at[slot, y, x]
-        source = mine if source is None else source
         fly.send(source, mine, s1.at[i, slot], r1.at[i, slot], {"yb": first[0], "xc": first[1]}, when)
         fly.send(source, mine, s2.at[i, slot, 0], r2.at[i, slot, 0], {"yb": second[0], "xc": second[1]}, when)
 
     def xy_pass(i, slot, when=None):
+        if form[i] in (HALF_X, HALF_Y):
+            return
         first, second = turns(i, slot)
         theirs = outs[i].at[slot, first[0], first[1]]
 
@@ -367,6 +462,12 @@
         fly.send(theirs, theirs, s2.at[i, slot, 1], r2.at[i, slot, 1], {"yb": second[0], "xc": second[1]}, when)
 
     def xy_end(i, slot):
+        if form[i] == HALF_X:
+            landed(spot(i, slot, y, 1 - x), r1.at[i, slot], x_peer)
+            return
+        if form[i] == HALF_Y:
+            landed(spot(i, slot, 1 - y, x), r1.at[i, slot], y_peer)
+            return
         _, second = turns(i, slot)
         device = {"yb": second[0], "xc": second[1]}
         landed(outs[i].at[slot, second[0], second[1]], r2.at[i, slot, 0], device)
@@ -376,7 +477,7 @@
         for way in range(2):
             z_send(i, way, 0, own[i])
         xy_own(i, z, None, own[i])
-    locals_ = [fly.local(own[i], outs[i].at[z, y, x], local_sem.at[i]) for i in range(full)]
+    locals_ = [fly.local(own[i], spot(i, z, y, x), local_sem.at[i]) for i in range(full)]
 
     fly.send(text_ref, text_out.at[core], t_s.at[0], t_s.at[1], core_peer)
     locals_.append(fly.local(text_ref, text_out.at[core], t_s.at[2]))
@@ -441,11 +542,13 @@
 
 def gather_weights(outer, kinds, arrays, mlp, text):
     shapes, own, whole = [], [], []
-    for (parts, keep), array in zip(kinds, arrays, strict=True):
+    for (parts, form), array in zip(kinds, arrays, strict=True):
         rows, width = array.shape
         half = width // 2 if parts else width
         own.append(pltpu.VMEM((rows, half), array.dtype))
-        if keep:
+        if form in (HALF_X, HALF_Y):
+            shapes.append(jax.ShapeDtypeStruct((outer, 2, rows, half), array.dtype))
+        elif form == KEEP:
             whole.append(pltpu.VMEM((outer, 2, 2, rows, half), array.dtype))
             shapes.append(jax.ShapeDtypeStruct((outer // 2, 2, 2, rows, width), array.dtype))
         else:
@@ -486,7 +589,7 @@
         cost_estimate=pl.CostEstimate(flops=10**11, bytes_accessed=10**8, transcendentals=0),
         name="gather_weights",
     )(*arrays, mlp, text)
-    return [value.reshape(-1, value.shape[-1]) for value in results]
+    return [value.reshape(-1, value.shape[-1]) if value.ndim != 4 or i >= nf else value for i, value in enumerate(results)]
 
 
 def plane_gather_kernel(own_ref, out_ref, local_sem, send, recv):
@@ -965,24 +1068,6 @@
     return lax.all_to_all(value, "sp", split_axis=split_axis, concat_axis=concat_axis, tiled=True)
 
 
-def rms_scale(total):
-    return lax.rsqrt(total / D + EPSILON)
-
-
-def square_sum(values):
-    return jnp.sum(values * values, axis=1)
-
-
-def rms_back(values, gain, grad):
-    scaled = grad * gain
-    return scaled, jnp.sum(scaled * values, axis=1)
-
-
-def rms_finish(values, inverse, scaled, total):
-    column = inverse[:, None]
-    return scaled * column - values * (column * column * column) * (total / D)[:, None]
-
-
 def body(
     tokens,
     text,
@@ -1027,12 +1112,12 @@
     ).reshape(small_rows, small_width)
     gathered = gather_weights(
         outer,
-        ((0, False), (1, False), (3, False), (1, True), (2, False), (1, False), (1, True)),
+        ((0, ALL_CHIPS), (1, ALL_CHIPS), (3, ALL_CHIPS), (1, KEEP), (2, HALF_X), (1, HALF_Y), (1, KEEP)),
         [small, *(w[0] for w in (mod_weight, self_in, self_out, cross_kv, cross_q, cross_out))],
         mlp_in[0],
         text,
     )
-    small_all, mod_matrix, self_proj, self_back, cross_kvproj, cross_qproj, cross_back = gathered[:7]
+    small_all, mod_matrix, self_proj, self_back, kv_half, q_half, cross_back = gathered[:7]
     up_matrix, text_all = gathered[7:]
     hid = mlp_out.shape[1] // 2
     down_part = lax.dynamic_slice_in_dim(mlp_out[0], core * hid, hid, 0)
@@ -1057,6 +1142,7 @@
         jnp.repeat(clip_pos, FRAME_TOK),
         jnp.tile(jnp.arange(FRAME_TOK, dtype=jnp.int32), group_frames),
     )
+    cosine, sine = jnp.concatenate([cosine, cosine], axis=1), jnp.concatenate([-sine, sine], axis=1)
     sinus = sinus_features(timestep[0]).astype(BF)
 
     mod_half = product(sinus, mod_matrix)
@@ -1068,6 +1154,9 @@
 
     grad_branch = frame_scaled(cotangent.astype(F32), gate_two).astype(BF)
     exchange = [(0, 1), (1, 0)]
+    place_y, place_x = lax.axis_index("yb"), lax.axis_index("xc")
+    kv_other = lax.ppermute(kv_half, "yb", exchange)
+    q_other = lax.ppermute(q_half, "xc", exchange)
     beside = [
         grad_branch,
         lax.ppermute(grad_branch, "xc", exchange),
@@ -1079,32 +1168,31 @@
     attn_float, back_attn_input = jax.vjp(modulated, residual, shift_one, scale_one)
     attn_input = gather(attn_float.astype(BF), "sp")
     joined = product(attn_input, self_proj)
-    raw_q, raw_k, raw_v = joined[:, :half], joined[:, half : 2 * half], joined[:, 2 * half :]
-    totals = lax.psum(jnp.stack([square_sum(raw_q), square_sum(raw_k)]), "sp")
-    inv_q, inv_k = rms_scale(totals[0]), rms_scale(totals[1])
-    query = rotate(raw_q * inv_q[:, None] * gain_own[0], cosine, sine).astype(BF)
-    key = rotate(raw_k * inv_k[:, None] * gain_own[1], cosine, sine).astype(BF)
-    value = raw_v.astype(BF)
-    self_mixed, self_lse = attend_forward(live_keys, query, key, value)
+    self_mixed, self_lse, *self_kept = attend_forward(
+        live_keys, [joined], gain_own[:2], cosine, sine, True, 5
+    )
     self_branch = pair_sum(product(self_mixed, self_back))
     residual = residual + frame_scaled(self_branch, gate_one)
+
+    def beside_own(own, other, place, axis):
+        pair = jnp.where(place == 0, jnp.stack([own, other], axis), jnp.stack([other, own], axis))
+        return pair.reshape(-1, own.shape[-1])
+
+    cross_kvproj = beside_own(kv_half, kv_other, place_y, 1)
+    cross_qproj = beside_own(q_half, q_other, place_x, 2)
+    text_raw = product(text_all, cross_kvproj)
+    cross_float, back_cross_norm = jax.vjp(layer_norm, residual)
+    cross_input = gather(cross_float.astype(BF), "sp")
+    cross_raw = product(cross_input, cross_qproj)
+    cross_mixed, cross_lse, *cross_kept = attend_forward(
+        all_keys, [cross_raw, text_raw], gain_own[2:], cosine, sine, False, 6
+    )
+    cross_branch = pair_sum(product(cross_mixed, cross_back))
+    residual = residual + cross_branch
     residual, *beside = lax.optimization_barrier((residual, *beside))
     beside = jnp.stack(beside)
     grad_branch_all = jnp.stack([beside, lax.ppermute(beside, "sp", exchange)], axis=1).reshape(-1, D)
 
-    text_raw = product(text_all, cross_kvproj)
-    raw_ck, raw_cv = text_raw[:, :half], text_raw[:, half:]
-    inv_ck = rms_scale(lax.psum(square_sum(raw_ck)[None], "sp")[0])
-    cross_key = (raw_ck * inv_ck[:, None] * gain_own[3]).astype(BF)
-    cross_value = raw_cv.astype(BF)
-
-    cross_float, back_cross_norm = jax.vjp(layer_norm, residual)
-    cross_input = gather(cross_float.astype(BF), "sp")
-    cross_raw = product(cross_input, cross_qproj)
-    inv_cq = rms_scale(lax.psum(square_sum(cross_raw)[None], "sp")[0])
-    cross_query = (cross_raw * inv_cq[:, None] * gain_own[2]).astype(BF)
-    cross_mixed, cross_lse = attend_forward(all_keys, cross_query, cross_key, cross_value)
-    residual = residual + pair_sum(product(cross_mixed, cross_back))
 
     mlp_float, back_mlp_input = jax.vjp(modulated, residual, shift_two, scale_two)
     mlp_input = plane_gather(mlp_float.astype(BF))
@@ -1133,23 +1221,12 @@
     grad_low = gather(grad_rows.astype(BF), "sp")
     grad_cross_back = product_tn(cross_mixed, grad_low).astype(BF)
     grad_cross_mixed = product_nt(grad_low, cross_back).astype(BF)
-    grad_cq, grad_ck, grad_cv = attend_backward(
-        all_keys, cross_query, cross_key, cross_value, cross_lse, grad_cross_mixed
-    )
-    grad_cq, grad_ck = grad_cq.astype(F32), grad_ck.astype(F32)
-    grad_gain_two = jnp.sum(grad_cq * cross_raw * inv_cq[:, None], axis=0)
-    grad_gain_three = jnp.sum(grad_ck * raw_ck * inv_ck[:, None], axis=0)
-    scaled_cq, dots_cq = rms_back(cross_raw, gain_own[2], grad_cq)
-    scaled_ck, dots_ck = rms_back(raw_ck, gain_own[3], grad_ck)
-    dots = lax.psum(jnp.concatenate([dots_cq, dots_ck])[None], "sp")[0]
-    dots_cq, dots_ck = dots[: dots_cq.shape[0]], dots[dots_cq.shape[0] :]
-    grad_cross_low = rms_finish(cross_raw, inv_cq, scaled_cq, dots_cq).astype(BF)
-    grad_text_low = jnp.concatenate(
-        [rms_finish(raw_ck, inv_ck, scaled_ck, dots_ck).astype(BF), grad_cv], axis=1
+    cross_saved = [*cross_kept[:2], cross_lse, *cross_kept[2:]]
+    grad_cross_low, grad_text_low, gains_cross = attend_backward(
+        all_keys, [cross_raw, text_raw], gain_own[2:], cosine, sine, False, 7, cross_saved, grad_cross_mixed
     )
     grad_cross_qproj = product_tn(cross_input, grad_cross_low).astype(BF)
     grad_cross_kvproj = product_tn(text_all, grad_text_low).astype(BF)
-    place_y, place_x = lax.axis_index("yb"), lax.axis_index("xc")
     kv_parts = grad_cross_kvproj.reshape(outer, 2, 2, in_rows, -1)
     q_parts = grad_cross_qproj.reshape(outer, 2, 2, in_rows, -1)
     kv_sent = lax.ppermute(lax.dynamic_index_in_dim(kv_parts, 1 - place_y, 1, False), "yb", exchange)
@@ -1161,23 +1238,9 @@
     grad_self_low = gather(frame_scaled(grad_rows, gate_one).astype(BF), "sp")
     grad_self_back = product_tn(self_mixed, grad_self_low).astype(BF)
     grad_self_mixed = product_nt(grad_self_low, self_back).astype(BF)
-    grad_q, grad_k, grad_v = attend_backward(
-        live_keys, query, key, value, self_lse, grad_self_mixed
-    )
-    grad_q = rotate(grad_q.astype(F32), cosine, -sine)
-    grad_k = rotate(grad_k.astype(F32), cosine, -sine)
-    grad_gain_zero = jnp.sum(grad_q * raw_q * inv_q[:, None], axis=0)
-    grad_gain_one = jnp.sum(grad_k * raw_k * inv_k[:, None], axis=0)
-    scaled_q, dots_q = rms_back(raw_q, gain_own[0], grad_q)
-    scaled_k, dots_k = rms_back(raw_k, gain_own[1], grad_k)
-    dots = lax.psum(jnp.stack([dots_q, dots_k]), "sp")
-    grad_joined_low = jnp.concatenate(
-        [
-            rms_finish(raw_q, inv_q, scaled_q, dots[0]).astype(BF),
-            rms_finish(raw_k, inv_k, scaled_k, dots[1]).astype(BF),
-            grad_v,
-        ],
-        axis=1,
+    self_saved = [*self_kept[:2], self_lse, *self_kept[2:]]
+    grad_joined_low, gains_self = attend_backward(
+        live_keys, [joined], gain_own[:2], cosine, sine, True, 8, self_saved, grad_self_mixed
     )
     grad_self_proj = product_tn(attn_input, grad_joined_low).astype(BF)
     grad_attn_input = pair_sum(product_nt(grad_joined_low, self_proj))
@@ -1189,7 +1252,7 @@
         axis=1,
     )
     grad_mod_half = swap(grad_modulation, 1, 0)
-    grad_gains = jnp.stack([grad_gain_zero, grad_gain_one, grad_gain_two, grad_gain_three])
+    grad_gains = jnp.concatenate([gains_self[:2], gains_cross[:2]])
     both = jnp.arange(2)[None, :, None] == core
     grad_gains = jnp.where(both, grad_gains[:, None, :], 0.0).reshape(4, shards, gain_len)
     grad_small = jnp.concatenate(

time: 783 us -> 747 us (0.954)
  other arithmetic: 77.4 us -> 54.9 us
  Pallas kernels: 447 us -> 431 us
  blocking collectives: 30.8 us -> 20.4 us
  local copies, waits for them, and re-layouts: 77.5 us -> 68.8 us
  waiting for transfers between devices: 25.3 us -> 33.7 us
    pallas_call x1, Pallas kernels: 191 us -> 159 us  [gather_weights(): pl.pallas_call(functools.partial(gather_kernel, outer, kinds), out_shape=...]
    pallas_call x4, Pallas kernels: 20.7 us -> 34.4 us  [attend_call(): pl.pallas_call(functools.partial(kernel, joint, rotary), out_shape=shapes...]
    psum x4 -> x0, blocking collectives: 12.5 us -> none  [the longest x1 3.32 us: body(): dots = lax.psum(jnp.stack([dots_q, dots_k]), 'sp')]
    ppermute x0 -> x2, waiting for transfers between devices: none -> 11.1 us  [the longest x1 11.1 us: body(): kv_other = lax.ppermute(kv_half, 'yb', exchange)]
    ppermute x1, waiting for transfers between devices: 17.1 us -> 6.74 us  [body(): lax.ppermute(lax.dynamic_index_in_dim(q_parts, 1 - place_x, 2, False), 'x...]
    reduce_sum x5 -> x0, other arithmetic: 10.2 us -> none  [the longest x2 3.06 us: square_sum(): return jnp.sum(values * values, axis=1)]
    unnamed x236 -> x188, local copies, waits for them, and re-layouts: 43.2 us -> 36.5 us
  transfers between devices with their start and end apart: 9 -> 11, of which waited for: 2 -> 3; matrix products, arithmetic and copies ran while one was open for 23% -> 21% of each run, Pallas kernels for 12% -> 15%
where the time goes in v5:
time: 747 us; the launch traced here: 734 us
  Pallas kernels  431 us (58%)
  matrix products  99.7 us (13%)
  local copies, waits for them, and re-layouts  68.8 us (9%)
  other arithmetic  54.9 us (7%)
  waiting for transfers between devices  33.7 us (5%)
  blocking collectives  20.4 us (3%)
  between operations  15.9 us (2%)
  starting transfers between devices  8.96 us (1%)
    pallas_call x1, Pallas kernels, reduce_weights(): pl.pallas_call(functools.partial(reduce_kernel, outer, kinds), out_shape=...  164 us
    pallas_call x1, Pallas kernels, gather_weights(): pl.pallas_call(functools.partial(gather_kernel, outer, kinds), out_shape=...  159 us
    dot_general x8, matrix products, product(): return jnp.dot(left, right, preferred_element_type=F32)  38.9 us
    unnamed x188, local copies, waits for them, and re-layouts  36.5 us
    pallas_call x1, Pallas kernels, plane_sum(): pl.pallas_call(plane_sum_kernel, out_shape=(shape, shape), in_specs=[VM,...  34.9 us
    pallas_call x4, Pallas kernels, attend_call(): pl.pallas_call(functools.partial(kernel, joint, rotary), out_shape=shapes...  34.4 us
    dot_general x6, matrix products, product_nt(): lax.dot_general(left, right, (((1,), (1,)), ((), ())), preferred_element_...  31 us
    dot_general x8, matrix products, product_tn(): lax.dot_general(left, right, (((0,), (0,)), ((), ())), preferred_element_...  29.9 us
  transfers between devices with their start and end apart: 11, of which 3 were waited for; matrix products, arithmetic and copies ran while one was open for 21% of the time, Pallas kernels for 15%

profile of v5, /device:TPU:0, one launch (start us, length us, event | category | flops | bytes accessed | tf_op | source)
XLA Modules:
  0.0 733.8 jit_solution(13308179496875479626)
XLA Ops:
  20.4 159.3 %gather_weights.1 = (f32[4,2,2,8,128]{4,3,2,1,0:T(8,128)S(1)}, bf16[4,2,2,16,4608]{4,3,2,1,0:T(8,128)(2,1)S(1)}, bf16[4,2,2,96,2304]{4,3,2,1,0:T(8,128)(2,1)}, b...) custom-call(f32[8,128]{1,0:T(8,128)S(1)} %maximum_bitcast_fusion.1.r, ...), custom_call_target="tpu_custom_call" | custom-call | flops 99999997952 | bytes 100000000 | tf_op jit(solution)/shard_map/gather_weights/pallas_call | solution.py:563
  192.3 4.8 all_to_all.32
  227.9 6.8 fusion.55.refs_0_
  236.2 7.4 %shard_map.238 = (bf16[256,768]{1,0:T(8,128)(2,1)}, f32[256,768]{1,0:T(8,128)}, bf16[256,768]{1,0:T(8,128)(2,1)}, bf16[256,768]{1,0:T(8,128)(2,1)}, f32[256,128]{1,0:T(8,128)}, /*index=5*/f32[256,128]{1,0:T(8,128)}) custom-call(s32[1]{0:T(128)S(6)} %mul.392.live_ref, f32[256,2304]{1,0:T(8,128)} %fusion.55.refs_0_, f32[2,768]{1,0:T(2,128)} %bitcast.259, ...), custom_call_target="tpu_custom_call" | custom-call | flops 201326592 | bytes 4855808 | tf_op jit(solution)/shard_map/pallas_call | solution.py:309
  260.4 11.1 %collective-permute-done.1 = bf16[4,2,96,1536]{3,2,1,0:T(8,128)(2,1)} collective-permute-done((bf16[4,2,96,1536]{3,2,1,0:T(8,128)(2,1)}, bf16[4,2,96,1536]{3,2,1,0:T(8,128)(2,1)}, u32[]{:S(2)}, u32[]{:S(2)}) %collective-permute-start.1) | collective-permute-done | bytes 2359328 | tf_op jit(solution)/shard_map/ppermute | solution.py:1158
  280.4 8.5 %shard_map.239 = (bf16[256,768]{1,0:T(8,128)(2,1)}, f32[256,768]{1,0:T(8,128)}, bf16[256,768]{1,0:T(8,128)(2,1)}, bf16[512,768]{1,0:T(8,128)(2,1)}, f32[256,128]{1,0:T(8,128)}, /*index=5*/f32[512,128]{1,0:T(8,128)}) custom-call(s32[1]{0:T(128)} %constant.131.clone.1.live_ref, f32[256,768]{1,0:T(8,128)} %fusion.57.refs_0_, f32[512,1536]{1,0:T(8,128)} %fusion.58.refs_1_, ...), custom_call_target="tpu_custom_call" | custom-call | flops 402653184 | bytes 6952960 | tf_op jit(solution)/shard_map/pallas_call | solution.py:309
  292.7 4.7 pair_sum.5
  303.9 20.0 %plane_gather.1 = bf16[2,2,2,128,1536]{4,3,2,1,0:T(8,128)(2,1)} custom-call(bf16[128,1536]{1,0:T(8,128)(2,1)} %get-tuple-element.116.own_ref), custom_call_target="tpu_custom_call" | custom-call | flops 10000000000 | bytes 10000000 | tf_op jit(solution)/shard_map/plane_gather/pallas_call | solution.py:635
  323.9 7.0 fusion.60
  335.7 5.9 convolution_convert_fusion.2
  341.6 10.5 %fusion.6 = bf16[1024,1120]{0,1:T(8,128)(2,1)S(1)} fusion(f32[1024,1120]{0,1:T(8,128)} %copy-done.83, bf16[1024,1536]{1,0:T(8,128)(2,1)} %bitcast.237, bf16[1120,1536]{1,0:T(8,128)(2,1)} %all-gather.2.cloned.1.call-done), kind=kOutput, calls=%fused_computation.15 | convolution fusion | flops 3546152960 | bytes 13467648 | tf_op jit(solution)/shard_map/dot_general | solution.py:42
  352.1 5.8 convolution_convert_fusion.4
  357.9 5.1 convolution_convert_fusion.1
  366.4 9.7 %convolution_convert_fusion.5 = bf16[1024,1536]{1,0:T(8,128)(2,1)} fusion(bf16[1120,1536]{1,0:T(8,128)(2,1)} %all-gather.2.cloned.1.call-done, f32[1024,1120]{0,1:T(8,128)} %copy-done.83), kind=kOutput, calls=%fused_computation.18 | convolution fusion | flops 3535110144 | bytes 11173888 | tf_op jit(solution)/shard_map/dot_general | solution.py:34
  376.1 34.9 %plane_sum.1 = (f32[128,1536]{1,0:T(8,128)}, f32[128,1536]{1,0:T(8,128)}) custom-call(bf16[2,2,2,128,1536]{4,3,2,1,0:T(8,128)(2,1)} %bitcast.271, bf16[2,2,2,128,1536]{4,3,2,1,0:T(8,128)(2,1)} %bitcast.268), custom_call_target="tpu_custom_call" | custom-call | flops 10000000000 | bytes 10000000 | tf_op jit(solution)/shard_map/plane_sum/pallas_call | solution.py:694
  420.7 10.2 %shard_map.240 = (bf16[256,768]{1,0:T(8,128)(2,1)}, bf16[512,1536]{1,0:T(8,128)(2,1)}, f32[8,768]{1,0:T(8,128)}) custom-call(s32[1]{0:T(128)} %constant.131.clone.1.live_ref, f32[256,768]{1,0:T(8,128)} %fusion.57.refs_0_, f32[512,1536]{1,0:T(8,128)} %fusion.58.refs_1_, f32[2,768]{1,0:T(2,128)} %bitcast.258, f32[256,128]{1,0:T(8,128)} %get-tuple-element.140.refs_2_.refs_3_, ...), custom_call_target="tpu_custom_call" | custom-call | flops 1006632960 | bytes 8943616 | tf_op jit(solution)/shard_map/pallas_call | solution.py:309
  445.1 5.7 copy.89
  457.8 8.2 %shard_map.241 = (bf16[256,2304]{1,0:T(8,128)(2,1)}, f32[8,768]{1,0:T(8,128)}) custom-call(s32[1]{0:T(128)S(6)} %mul.392.live_ref, f32[256,2304]{1,0:T(8,128)} %fusion.55.refs_0_, f32[2,768]{1,0:T(2,128)} %bitcast.260, f32[256,128]{1,0:T(8,128)} %get-tuple-element.140.refs_2_.refs_3_, f32[256,128]{1,0:T(8,128)} %get-tuple-element.141.refs_3_.refs_4_, ...), custom_call_target="tpu_custom_call" | custom-call | flops 503316480 | bytes 6060032 | tf_op jit(solution)/shard_map/pallas_call | solution.py:309
  466.0 6.5 fusion.62.part_ref
  472.6 4.8 pair_sum.7
  513.6 4.9 convolution_convert_fusion
  518.5 6.7 collective-permute-done.6
  527.7 15.8 %collective-permute-done.7 = bf16[4,2,96,1536]{3,2,1,0:T(8,128)(2,1)} collective-permute-done((bf16[4,2,96,1536]{3,2,1,0:T(8,128)(2,1)}, bf16[4,2,96,1536]{3,2,1,0:T(8,128)(2,1)}, u32[]{:S(2)}, u32[]{:S(2)}) %collective-permute-start.7) | collective-permute-done | bytes 2359328 | tf_op jit(solution)/shard_map/ppermute | solution.py:1232
  546.8 164.0 %reduce_weights.1 = (f32[96,1536]{1,0:T(8,128)}, f32[96,3072]{1,0:T(8,128)}, f32[96,1536]{1,0:T(8,128)}, f32[96,1536]{1,0:T(8,128)}, f32[96,4608]{1,0:T(8,128)},...) custom-call(bf16[4,2,96,768]{3,2,1,0:T(8,128)(2,1)} %bitcast_add_fusion.1.refs_0_, ...), custom_call_target="tpu_custom_call" | custom-call | flops 99999997952 | bytes 100000000 | tf_op jit(solution)/shard_map/reduce_weights/pallas_call | solution.py:1016
  (333 shorter events, 189.4 us)
Async XLA Ops:
  7.2 334.4 %all-gather.2.cloned.1.call-start = ((), (), s32[]{:S(2)}) async-start(), calls=%async_computation.4 | async-start | bytes 4300800 | tf_op jit(solution)/shard_map/all_gather | solution.py:1060
  200.1 98.7 %collective-permute-start.4 = (bf16[128,1536]{1,0:T(8,128)(2,1)}, bf16[128,1536]{1,0:T(8,128)(2,1)}, u32[]{:S(2)}, u32[]{:S(2)}) collective-permute-start(bf16[128,1536]{1,0:T(8,128)(2,1)} %fusion.16), channel_id=1, source_target_pairs={{0,6},{2,4},{4,2},{6,0},{1,7},{3,5},{5,3},{7,1},{8,14},{10,12},{12... | collective-permute-start | bytes 1179656 | tf_op jit(solution)/shard_map/ppermute | solution.py:1164
  201.6 97.2 %collective-permute-start.3 = (bf16[128,1536]{1,0:T(8,128)(2,1)}, bf16[128,1536]{1,0:T(8,128)(2,1)}, u32[]{:S(2)}, u32[]{:S(2)}) collective-permute-start(bf16[128,1536]{1,0:T(8,128)(2,1)} %fusion.16), channel_id=1, source_target_pairs={{0,4},{4,0},{1,5},{5,1},{2,6},{6,2},{3,7},{7,3},{8,12},{12,8},{9,1... | collective-permute-start | bytes 1179656 | tf_op jit(solution)/shard_map/ppermute | solution.py:1163
  203.0 95.9 %collective-permute-start.2 = (bf16[128,1536]{1,0:T(8,128)(2,1)}, bf16[128,1536]{1,0:T(8,128)(2,1)}, u32[]{:S(2)}, u32[]{:S(2)}) collective-permute-start(bf16[128,1536]{1,0:T(8,128)(2,1)} %fusion.16), channel_id=1, source_target_pairs={{0,2},{2,0},{1,3},{3,1},{4,6},{6,4},{5,7},{7,5},{8,10},{10,8},{9,1... | collective-permute-start | bytes 1179656 | tf_op jit(solution)/shard_map/ppermute | solution.py:1162
  203.6 343.2 %reduce-scatter.5.cloned.1.call-start = ((), (), s32[]{:S(2)}) async-start(), calls=%async_computation.5 | async-start | bytes 4300800 | tf_op jit(solution)/shard_map/reduce_scatter | solution.py:1064
  203.7 52.5 %collective-permute-start = (bf16[4,2,96,768]{3,2,1,0:T(8,128)(2,1)S(1)}, bf16[4,2,96,768]{3,2,1,0:T(8,128)(2,1)}, u32[]{:S(2)}, u32[]{:S(2)}) collective-permute-start(bf16[4,2,96,768]{3,2,1,0:T(8,128)(2,1)S(1)} %get-tuple-element.65), channel_id=1, source_target_pairs={{0,2},{2,0},{1,3},{3,1},{4,6},{6,4},{5,7},{7,5},{8,10},{10,8},{9,1... | collective-permute-start | bytes 3538952 | tf_op jit(solution)/shard_map/ppermute | solution.py:1159
  205.2 66.3 %collective-permute-start.1 = (bf16[4,2,96,1536]{3,2,1,0:T(8,128)(2,1)}, bf16[4,2,96,1536]{3,2,1,0:T(8,128)(2,1)}, u32[]{:S(2)}, u32[]{:S(2)}) collective-permute-start(bf16[4,2,96,1536]{3,2,1,0:T(8,128)(2,1)} %get-tuple-element.67), channel_id=1, source_target_pairs={{0,4},{4,0},{1,5},{5,1},{2,6},{6,2},{3,7},{7,3},{8,12},{12,8},{9,1... | collective-permute-start | bytes 7077896 | tf_op jit(solution)/shard_map/ppermute | solution.py:1158
  258.6 12.9 %copy-start.17 = (bf16[4,2,2,96,768]{4,3,2,1,0:T(8,128)(2,1)}, bf16[4,2,2,96,768]{4,3,2,1,0:T(8,128)(2,1)S(1)}, u32[]{:S(2)}) copy-start(bf16[4,2,2,96,768]{4,3,2,1,0:T(8,128)(2,1)S(1)} %copy.79) | copy-start | bytes 7077892
  258.7 12.9 %copy-start.39 = (bf16[4,2,96,1536]{3,2,1,0:T(8,128)(2,1)S(1)}, bf16[4,2,96,1536]{3,2,1,0:T(8,128)(2,1)}, u32[]{:S(2)}) copy-start(bf16[4,2,96,1536]{3,2,1,0:T(8,128)(2,1)} %get-tuple-element.67) | copy-start | bytes 7077892
  302.3 28.7 %collective-permute-start.5 = (bf16[4,128,1536]{2,1,0:T(8,128)(2,1)}, bf16[4,128,1536]{2,1,0:T(8,128)(2,1)}, u32[]{:S(2)}, u32[]{:S(2)}) collective-permute-start(bf16[4,128,1536]{2,1,0:T(8,128)(2,1)} %get-tuple-element.121), channel_id=1, source_target_pairs={{0,1},{1,0},{2,3},{3,2},{4,5},{5,4},{6,7},{7,6},{8,9},{9,8},{10,11... | collective-permute-start | bytes 4718600 | tf_op jit(solution)/shard_map/ppermute | solution.py:1194
  302.4 21.5 %copy-start.60 = (f32[128]{0:T(128)}, f32[128]{0:T(128)S(1)}, u32[]{:S(2)}) copy-start(f32[128]{0:T(128)S(1)} %broadcast_multiply_fusion) | copy-start | bytes 1540
  302.6 21.3 %copy-start.76 = (f32[128]{0:T(128)}, f32[128]{0:T(128)S(1)}, u32[]{:S(2)}) copy-start(f32[128]{0:T(128)S(1)} %multiply_reduce_fusion.2) | copy-start | bytes 1540
  302.6 21.3 %copy-start.65 = (f32[128]{0:T(128)}, f32[128]{0:T(128)S(1)}, u32[]{:S(2)}) copy-start(f32[128]{0:T(128)S(1)} %fusion.46) | copy-start | bytes 1540
  363.1 183.7 %reduce-scatter.7.cloned.1.call-start = ((), (), s32[]{:S(2)}) async-start(), calls=%async_computation.6 | async-start | bytes 4423680 | tf_op jit(solution)/shard_map/reduce_scatter | solution.py:1064
  419.2 11.8 %copy-start.33 = (bf16[256,1536]{1,0:T(8,128)(2,1)}, bf16[256,1536]{1,0:T(8,128)(2,1)S(1)}, u32[]{:S(2)}) copy-start(bf16[256,1536]{1,0:T(8,128)(2,1)S(1)} %all_gather.18) | copy-start | bytes 2359300
  472.6 11.0 %copy-start.12 = (bf16[2,256,1536]{2,1,0:T(8,128)(2,1)S(1)}, bf16[2,256,1536]{2,1,0:T(8,128)(2,1)}, u32[]{:S(2)}) copy-start(bf16[2,256,1536]{2,1,0:T(8,128)(2,1)} %copy-done.10) | copy-start | bytes 4718596
  489.6 53.9 %collective-permute-start.7 = (bf16[4,2,96,1536]{3,2,1,0:T(8,128)(2,1)}, bf16[4,2,96,1536]{3,2,1,0:T(8,128)(2,1)}, u32[]{:S(2)}, u32[]{:S(2)}) collective-permute-start(bf16[4,2,96,1536]{3,2,1,0:T(8,128)(2,1)} %dynamic-slice_bitcast_fusion), channel_id=1, source_target_pairs={{0,4},{4,0},{1,5},{5,1},{2,6},{6,2},{3,7},{7,3},{8,12},{12,8},{9,1... | collective-permute-start | bytes 7077896 | tf_op jit(solution)/shard_map/ppermute | solution.py:1232
  495.5 12.3 %copy-start.41 = (bf16[256,768]{1,0:T(8,128)(2,1)S(1)}, bf16[256,768]{1,0:T(8,128)(2,1)}, u32[]{:S(2)}) copy-start(bf16[256,768]{1,0:T(8,128)(2,1)} %get-tuple-element.63) | copy-start | bytes 1179652
  496.6 28.6 %collective-permute-start.6 = (bf16[4,2,96,768]{3,2,1,0:T(8,128)(2,1)}, bf16[4,2,96,768]{3,2,1,0:T(8,128)(2,1)}, u32[]{:S(2)}, u32[]{:S(2)}) collective-permute-start(bf16[4,2,96,768]{3,2,1,0:T(8,128)(2,1)} %dynamic-slice_bitcast_fusion.1), channel_id=1, source_target_pairs={{0,2},{2,0},{1,3},{3,1},{4,6},{6,4},{5,7},{7,5},{8,10},{10,8},{9,1... | collective-permute-start | bytes 3538952 | tf_op jit(solution)/shard_map/ppermute | solution.py:1233
  498.8 12.5 %copy-start.34 = (bf16[256,1536]{1,0:T(8,128)(2,1)S(1)}, bf16[256,1536]{1,0:T(8,128)(2,1)}, u32[]{:S(2)}) copy-start(bf16[256,1536]{1,0:T(8,128)(2,1)} %copy-done.33) | copy-start | bytes 2359300
  498.8 12.5 %copy-start.42 = (bf16[256,768]{1,0:T(8,128)(2,1)S(1)}, bf16[256,768]{1,0:T(8,128)(2,1)}, u32[]{:S(2)}) copy-start(bf16[256,768]{1,0:T(8,128)(2,1)} %get-tuple-element.68) | copy-start | bytes 1179652
  511.3 32.1 %slice-start = ((s8[4718592]{0:T(1024)(128)(4,1)}), s8[4194304]{0:T(1024)(128)(4,1)S(1)}, s32[]{:S(2)}) async-start(s8[4718592]{0:T(1024)(128)(4,1)} %bitcast.230), calls=%async_computation.7 | async-start | bytes 8388608
  513.6 11.6 %copy-start.19 = (bf16[1536,768]{1,0:T(8,128)(2,1)S(1)}, bf16[1536,768]{1,0:T(8,128)(2,1)}, u32[]{:S(2)}) copy-start(bf16[1536,768]{1,0:T(8,128)(2,1)} %copy-done.18) | copy-start | bytes 7077892
  513.6 29.8 %slice-start.1 = ((s8[4718592]{0:T(1024)(128)(4,1)}), s8[524288]{0:T(1024)(128)(4,1)S(1)}, s32[]{:S(2)}) async-start(s8[4718592]{0:T(1024)(128)(4,1)} %bitcast.230), calls=%async_computation.8 | async-start | bytes 1048576
  (73 other events, 280.4 us)
Sparse Core Ops, SparseCore 0:
  203.8 70.2 all-gather.1
  363.2 66.8 reduce-scatter.4
  455.3 68.5 reduce-scatter.6

commit v6 on v5

--- a/solution.py
+++ b/solution.py
@@ -3,6 +3,7 @@
 
 import jax
 import jax.numpy as jnp
+import numpy as np
 from jax import lax
 from jax.experimental import pallas as pl
 from jax.experimental.pallas import tpu as pltpu
@@ -54,34 +55,28 @@
     return jnp.concatenate([jnp.cos(angles), jnp.sin(angles)], axis=1)
 
 
-def rotary_tables(frame_pos, token_spot):
+def rotary_tables(frames):
     half_dim = HD // 2
     side_pairs = HD // 6
     lead_pairs = half_dim - 2 * side_pairs
-    pair_index = jnp.arange(half_dim)
-    log_base = -math.log(10000.0)
-    lead_part = pair_index < lead_pairs
-    side_part = jnp.logical_and(pair_index >= lead_pairs, pair_index < lead_pairs + side_pairs)
-    last_part = pair_index >= lead_pairs + side_pairs
-    frame_rate = jnp.where(
-        lead_part, jnp.exp(log_base * pair_index.astype(F32) / lead_pairs), 0.0
-    )
-    row_rate = jnp.where(
-        side_part, jnp.exp(log_base * (pair_index - lead_pairs).astype(F32) / side_pairs), 0.0
-    )
-    column_rate = jnp.where(
-        last_part,
-        jnp.exp(log_base * (pair_index - lead_pairs - side_pairs).astype(F32) / side_pairs),
-        0.0,
-    )
-    patch_row = (token_spot // WP).astype(F32)
-    patch_column = (token_spot % WP).astype(F32)
+    pair = np.arange(half_dim)
+    lead = pair < lead_pairs
+    side = (pair >= lead_pairs) & (pair < lead_pairs + side_pairs)
+    last = pair >= lead_pairs + side_pairs
+
+    def rates(part, start, count):
+        rate = np.exp(np.float32(-math.log(10000.0)) * (pair - start).astype(np.float32) / np.float32(count))
+        return np.where(part, rate, 0.0).astype(np.float32)
+
+    spot = np.tile(np.arange(FRAME_TOK), frames)
+    frame = np.repeat(np.arange(frames), FRAME_TOK).astype(np.float32)
     angles = (
-        frame_pos.astype(F32)[:, None] * frame_rate[None, :]
-        + patch_row[:, None] * row_rate[None, :]
-        + patch_column[:, None] * column_rate[None, :]
-    )
-    return (jnp.cos(angles), jnp.sin(angles))
+        frame[:, None] * rates(lead, 0, lead_pairs)[None]
+        + (spot // WP).astype(np.float32)[:, None] * rates(side, lead_pairs, side_pairs)[None]
+        + (spot % WP).astype(np.float32)[:, None] * rates(last, lead_pairs + side_pairs, side_pairs)[None]
+    ).astype(np.float32)
+    cosine, sine = np.cos(angles), np.sin(angles)
+    return np.concatenate([cosine, cosine], axis=1), np.concatenate([-sine, sine], axis=1)
 
 
 def modulated(residual, shift, scale):
@@ -804,13 +799,10 @@
         width = width_of(p)
         return held.at[(*place, slice(None), pl.ds(part * width, width))]
 
-    frame_width = frames_ref.shape[1]
-    frame_mine = pl.ds(pl.multiple_of(core * frame_width, frame_width), frame_width)
-    frame_other = pl.ds(pl.multiple_of((1 - core) * frame_width, frame_width), frame_width)
-    frame_copy = fly.local(frames_ref, frames_out.at[here, :, frame_mine], l_s.at[0])
+    frame_copy = fly.local(frames_ref, frames_out.at[here, core], l_s.at[0])
     small_copy = fly.local(small_ref.at[here], small_in.at[here], l_s.at[1])
     for j, index in enumerate(others):
-        fly.send(frames_ref, frames_out.at[here, :, frame_mine], f_s.at[j], f_r.at[here], chip(index))
+        fly.send(frames_ref, frames_out.at[here, core], f_s.at[j], f_r.at[here], chip(index))
         fly.send(small_ref.at[index], small_in.at[here], m_s.at[j], m_r.at[here], chip(index))
 
     near_by = ((y, 1 - x), (1 - y, x), (1 - y, 1 - x))
@@ -971,15 +963,15 @@
         if tick == total:
             frame_copy.wait()
             for index in others:
-                landed(frames_out.at[index, :, frame_mine], f_r.at[index], chip(index))
-            fly.send(frames_out.at[:, :, frame_mine], frames_out.at[:, :, frame_mine], p_s.at[6], p_r.at[6], core_peer)
+                landed(frames_out.at[index, core], f_r.at[index], chip(index))
+            fly.send(frames_out.at[:, core], frames_out.at[:, core], p_s.at[6], p_r.at[6], core_peer)
             small_copy.wait()
             for index in others:
                 landed(small_in.at[index], m_r.at[index], chip(index))
             small_own[...] = jnp.sum(small_in[...], axis=0)
             fly.send(small_own, small_peer, l_s.at[2], l_s.at[3], core_peer)
 
-    landed(frames_out.at[:, :, frame_other], p_r.at[6], core_peer)
+    landed(frames_out.at[:, 1 - core], p_r.at[6], core_peer)
     landed(small_peer, l_s.at[3], core_peer)
     small_out[...] = small_own[...] + small_peer[...]
     for p, (i, part) in enumerate(pieces):
@@ -1007,7 +999,7 @@
             chain.append(pltpu.VMEM((outer + 1, rows, width), BF))
         if form == SPLIT:
             whole.append(pltpu.VMEM((outer, 2, 2, rows, full_width), BF))
-    shapes.append(jax.ShapeDtypeStruct((shards, frames.shape[0], 2 * frames.shape[1]), frames.dtype))
+    shapes.append(jax.ShapeDtypeStruct((shards, 2, *frames.shape), frames.dtype))
     shapes.append(jax.ShapeDtypeStruct(small.shape[1:], F32))
     shapes.append(jax.ShapeDtypeStruct((up.shape[1], 2 * PLANE * up.shape[2]), F32))
     shapes.append(jax.ShapeDtypeStruct((2 * down.shape[0], down.shape[1]), F32))
@@ -1056,16 +1048,48 @@
     return results[:count], *results[count:]
 
 
+def modulation_kernel(sinus_ref, matrix_ref, bias_ref, out_ref, half, send, recv):
+    core = lax.axis_index("sp")
+    core_peer = {"sp": 1 - core}
+    fly = Flights()
+    greet((core_peer,))
+    frames, width = out_ref.shape[0], matrix_ref.shape[1]
+    half[...] = product(sinus_ref[...], matrix_ref[...]) + bias_ref[...]
+    for side in range(2):
+
+        @pl.when(core == side)
+        def _(side=side):
+            out_ref[:, side * width : (side + 1) * width] = half[side * frames : (side + 1) * frames, :]
+            half[:frames, :] = half[(1 - side) * frames : (2 - side) * frames, :]
+
+    columns = pl.ds(pl.multiple_of(core * width, width), width)
+    others = pl.ds(pl.multiple_of((1 - core) * width, width), width)
+    fly.send(half.at[pl.ds(0, frames)], out_ref.at[:, columns], send.at[0], recv.at[0], core_peer)
+    landed(out_ref.at[:, others], recv.at[0], core_peer)
+    fly.drain()
+
+
+def modulate(sinus, matrix, bias):
+    dma = pltpu.SemaphoreType.DMA
+    frames, width = sinus.shape[0], matrix.shape[1]
+    return pl.pallas_call(
+        modulation_kernel,
+        out_shape=jax.ShapeDtypeStruct((frames // 2, 2 * width), F32),
+        in_specs=[VM, VM, VM],
+        out_specs=VM,
+        scratch_shapes=[pltpu.VMEM((frames, width), F32), dma((1,)), dma((1,))],
+        compiler_params=pltpu.CompilerParams(collective_id=9, has_side_effects=True),
+        cost_estimate=pl.CostEstimate(flops=10**9, bytes_accessed=10**7, transcendentals=0),
+        name="modulation",
+    )(sinus, matrix, bias)
+
+
 def gather(value, axes, axis=0):
     return lax.all_gather(value, axes, axis=axis, tiled=True)
 
 
 def scatter(value, axes, axis=0):
     return lax.psum_scatter(value, axes, scatter_dimension=axis, tiled=True)
-
-
-def swap(value, split_axis, concat_axis):
-    return lax.all_to_all(value, "sp", split_axis=split_axis, concat_axis=concat_axis, tiled=True)
 
 
 def body(
@@ -1112,13 +1136,19 @@
     ).reshape(small_rows, small_width)
     gathered = gather_weights(
         outer,
-        ((0, ALL_CHIPS), (1, ALL_CHIPS), (3, ALL_CHIPS), (1, KEEP), (2, HALF_X), (1, HALF_Y), (1, KEEP)),
-        [small, *(w[0] for w in (mod_weight, self_in, self_out, cross_kv, cross_q, cross_out))],
+        ((0, ALL_CHIPS), (1, ALL_CHIPS), (3, ALL_CHIPS), (1, KEEP), (1, ALL_CHIPS), (1, HALF_X), (1, HALF_Y), (1, KEEP)),
+        [
+            small,
+            *(w[0] for w in (mod_weight, self_in, self_out, cross_q)),
+            cross_kv[0, :, :D],
+            cross_kv[0, :, D:],
+            cross_out[0],
+        ],
         mlp_in[0],
         text,
     )
-    small_all, mod_matrix, self_proj, self_back, kv_half, q_half, cross_back = gathered[:7]
-    up_matrix, text_all = gathered[7:]
+    small_all, mod_matrix, self_proj, self_back, cross_qproj, k_half, v_half, cross_back = gathered[:8]
+    up_matrix, text_all = gathered[8:]
     hid = mlp_out.shape[1] // 2
     down_part = lax.dynamic_slice_in_dim(mlp_out[0], core * hid, hid, 0)
     down_part, small_all = lax.optimization_barrier((down_part, small_all))
@@ -1137,17 +1167,11 @@
     live_keys = clip_frames * FRAME_TOK
     all_keys = jnp.full((1,), TXT, jnp.int32)
     own_steps = lax.dynamic_slice_in_dim(timestep[0], own_frame, frame_count)
-    clip_pos = jnp.arange(group_frames, dtype=jnp.int32)
-    cosine, sine = rotary_tables(
-        jnp.repeat(clip_pos, FRAME_TOK),
-        jnp.tile(jnp.arange(FRAME_TOK, dtype=jnp.int32), group_frames),
-    )
-    cosine, sine = jnp.concatenate([cosine, cosine], axis=1), jnp.concatenate([-sine, sine], axis=1)
+    cosine, sine = (jnp.asarray(table) for table in rotary_tables(group_frames))
     sinus = sinus_features(timestep[0]).astype(BF)
 
-    mod_half = product(sinus, mod_matrix)
-    mod_half = mod_half + lax.dynamic_slice_in_dim(bias_all, core * 3 * D, 3 * D)[None]
-    modulation = swap(mod_half, 0, 1)
+    bias_half = lax.dynamic_slice_in_dim(bias_all, core * 3 * D, 3 * D)[None]
+    modulation = modulate(sinus, mod_matrix, bias_half)
     shift_one, scale_one, gate_one, shift_two, scale_two, gate_two = jnp.split(
         modulation, 6, axis=1
     )
@@ -1155,22 +1179,22 @@
     grad_branch = frame_scaled(cotangent.astype(F32), gate_two).astype(BF)
     exchange = [(0, 1), (1, 0)]
     place_y, place_x = lax.axis_index("yb"), lax.axis_index("xc")
-    kv_other = lax.ppermute(kv_half, "yb", exchange)
-    q_other = lax.ppermute(q_half, "xc", exchange)
+    k_other = lax.ppermute(k_half, "yb", exchange)
+    v_other = lax.ppermute(v_half, "xc", exchange)
+    residual = tokens.astype(F32)
+    attn_float, back_attn_input = jax.vjp(modulated, residual, shift_one, scale_one)
+    attn_input = gather(attn_float.astype(BF), "sp")
+    joined = product(attn_input, self_proj)
+    self_mixed, self_lse, *self_kept = attend_forward(
+        live_keys, [joined], gain_own[:2], cosine, sine, True, 5
+    )
+    grad_branch, self_mixed = lax.optimization_barrier((grad_branch, self_mixed))
     beside = [
         grad_branch,
         lax.ppermute(grad_branch, "xc", exchange),
         lax.ppermute(grad_branch, "yb", exchange),
         lax.ppermute(grad_branch, PL, [(0, 3), (1, 2), (2, 1), (3, 0)]),
     ]
-
-    residual = tokens.astype(F32)
-    attn_float, back_attn_input = jax.vjp(modulated, residual, shift_one, scale_one)
-    attn_input = gather(attn_float.astype(BF), "sp")
-    joined = product(attn_input, self_proj)
-    self_mixed, self_lse, *self_kept = attend_forward(
-        live_keys, [joined], gain_own[:2], cosine, sine, True, 5
-    )
     self_branch = pair_sum(product(self_mixed, self_back))
     residual = residual + frame_scaled(self_branch, gate_one)
 
@@ -1178,8 +1202,9 @@
         pair = jnp.where(place == 0, jnp.stack([own, other], axis), jnp.stack([other, own], axis))
         return pair.reshape(-1, own.shape[-1])
 
-    cross_kvproj = beside_own(kv_half, kv_other, place_y, 1)
-    cross_qproj = beside_own(q_half, q_other, place_x, 2)
+    cross_kvproj = jnp.concatenate(
+        [beside_own(k_half, k_other, place_y, 1), beside_own(v_half, v_other, place_x, 2)], axis=1
+    )
     text_raw = product(text_all, cross_kvproj)
     cross_float, back_cross_norm = jax.vjp(layer_norm, residual)
     cross_input = gather(cross_float.astype(BF), "sp")
@@ -1251,7 +1276,6 @@
         [grad_shift_one, grad_scale_one, grad_gate_one, grad_shift_two, grad_scale_two, grad_gate_two],
         axis=1,
     )
-    grad_mod_half = swap(grad_modulation, 1, 0)
     grad_gains = jnp.concatenate([gains_self[:2], gains_cross[:2]])
     both = jnp.arange(2)[None, :, None] == core
     grad_gains = jnp.where(both, grad_gains[:, None, :], 0.0).reshape(4, shards, gain_len)
@@ -1269,7 +1293,7 @@
         outer,
         ((1, OVER_Y), (2, OVER_X), (1, SPLIT), (1, SPLIT), (3, PLAIN)),
         [q_near, kv_near, grad_cross_back, grad_self_back, grad_self_proj],
-        grad_mod_half.astype(BF),
+        grad_modulation.astype(BF),
         grad_small,
         up_owned.reshape(PLANE, -1, up_owned.shape[1]),
         down_owned,

time: 747 us -> 755 us (1.011)
  waiting for transfers between devices: 33.7 us -> 59.8 us
  blocking collectives: 20.4 us -> 10.2 us
  Pallas kernels: 431 us -> 440 us
    ppermute x2, waiting for transfers between devices: 11.1 us -> 24.6 us  [the longest x1 24.6 us: body(): k_other = lax.ppermute(k_half, 'yb', exchange)]
    ppermute x1, waiting for transfers between devices: 6.74 us -> 15.8 us  [body(): lax.ppermute(lax.dynamic_index_in_dim(q_parts, 1 - place_x, 2, False), 'x...]
    all_to_all x2 -> x0, blocking collectives: 8.76 us -> none  [swap(): lax.all_to_all(value, 'sp', split_axis=split_axis, concat_axis=concat_axi...]
    dot_general x8 -> x7, matrix products: 38.9 us -> 35.8 us  [product(): return jnp.dot(left, right, preferred_element_type=F32)]
  transfers between devices with their start and end apart: 11 -> 11, of which waited for: 3 -> 3; matrix products, arithmetic and copies ran while one was open for 21% -> 16% of each run, Pallas kernels for 15% -> 14%
where the time goes in v6:
time: 755 us; the launch traced here: 743 us
  Pallas kernels  440 us (58%)
  matrix products  93.1 us (12%)
  local copies, waits for them, and re-layouts  67 us (9%)
  waiting for transfers between devices  59.8 us (8%)
  other arithmetic  48.7 us (6%)
  between operations  15.8 us (2%)
  blocking collectives  10.2 us (1%)
  starting transfers between devices  8.05 us (1%)
    pallas_call x1, Pallas kernels, gather_weights(): pl.pallas_call(functools.partial(gather_kernel, outer, kinds), out_shape=...  166 us
    pallas_call x1, Pallas kernels, reduce_weights(): pl.pallas_call(functools.partial(reduce_kernel, outer, kinds), out_shape=...  162 us
    unnamed x188, local copies, waits for them, and re-layouts  39.6 us
    dot_general x7, matrix products, product(): return jnp.dot(left, right, preferred_element_type=F32)  35.8 us
    pallas_call x1, Pallas kernels, plane_sum(): pl.pallas_call(plane_sum_kernel, out_shape=(shape, shape), in_specs=[VM,...  35 us
    pallas_call x4, Pallas kernels, attend_call(): pl.pallas_call(functools.partial(kernel, joint, rotary), out_shape=shapes...  34.4 us
    dot_general x6, matrix products, product_nt(): lax.dot_general(left, right, (((1,), (1,)), ((), ())), preferred_element_...  29.9 us
    dot_general x8, matrix products, product_tn(): lax.dot_general(left, right, (((0,), (0,)), ((), ())), preferred_element_...  27.4 us
  transfers between devices with their start and end apart: 11, of which 3 were waited for; matrix products, arithmetic and copies ran while one was open for 16% of the time, Pallas kernels for 14%

profile of v6, /device:TPU:0, one launch (start us, length us, event | category | flops | bytes accessed | tf_op | source)
XLA Modules:
  0.0 742.7 jit_solution(17431769303452257329)
XLA Ops:
  23.0 165.9 %gather_weights.1 = (f32[4,2,2,8,128]{4,3,2,1,0:T(8,128)S(1)}, bf16[4,2,2,16,4608]{4,3,2,1,0:T(8,128)(2,1)S(1)}, bf16[4,2,2,96,2304]{4,3,2,1,0:T(8,128)(2,1)}, b...) custom-call(f32[8,128]{1,0:T(8,128)S(1)} %maximum_bitcast_fusion.1.r, ...), custom_call_target="tpu_custom_call" | custom-call | flops 99999997952 | bytes 100000000 | tf_op jit(solution)/shard_map/gather_weights/pallas_call | solution.py:558
  223.4 6.4 fusion.47.refs_0_
  229.9 7.4 shard_map.256
  247.2 4.8 pair_sum.4
  259.0 24.6 %collective-permute-done = bf16[4,2,96,768]{3,2,1,0:T(8,128)(2,1)} collective-permute-done((bf16[4,2,96,768]{3,2,1,0:T(8,128)(2,1)}, bf16[4,2,96,768]{3,2,1,0:T(8,128)(2,1)}, u32[]{:S(2)}, u32[]{:S(2)}) %collective-permute-start) | collective-permute-done | bytes 1179680 | tf_op jit(solution)/shard_map/ppermute | solution.py:1182
  293.7 8.6 %shard_map.257 = (bf16[256,768]{1,0:T(8,128)(2,1)}, f32[256,768]{1,0:T(8,128)}, bf16[256,768]{1,0:T(8,128)(2,1)}, bf16[512,768]{1,0:T(8,128)(2,1)}, f32[256,128]{1,0:T(8,128)}, /*index=5*/f32[512,128]{1,0:T(8,128)}) custom-call(s32[1]{0:T(128)} %constant.87.clone.1.live_ref, f32[256,768]{1,0:T(8,128)} %fusion.49.refs_0_, f32[512,1536]{1,0:T(8,128)} %fusion.refs_1_, ...), custom_call_target="tpu_custom_call" | custom-call | flops 402653184 | bytes 6952960 | tf_op jit(solution)/shard_map/pallas_call | solution.py:304
  317.7 20.0 %plane_gather.1 = bf16[2,2,2,128,1536]{4,3,2,1,0:T(8,128)(2,1)} custom-call(bf16[128,1536]{1,0:T(8,128)(2,1)} %get-tuple-element.122.own_ref), custom_call_target="tpu_custom_call" | custom-call | flops 10000000000 | bytes 10000000 | tf_op jit(solution)/shard_map/plane_gather/pallas_call | solution.py:630
  337.7 7.0 fusion.51
  349.5 5.5 convolution_convert_fusion.2
  354.9 10.5 %fusion.10 = bf16[1024,1120]{0,1:T(8,128)(2,1)S(1)} fusion(f32[1024,1120]{0,1:T(8,128)} %copy-done.83, bf16[1024,1536]{1,0:T(8,128)(2,1)} %bitcast.229, bf16[1120,1536]{1,0:T(8,128)(2,1)} %all-gather.2.cloned.1.call-done), kind=kOutput, calls=%fused_computation.17 | convolution fusion | flops 3546152960 | bytes 13467648 | tf_op jit(solution)/shard_map/dot_general | solution.py:43
  365.5 6.0 convolution_convert_fusion.4
  371.4 5.1 convolution_convert_fusion.1
  379.7 9.8 %convolution_convert_fusion.5 = bf16[1024,1536]{1,0:T(8,128)(2,1)} fusion(bf16[1120,1536]{1,0:T(8,128)(2,1)} %all-gather.2.cloned.1.call-done, f32[1024,1120]{0,1:T(8,128)} %copy-done.83), kind=kOutput, calls=%fused_computation.20 | convolution fusion | flops 3535110144 | bytes 11173888 | tf_op jit(solution)/shard_map/dot_general | solution.py:35
  389.5 35.0 %plane_sum.1 = (f32[128,1536]{1,0:T(8,128)}, f32[128,1536]{1,0:T(8,128)}) custom-call(bf16[2,2,2,128,1536]{4,3,2,1,0:T(8,128)(2,1)} %bitcast.264, bf16[2,2,2,128,1536]{4,3,2,1,0:T(8,128)(2,1)} %bitcast.261), custom_call_target="tpu_custom_call" | custom-call | flops 10000000000 | bytes 10000000 | tf_op jit(solution)/shard_map/plane_sum/pallas_call | solution.py:689
  434.4 10.2 %shard_map.258 = (bf16[256,768]{1,0:T(8,128)(2,1)}, bf16[512,1536]{1,0:T(8,128)(2,1)}, f32[8,768]{1,0:T(8,128)}) custom-call(s32[1]{0:T(128)} %constant.87.clone.1.live_ref, f32[256,768]{1,0:T(8,128)} %fusion.49.refs_0_, f32[512,1536]{1,0:T(8,128)} %fusion.refs_1_, f32[2,768]{1,0:T(2,128)} %bitcast.251, f32[256,128]{1,0:T(8,128)} %constant.101.clone.refs_2_.refs_3_, ...), custom_call_target="tpu_custom_call" | custom-call | flops 1006632960 | bytes 8943616 | tf_op jit(solution)/shard_map/pallas_call | solution.py:304
  448.4 4.8 pair_sum.6
  458.8 5.7 copy.66
  469.6 8.2 %shard_map.259 = (bf16[256,2304]{1,0:T(8,128)(2,1)}, f32[8,768]{1,0:T(8,128)}) custom-call(s32[1]{0:T(128)S(6)} %mul.302.live_ref, f32[256,2304]{1,0:T(8,128)} %fusion.47.refs_0_, f32[2,768]{1,0:T(2,128)} %bitcast.253, f32[256,128]{1,0:T(8,128)} %constant.101.clone.refs_2_.refs_3_, f32[256,128]{1,0:T(8,128)} %constant.102.clone.refs_3_.refs_4_, ...), custom_call_target="tpu_custom_call" | custom-call | flops 503316480 | bytes 6060032 | tf_op jit(solution)/shard_map/pallas_call | solution.py:304
  477.8 6.5 fusion.53.part_ref
  484.4 4.8 pair_sum.7
  515.7 4.9 convolution_convert_fusion
  520.6 15.8 %collective-permute-done.6 = bf16[4,2,96,768]{3,2,1,0:T(8,128)(2,1)S(1)} collective-permute-done((bf16[4,2,96,768]{3,2,1,0:T(8,128)(2,1)S(1)}, bf16[4,2,96,768]{3,2,1,0:T(8,128)(2,1)S(1)}, u32[]{:S(2)}, u32[]{:S(2)}) %collective-permute-start.6) | collective-permute-done | bytes 1179680 | tf_op jit(solution)/shard_map/ppermute | solution.py:1258
  537.5 19.4 %collective-permute-done.7 = bf16[4,2,96,1536]{3,2,1,0:T(8,128)(2,1)} collective-permute-done((bf16[4,2,96,1536]{3,2,1,0:T(8,128)(2,1)}, bf16[4,2,96,1536]{3,2,1,0:T(8,128)(2,1)}, u32[]{:S(2)}, u32[]{:S(2)}) %collective-permute-start.7) | collective-permute-done | bytes 2359328 | tf_op jit(solution)/shard_map/ppermute | solution.py:1257
  560.2 161.5 %reduce_weights.1 = (f32[96,1536]{1,0:T(8,128)}, f32[96,3072]{1,0:T(8,128)}, f32[96,1536]{1,0:T(8,128)}, f32[96,1536]{1,0:T(8,128)}, f32[96,4608]{1,0:T(8,128)},...) custom-call(bf16[4,2,96,768]{3,2,1,0:T(8,128)(2,1)} %bitcast_add_fusion.1.refs_0, ...), custom_call_target="tpu_custom_call" | custom-call | flops 99999997952 | bytes 100000000 | tf_op jit(solution)/shard_map/reduce_weights/pallas_call | solution.py:1008
  (321 shorter events, 168.6 us)
Async XLA Ops:
  7.2 347.7 %all-gather.2.cloned.1.call-start = ((), (), s32[]{:S(2)}) async-start(), calls=%async_computation.2 | async-start | bytes 4300800 | tf_op jit(solution)/shard_map/all_gather | solution.py:1088
  7.2 194.4 %copy-start.70 = (f32[128]{0:T(128)}, f32[128]{0:T(128)S(1)}, u32[]{:S(2)}) copy-start(f32[128]{0:T(128)S(1)} %multiply_exponential_fusion) | copy-start | bytes 1540
  221.4 8.5 %copy-start.26 = (bf16[256,1536]{1,0:T(8,128)(2,1)}, bf16[256,1536]{1,0:T(8,128)(2,1)S(1)}, u32[]{:S(2)}) copy-start(bf16[256,1536]{1,0:T(8,128)(2,1)S(1)} %all_gather.15) | copy-start | bytes 2359300
  237.3 74.9 %collective-permute-start.4 = (bf16[128,1536]{1,0:T(8,128)(2,1)}, bf16[128,1536]{1,0:T(8,128)(2,1)}, u32[]{:S(2)}, u32[]{:S(2)}) collective-permute-start(bf16[128,1536]{1,0:T(8,128)(2,1)} %fusion.17), channel_id=1, source_target_pairs={{0,6},{2,4},{4,2},{6,0},{1,7},{3,5},{5,3},{7,1},{8,14},{10,12},{12... | collective-permute-start | bytes 1179656 | tf_op jit(solution)/shard_map/ppermute | solution.py:1196
  238.8 73.4 %collective-permute-start.3 = (bf16[128,1536]{1,0:T(8,128)(2,1)}, bf16[128,1536]{1,0:T(8,128)(2,1)}, u32[]{:S(2)}, u32[]{:S(2)}) collective-permute-start(bf16[128,1536]{1,0:T(8,128)(2,1)} %fusion.17), channel_id=1, source_target_pairs={{0,4},{4,0},{1,5},{5,1},{2,6},{6,2},{3,7},{7,3},{8,12},{12,8},{9,1... | collective-permute-start | bytes 1179656 | tf_op jit(solution)/shard_map/ppermute | solution.py:1195
  240.3 71.9 %collective-permute-start.2 = (bf16[128,1536]{1,0:T(8,128)(2,1)}, bf16[128,1536]{1,0:T(8,128)(2,1)}, u32[]{:S(2)}, u32[]{:S(2)}) collective-permute-start(bf16[128,1536]{1,0:T(8,128)(2,1)} %fusion.17), channel_id=1, source_target_pairs={{0,2},{2,0},{1,3},{3,1},{4,6},{6,4},{5,7},{7,5},{8,10},{10,8},{9,1... | collective-permute-start | bytes 1179656 | tf_op jit(solution)/shard_map/ppermute | solution.py:1194
  240.9 319.4 %reduce-scatter.5.cloned.1.call-start = ((), (), s32[]{:S(2)}) async-start(), calls=%async_computation.3 | async-start | bytes 4300800 | tf_op jit(solution)/shard_map/reduce_scatter | solution.py:1092
  240.9 42.7 %collective-permute-start = (bf16[4,2,96,768]{3,2,1,0:T(8,128)(2,1)}, bf16[4,2,96,768]{3,2,1,0:T(8,128)(2,1)}, u32[]{:S(2)}, u32[]{:S(2)}) collective-permute-start(bf16[4,2,96,768]{3,2,1,0:T(8,128)(2,1)} %copy-done), channel_id=1, source_target_pairs={{0,4},{4,0},{1,5},{5,1},{2,6},{6,2},{3,7},{7,3},{8,12},{12,8},{9,1... | collective-permute-start | bytes 3538952 | tf_op jit(solution)/shard_map/ppermute | solution.py:1182
  242.3 43.3 %collective-permute-start.1 = (bf16[4,2,96,768]{3,2,1,0:T(8,128)(2,1)S(1)}, bf16[4,2,96,768]{3,2,1,0:T(8,128)(2,1)}, u32[]{:S(2)}, u32[]{:S(2)}) collective-permute-start(bf16[4,2,96,768]{3,2,1,0:T(8,128)(2,1)S(1)} %get-tuple-element.72), channel_id=1, source_target_pairs={{0,2},{2,0},{1,3},{3,1},{4,6},{6,4},{5,7},{7,5},{8,10},{10,8},{9,1... | collective-permute-start | bytes 3538952 | tf_op jit(solution)/shard_map/ppermute | solution.py:1183
  254.6 29.1 %copy-start.1 = (bf16[4,2,96,768]{3,2,1,0:T(8,128)(2,1)S(1)}, bf16[4,2,96,768]{3,2,1,0:T(8,128)(2,1)}, u32[]{:S(2)}) copy-start(bf16[4,2,96,768]{3,2,1,0:T(8,128)(2,1)} %copy-done) | copy-start | bytes 3538948
  257.3 26.3 %copy-start.30 = (bf16[256,1536]{1,0:T(8,128)(2,1)}, bf16[256,1536]{1,0:T(8,128)(2,1)S(1)}, u32[]{:S(2)}) copy-start(bf16[256,1536]{1,0:T(8,128)(2,1)S(1)} %all_gather.16) | copy-start | bytes 2359300
  316.1 28.6 %collective-permute-start.5 = (bf16[4,128,1536]{2,1,0:T(8,128)(2,1)}, bf16[4,128,1536]{2,1,0:T(8,128)(2,1)}, u32[]{:S(2)}, u32[]{:S(2)}) collective-permute-start(bf16[4,128,1536]{2,1,0:T(8,128)(2,1)} %get-tuple-element.127), channel_id=1, source_target_pairs={{0,1},{1,0},{2,3},{3,2},{4,5},{5,4},{6,7},{7,6},{8,9},{9,8},{10,11... | collective-permute-start | bytes 4718600 | tf_op jit(solution)/shard_map/ppermute | solution.py:1219
  316.2 21.5 %copy-start.65 = (f32[128]{0:T(128)}, f32[128]{0:T(128)S(1)}, u32[]{:S(2)}) copy-start(f32[128]{0:T(128)S(1)} %broadcast_multiply_fusion) | copy-start | bytes 1540
  316.4 21.3 %copy-start.78 = (f32[128]{0:T(128)}, f32[128]{0:T(128)S(1)}, u32[]{:S(2)}) copy-start(f32[128]{0:T(128)S(1)} %multiply_reduce_fusion.2) | copy-start | bytes 1540
  316.4 21.3 %copy-start.67 = (f32[128]{0:T(128)}, f32[128]{0:T(128)S(1)}, u32[]{:S(2)}) copy-start(f32[128]{0:T(128)S(1)} %fusion.37) | copy-start | bytes 1540
  337.7 7.0 copy-start.24
  354.9 10.5 %copy-start.81 = (bf16[4,4,96,1120]{3,2,1,0:T(8,128)(2,1)S(1)}, bf16[4,4,96,1120]{3,2,1,0:T(8,128)(2,1)}, u32[]{:S(2)}) copy-start(bf16[4,4,96,1120]{3,2,1,0:T(8,128)(2,1)} %get-tuple-element.77) | copy-start | bytes 10321924
  376.6 183.6 %reduce-scatter.7.cloned.1.call-start = ((), (), s32[]{:S(2)}) async-start(), calls=%async_computation.4 | async-start | bytes 4423680 | tf_op jit(solution)/shard_map/reduce_scatter | solution.py:1092
  432.8 11.8 %copy-start.33 = (bf16[256,1536]{1,0:T(8,128)(2,1)}, bf16[256,1536]{1,0:T(8,128)(2,1)S(1)}, u32[]{:S(2)}) copy-start(bf16[256,1536]{1,0:T(8,128)(2,1)S(1)} %all_gather.18) | copy-start | bytes 2359300
  484.4 10.9 %copy-start.15 = (bf16[2,256,1536]{2,1,0:T(8,128)(2,1)S(1)}, bf16[2,256,1536]{2,1,0:T(8,128)(2,1)}, u32[]{:S(2)}) copy-start(bf16[2,256,1536]{2,1,0:T(8,128)(2,1)} %copy-done.13) | copy-start | bytes 4718596
  503.1 53.7 %collective-permute-start.7 = (bf16[4,2,96,1536]{3,2,1,0:T(8,128)(2,1)}, bf16[4,2,96,1536]{3,2,1,0:T(8,128)(2,1)}, u32[]{:S(2)}, u32[]{:S(2)}) collective-permute-start(bf16[4,2,96,1536]{3,2,1,0:T(8,128)(2,1)} %dynamic-slice_bitcast_fusion), channel_id=1, source_target_pairs={{0,4},{4,0},{1,5},{5,1},{2,6},{6,2},{3,7},{7,3},{8,12},{12,8},{9,1... | collective-permute-start | bytes 7077896 | tf_op jit(solution)/shard_map/ppermute | solution.py:1257
  508.5 27.8 %collective-permute-start.6 = (bf16[4,2,96,768]{3,2,1,0:T(8,128)(2,1)S(1)}, bf16[4,2,96,768]{3,2,1,0:T(8,128)(2,1)S(1)}, u32[]{:S(2)}, u32[]{:S(2)}) collective-permute-start(bf16[4,2,96,768]{3,2,1,0:T(8,128)(2,1)S(1)} %dynamic-slice_bitcast_fusion.1), channel_id=1, source_target_pairs={{0,2},{2,0},{1,3},{3,1},{4,6},{6,4},{5,7},{7,5},{8,10},{10,8},{9,1... | collective-permute-start | bytes 3538952 | tf_op jit(solution)/shard_map/ppermute | solution.py:1258
  513.4 43.4 %slice-start = ((s8[4718592]{0:T(1024)(128)(4,1)}), s8[4194304]{0:T(1024)(128)(4,1)S(1)}, s32[]{:S(2)}) async-start(s8[4718592]{0:T(1024)(128)(4,1)} %bitcast.223), calls=%async_computation.5 | async-start | bytes 8388608
  515.7 41.2 %slice-start.1 = ((s8[4718592]{0:T(1024)(128)(4,1)}), s8[524288]{0:T(1024)(128)(4,1)S(1)}, s32[]{:S(2)}) async-start(s8[4718592]{0:T(1024)(128)(4,1)} %bitcast.223), calls=%async_computation.6 | async-start | bytes 1048576
  (73 other events, 208.0 us)
Sparse Core Ops, SparseCore 0:
  241.0 68.5 all-gather.1
  376.7 65.2 reduce-scatter.4
  469.7 66.6 reduce-scatter.6

commit v7 on v6

--- a/solution.py
+++ b/solution.py
@@ -201,7 +201,7 @@
     return values * cos_ref[...] + sign * (pltpu.roll(values, HD // 2, 1) * sin_ref[...])
 
 
-def attend_forward_kernel(joint, rotary, live_ref, *refs):
+def attend_forward_kernel(joint, rotary, gain_row, live_ref, *refs):
     view, width, refs = raw_views(joint, refs)
     gain_ref, cos_ref, sin_ref, refs = *refs[:3], refs[3:]
     out_ref, lse_ref, query_ref, key_ref, inv_q_ref, inv_k_ref, refs = *refs[:6], refs[6:]
@@ -224,8 +224,9 @@
     allowed = spot < live_ref[0]
     for head in range(heads):
         part = slice(head * HD, (head + 1) * HD)
-        query = view(0, head) * inv_q_ref[...] * gain_ref[0:1, part]
-        key = view(1, head) * inv_k_ref[...] * gain_ref[1:2, part]
+        column = pl.ds(pl.multiple_of(lax.axis_index("sp") * width + head * HD, HD), HD)
+        query = view(0, head) * inv_q_ref[...] * gain_ref[gain_row : gain_row + 1, column]
+        key = view(1, head) * inv_k_ref[...] * gain_ref[gain_row + 1 : gain_row + 2, column]
         if rotary:
             query, key = turned(query, cos_ref, sin_ref, 1.0), turned(key, cos_ref, sin_ref, 1.0)
         query, key, value = query.astype(BF), key.astype(BF), view(2, head).astype(BF)
@@ -239,7 +240,7 @@
     fly.drain()
 
 
-def attend_backward_kernel(joint, rotary, live_ref, *refs):
+def attend_backward_kernel(joint, rotary, gain_row, live_ref, *refs):
     view, width, refs = raw_views(joint, refs)
     gain_ref, cos_ref, sin_ref, refs = *refs[:3], refs[3:]
     query_ref, key_ref, lse_ref, inv_q_ref, inv_k_ref, do_ref, refs = *refs[:6], refs[6:]
@@ -276,7 +277,8 @@
                 grad_rows = turned(grad_rows, cos_ref, sin_ref, -1.0)
             raw = view(which, head)
             gain_out[which : which + 1, part] = jnp.sum(grad_rows * raw * inverse[...], axis=0, keepdims=True)
-            scaled = grad_rows * gain_ref[which : which + 1, part]
+            column = pl.ds(pl.multiple_of(lax.axis_index("sp") * width + head * HD, HD), HD)
+            scaled = grad_rows * gain_ref[gain_row + which : gain_row + which + 1, column]
             held[:, part] = scaled
             dots[which] = scaled * raw if head == 0 else dots[which] + scaled * raw
     for which, own, peer in ((0, q_dot, q_peer), (1, k_dot, k_peer)):
@@ -302,7 +304,7 @@
     arrays = [*raws, *others]
     moved = sum(v.size * v.dtype.itemsize for v in [*arrays, *shapes])
     return pl.pallas_call(
-        functools.partial(kernel, joint, rotary),
+        functools.partial(kernel, joint, rotary, 0 if rotary else 2),
         out_shape=shapes,
         in_specs=[SM] + [VM] * len(arrays),
         out_specs=[VM] * len(shapes),
@@ -356,14 +358,15 @@
 def gather_kernel(outer, kinds, *refs):
     full = len(kinds)
     ins, refs = refs[:full], refs[full:]
-    mlp_ref, text_ref, refs = refs[0], refs[1], refs[2:]
+    mlp_in, text_ref, refs = refs[0], refs[1], refs[2:]
     outs, refs = list(refs[:full]), refs[full:]
-    up_out, text_out, refs = refs[0], refs[1], refs[2:]
+    bias_out, gain_out, step_out, up_out, text_out, refs = *refs[:5], refs[5:]
     own, refs = refs[:full], refs[full:]
     halves = [i for i, kind in enumerate(kinds) if kind[1] == KEEP]
     form = [kind[1] for kind in kinds]
     whole, refs = refs[: len(halves)], refs[len(halves) :]
-    up_own, local_sem, zs, zr, s1, r1, s2, r2, a_s, a_r, f_s, f_r, f_l, t_s = refs
+    small_all, mlp_ref, up_own, local_sem, zs, zr, s1, r1, s2, r2, a_s, a_r, f_s, f_r, f_l, t_s, i_s = refs
+    outs[0] = small_all
     z, y, x = (lax.axis_index(name) for name in FS)
     core = lax.axis_index("sp")
     here = 2 * y + x
@@ -379,15 +382,17 @@
     above, below = {"za": z + 1}, {"za": z - 1}
     core_peer = {"sp": 1 - core}
     has_above, has_below = z + 1 < outer, z >= 1
+    loads = []
+    for i, (parts, _, base, of) in enumerate(kinds):
+        width = ins[i].shape[1] // (2 * of)
+        for part in range(parts):
+            column = pl.multiple_of((2 * (base + part) + core) * width, width)
+            span = slice(part * width, (part + 1) * width)
+            loads.append((i, fly.local(ins[i].at[:, pl.ds(column, width)], own[i].at[:, span], i_s.at[i, part])))
+        if parts == 0:
+            loads.append((i, fly.local(ins[i], own[i], i_s.at[i, 0])))
+    mlp_load = fly.local(mlp_in, mlp_ref, i_s.at[full, 0])
     greet((x_peer, y_peer, diagonal, core_peer), ((has_above, above), (has_below, below)))
-
-    for i, (parts, _) in enumerate(kinds):
-        if parts == 0:
-            own[i][...] = ins[i][...]
-        for part in range(parts):
-            width = ins[i].shape[1] // (2 * parts)
-            column = pl.multiple_of((2 * part + core) * width, width)
-            own[i][:, part * width : (part + 1) * width] = ins[i][:, pl.ds(column, width)]
 
     def spot(i, slot, ty, tx):
         if form[i] == HALF_X:
@@ -469,6 +474,9 @@
         landed(outs[i].at[slot, 1 - y, 1 - x], r2.at[i, slot, 1], device)
 
     for i in range(full):
+        for index, load in loads:
+            if index == i:
+                load.wait()
         for way in range(2):
             z_send(i, way, 0, own[i])
         xy_own(i, z, None, own[i])
@@ -476,6 +484,7 @@
 
     fly.send(text_ref, text_out.at[core], t_s.at[0], t_s.at[1], core_peer)
     locals_.append(fly.local(text_ref, text_out.at[core], t_s.at[2]))
+    mlp_load.wait()
     hid = mlp_ref.shape[1] // (outer * PLANE * 2)
     for own_core in range(2):
 
@@ -516,6 +525,14 @@
     for i in (*halves, *(i for i in range(full) if i not in halves)):
         for slot in range(outer):
             xy_end(i, slot)
+        if i == 0:
+            bias_len = bias_out.shape[1] // (outer * PLANE)
+            gain_len = gain_out.shape[1] // (outer * PLANE)
+            for chip in range(outer * PLANE):
+                rows = small_all.at[chip // PLANE, (chip // 2) % 2, chip % 2]
+                bias_out[:, chip * bias_len : (chip + 1) * bias_len] = rows[0:1, :bias_len]
+                gain_out[:, chip * gain_len : (chip + 1) * gain_len] = rows[1:5, :gain_len]
+                step_out[chip : chip + 1, :] = rows[5:6, : step_out.shape[1]]
         if i not in halves:
             continue
         j, part = halves.index(i), outer // 2
@@ -535,19 +552,25 @@
     fly.drain()
 
 
-def gather_weights(outer, kinds, arrays, mlp, text):
+def gather_weights(outer, kinds, arrays, mlp, text, small_lens):
     shapes, own, whole = [], [], []
-    for (parts, form), array in zip(kinds, arrays, strict=True):
+    for (parts, form, _, of), array in zip(kinds, arrays, strict=True):
         rows, width = array.shape
-        half = width // 2 if parts else width
+        half = width * parts // (2 * of) if parts else width
         own.append(pltpu.VMEM((rows, half), array.dtype))
         if form in (HALF_X, HALF_Y):
             shapes.append(jax.ShapeDtypeStruct((outer, 2, rows, half), array.dtype))
         elif form == KEEP:
             whole.append(pltpu.VMEM((outer, 2, 2, rows, half), array.dtype))
-            shapes.append(jax.ShapeDtypeStruct((outer // 2, 2, 2, rows, width), array.dtype))
+            shapes.append(jax.ShapeDtypeStruct((outer // 2, 2, 2, rows, 2 * half), array.dtype))
         else:
             shapes.append(jax.ShapeDtypeStruct((outer, 2, 2, rows, half), array.dtype))
+    bias_len, gain_len, _ = small_lens
+    chips = outer * PLANE
+    shapes[0] = jax.ShapeDtypeStruct((8, 128), F32)
+    shapes.append(jax.ShapeDtypeStruct((1, chips * bias_len), F32))
+    shapes.append(jax.ShapeDtypeStruct((4, chips * gain_len), F32))
+    shapes.append(jax.ShapeDtypeStruct((chips, 128), F32))
     rows, units = mlp.shape
     mine = units // (2 * PLANE)
     shapes.append(jax.ShapeDtypeStruct((outer, PLANE, rows, mine), mlp.dtype))
@@ -558,11 +581,13 @@
     results = pl.pallas_call(
         functools.partial(gather_kernel, outer, kinds),
         out_shape=shapes,
-        in_specs=[VM] * (nf + 2),
-        out_specs=[ANY] * len(shapes),
+        in_specs=[ANY] * (nf + 2),
+        out_specs=[*[ANY] * nf, VM, VM, VM, ANY, ANY],
         scratch_shapes=[
             *own,
             *whole,
+            pltpu.VMEM((outer, 2, 2, *arrays[0].shape), F32),
+            pltpu.VMEM(mlp.shape, mlp.dtype),
             pltpu.VMEM((PLANE, rows, mine), mlp.dtype),
             dma((nf + 1,)),
             dma((nf + 1, 2, hops)),
@@ -577,6 +602,7 @@
             dma((nh,)),
             dma((nh,)),
             dma((3,)),
+            dma((nf + 1, 3)),
         ],
         compiler_params=pltpu.CompilerParams(
             collective_id=0, has_side_effects=True, vmem_limit_bytes=40 * 1024 * 1024
@@ -584,7 +610,9 @@
         cost_estimate=pl.CostEstimate(flops=10**11, bytes_accessed=10**8, transcendentals=0),
         name="gather_weights",
     )(*arrays, mlp, text)
-    return [value.reshape(-1, value.shape[-1]) if value.ndim != 4 or i >= nf else value for i, value in enumerate(results)]
+    flat = [value.reshape(-1, value.shape[-1]) if value.ndim == 5 else value for value in results[1:nf]]
+    bias, gains, steps, up, texts = results[nf:]
+    return flat, bias, gains, steps, up.reshape(-1, up.shape[-1]), texts.reshape(-1, texts.shape[-1])
 
 
 def plane_gather_kernel(own_ref, out_ref, local_sem, send, recv):
@@ -828,8 +856,8 @@
 
             @pl.when(core == side)
             def _(side=side):
-                down_out[side * hid : (side + 1) * hid, :] = down_ref[...].astype(F32)
-                down_out[(1 - side) * hid : (2 - side) * hid, :] = down_in[...].astype(F32)
+                down_out[side * hid : (side + 1) * hid, :] = down_ref[...]
+                down_out[(1 - side) * hid : (2 - side) * hid, :] = down_in[...]
 
     def feed_forward_rows():
         hid = down_ref.shape[0]
@@ -838,7 +866,7 @@
             for place in range(PLANE):
                 for side in range(2):
                     column = ((slot * PLANE + place) * 2 + side) * hid
-                    up_out[:, column : column + hid] = up_in[side, place, :, slot * hid : (slot + 1) * hid].astype(F32)
+                    up_out[:, column : column + hid] = up_in[side, place, :, slot * hid : (slot + 1) * hid]
 
     def slot_at(step):
         if step == outer - 1:
@@ -926,7 +954,7 @@
             at = pl.ds(pl.multiple_of(index * step, step), step)
             upper = jnp.where(has_above, chain[p][slot, at, :].astype(F32), 0.0)
             lower = jnp.where(has_below, chain[p][slot + 1, at, :].astype(F32), 0.0)
-            outs[i][at, pl.ds(column, width)] = plane[p][slot, at, :].astype(F32) + upper + lower
+            outs[i][at, pl.ds(column, width)] = (plane[p][slot, at, :].astype(F32) + upper + lower).astype(BF)
             return carry
 
         lax.fori_loop(0, rows // step, chunk, 0)
@@ -991,7 +1019,7 @@
             grad = grad.reshape(lead, 2, 2, -1, grad.shape[-1])
         rows, width = grad.shape[-2], full_width // parts
         shaped.append(grad)
-        shapes.append(jax.ShapeDtypeStruct((rows, 2 * full_width), F32))
+        shapes.append(jax.ShapeDtypeStruct((rows, 2 * full_width), BF))
         for _ in range(parts):
             if form in (PLAIN, SPLIT):
                 near.append(pltpu.VMEM((outer, 2, rows, width), BF))
@@ -1001,8 +1029,8 @@
             whole.append(pltpu.VMEM((outer, 2, 2, rows, full_width), BF))
     shapes.append(jax.ShapeDtypeStruct((shards, 2, *frames.shape), frames.dtype))
     shapes.append(jax.ShapeDtypeStruct(small.shape[1:], F32))
-    shapes.append(jax.ShapeDtypeStruct((up.shape[1], 2 * PLANE * up.shape[2]), F32))
-    shapes.append(jax.ShapeDtypeStruct((2 * down.shape[0], down.shape[1]), F32))
+    shapes.append(jax.ShapeDtypeStruct((up.shape[1], 2 * PLANE * up.shape[2]), BF))
+    shapes.append(jax.ShapeDtypeStruct((2 * down.shape[0], down.shape[1]), BF))
     dma = pltpu.SemaphoreType.DMA
     count, total, nsplit = len(kinds), len(plane), len(whole)
     results = pl.pallas_call(
@@ -1054,7 +1082,8 @@
     fly = Flights()
     greet((core_peer,))
     frames, width = out_ref.shape[0], matrix_ref.shape[1]
-    half[...] = product(sinus_ref[...], matrix_ref[...]) + bias_ref[...]
+    mine = pl.ds(pl.multiple_of(core * width, width), width)
+    half[...] = product(sinus_ref[...], matrix_ref[...]) + bias_ref[:, mine]
     for side in range(2):
 
         @pl.when(core == side)
@@ -1109,7 +1138,6 @@
     mlp_out,
     cotangent,
 ):
-    half = D // 2
     row_count = tokens.shape[0]
     frame_count = row_count // FRAME_TOK
     group_frames = timestep.shape[1]
@@ -1126,43 +1154,36 @@
     small_width = -(-(small_len + group_frames) // (small_rows * 128)) * 128
     small_room = small_rows * small_width
 
-    small = jnp.concatenate(
+    small_own = jnp.zeros((8, -(-max(bias_len, 128) // 128) * 128), F32)
+    small_own = small_own.at[0, :bias_len].set(mod_bias[0].astype(F32))
+    small_own = small_own.at[1:5, :gain_len].set(qk_gains[0].astype(F32))
+    small_own = small_own.at[5, :group_frames].set(timestep[0].astype(F32))
+    weights, bias_all, gain_all, steps_all, up_matrix, text_all = gather_weights(
+        outer,
+        (
+            (0, ALL_CHIPS, 0, 1),
+            (1, ALL_CHIPS, 0, 1),
+            (3, ALL_CHIPS, 0, 3),
+            (1, KEEP, 0, 1),
+            (1, HALF_Y, 0, 1),
+            (1, HALF_X, 0, 2),
+            (1, HALF_Y, 1, 2),
+            (1, KEEP, 0, 1),
+        ),
         [
-            mod_bias[0].astype(F32),
-            qk_gains[0].reshape(-1).astype(F32),
-            timestep[0].astype(F32),
-            jnp.zeros((small_room - small_len - group_frames,), F32),
-        ]
-    ).reshape(small_rows, small_width)
-    gathered = gather_weights(
-        outer,
-        ((0, ALL_CHIPS), (1, ALL_CHIPS), (3, ALL_CHIPS), (1, KEEP), (1, ALL_CHIPS), (1, HALF_X), (1, HALF_Y), (1, KEEP)),
-        [
-            small,
-            *(w[0] for w in (mod_weight, self_in, self_out, cross_q)),
-            cross_kv[0, :, :D],
-            cross_kv[0, :, D:],
-            cross_out[0],
+            small_own,
+            *(w[0] for w in (mod_weight, self_in, self_out, cross_q, cross_kv, cross_kv, cross_out)),
         ],
         mlp_in[0],
         text,
+        (bias_len, gain_len, group_frames),
     )
-    small_all, mod_matrix, self_proj, self_back, cross_qproj, k_half, v_half, cross_back = gathered[:8]
-    up_matrix, text_all = gathered[8:]
+    mod_matrix, self_proj, self_back, q_half, k_half, v_half, cross_back = weights
     hid = mlp_out.shape[1] // 2
     down_part = lax.dynamic_slice_in_dim(mlp_out[0], core * hid, hid, 0)
-    down_part, small_all = lax.optimization_barrier((down_part, small_all))
+    down_part, bias_all = lax.optimization_barrier((down_part, bias_all))
     down_matrix = gather(down_part, "za")
-    small_all = small_all.reshape(shards, small_room)
-    bias_all = small_all[:, :bias_len].reshape(-1)
-    gain_all = (
-        small_all[:, bias_len:small_len]
-        .reshape(shards, 4, gain_len)
-        .transpose(1, 0, 2)
-        .reshape(4, 2, half)
-    )
-    gain_own = lax.dynamic_index_in_dim(gain_all, core, 1, keepdims=False)
-    steps_all = small_all[:, small_len : small_len + group_frames].reshape(-1)
+    steps_all = steps_all[:, :group_frames].reshape(-1)
 
     live_keys = clip_frames * FRAME_TOK
     all_keys = jnp.full((1,), TXT, jnp.int32)
@@ -1170,8 +1191,7 @@
     cosine, sine = (jnp.asarray(table) for table in rotary_tables(group_frames))
     sinus = sinus_features(timestep[0]).astype(BF)
 
-    bias_half = lax.dynamic_slice_in_dim(bias_all, core * 3 * D, 3 * D)[None]
-    modulation = modulate(sinus, mod_matrix, bias_half)
+    modulation = modulate(sinus, mod_matrix, bias_all)
     shift_one, scale_one, gate_one, shift_two, scale_two, gate_two = jnp.split(
         modulation, 6, axis=1
     )
@@ -1181,12 +1201,13 @@
     place_y, place_x = lax.axis_index("yb"), lax.axis_index("xc")
     k_other = lax.ppermute(k_half, "yb", exchange)
     v_other = lax.ppermute(v_half, "xc", exchange)
+    q_other = lax.ppermute(q_half, "xc", exchange)
     residual = tokens.astype(F32)
     attn_float, back_attn_input = jax.vjp(modulated, residual, shift_one, scale_one)
     attn_input = gather(attn_float.astype(BF), "sp")
     joined = product(attn_input, self_proj)
     self_mixed, self_lse, *self_kept = attend_forward(
-        live_keys, [joined], gain_own[:2], cosine, sine, True, 5
+        live_keys, [joined], gain_all, cosine, sine, True, 5
     )
     grad_branch, self_mixed = lax.optimization_barrier((grad_branch, self_mixed))
     beside = [
@@ -1205,12 +1226,13 @@
     cross_kvproj = jnp.concatenate(
         [beside_own(k_half, k_other, place_y, 1), beside_own(v_half, v_other, place_x, 2)], axis=1
     )
+    cross_qproj = beside_own(q_half, q_other, place_x, 2)
     text_raw = product(text_all, cross_kvproj)
     cross_float, back_cross_norm = jax.vjp(layer_norm, residual)
     cross_input = gather(cross_float.astype(BF), "sp")
     cross_raw = product(cross_input, cross_qproj)
     cross_mixed, cross_lse, *cross_kept = attend_forward(
-        all_keys, [cross_raw, text_raw], gain_own[2:], cosine, sine, False, 6
+        all_keys, [cross_raw, text_raw], gain_all, cosine, sine, False, 6
     )
     cross_branch = pair_sum(product(cross_mixed, cross_back))
     residual = residual + cross_branch
@@ -1248,7 +1270,7 @@
     grad_cross_mixed = product_nt(grad_low, cross_back).astype(BF)
     cross_saved = [*cross_kept[:2], cross_lse, *cross_kept[2:]]
     grad_cross_low, grad_text_low, gains_cross = attend_backward(
-        all_keys, [cross_raw, text_raw], gain_own[2:], cosine, sine, False, 7, cross_saved, grad_cross_mixed
+        all_keys, [cross_raw, text_raw], gain_all, cosine, sine, False, 7, cross_saved, grad_cross_mixed
     )
     grad_cross_qproj = product_tn(cross_input, grad_cross_low).astype(BF)
     grad_cross_kvproj = product_tn(text_all, grad_text_low).astype(BF)
@@ -1265,7 +1287,7 @@
     grad_self_mixed = product_nt(grad_self_low, self_back).astype(BF)
     self_saved = [*self_kept[:2], self_lse, *self_kept[2:]]
     grad_joined_low, gains_self = attend_backward(
-        live_keys, [joined], gain_own[:2], cosine, sine, True, 8, self_saved, grad_self_mixed
+        live_keys, [joined], gain_all, cosine, sine, True, 8, self_saved, grad_self_mixed
     )
     grad_self_proj = product_tn(attn_input, grad_joined_low).astype(BF)
     grad_attn_input = pair_sum(product_nt(grad_joined_low, self_proj))
@@ -1298,7 +1320,8 @@
         up_owned.reshape(PLANE, -1, up_owned.shape[1]),
         down_owned,
     )
-    cross_q_grad, cross_kv_grad, cross_out_grad, self_out_grad, self_in_grad = owned
+    owned = [rows.astype(F32) for rows in (*owned, mlp_in_grad, mlp_out_grad)]
+    cross_q_grad, cross_kv_grad, cross_out_grad, self_out_grad, self_in_grad, mlp_in_grad, mlp_out_grad = owned
     small_owned = small_owned.reshape(-1)[:small_len]
     sinus_all = sinus_features(steps_all).astype(BF)
     own_features = mod_weight.shape[1]

time: 755 us -> 750 us (level)
  local copies, waits for them, and re-layouts: 67 us -> 42.1 us
  waiting for transfers between devices: 59.8 us -> 73.3 us
  other arithmetic: 48.7 us -> 58.2 us
  Pallas kernels: 440 us -> 432 us
    ppermute x1, waiting for transfers between devices: 24.6 us -> 0.01 us  [body(): k_other = lax.ppermute(k_half, 'yb', exchange)]
    ppermute x1, waiting for transfers between devices: 0.01 us -> 22.4 us  [body(): v_other = lax.ppermute(v_half, 'xc', exchange)]
    ppermute x0 -> x1, waiting for transfers between devices: none -> 17.9 us  [body(): q_other = lax.ppermute(q_half, 'xc', exchange)]
    unnamed x188 -> x195, local copies, waits for them, and re-layouts: 39.6 us -> 29 us
    broadcast_in_dim x0 -> x6, other arithmetic: none -> 8.69 us  [the longest x1 2.22 us: body(): mlp_out_grad[None]]
  transfers between devices with their start and end apart: 11 -> 12, of which waited for: 3 -> 4; matrix products, arithmetic and copies ran while one was open for 16% -> 16% of each run, Pallas kernels for 14% -> 14%
where the time goes in v7:
time: 750 us; the launch traced here: 736 us
  Pallas kernels  432 us (58%)
  matrix products  96.1 us (13%)
  waiting for transfers between devices  73.3 us (10%)
  other arithmetic  58.2 us (8%)
  local copies, waits for them, and re-layouts  42.1 us (6%)
  between operations  15.9 us (2%)
  blocking collectives  10.1 us (1%)
  starting transfers between devices  8.29 us (1%)
    pallas_call x1, Pallas kernels, gather_weights(): pl.pallas_call(functools.partial(gather_kernel, outer, kinds), out_shape=...  162 us
    pallas_call x1, Pallas kernels, reduce_weights(): pl.pallas_call(functools.partial(reduce_kernel, outer, kinds), out_shape=...  157 us
    dot_general x7, matrix products, product(): return jnp.dot(left, right, preferred_element_type=F32)  37.3 us
    pallas_call x1, Pallas kernels, plane_sum(): pl.pallas_call(plane_sum_kernel, out_shape=(shape, shape), in_specs=[VM,...  35 us
    pallas_call x4, Pallas kernels, attend_call(): pl.pallas_call(functools.partial(kernel, joint, rotary, 0 if rotary else...  34.3 us
    dot_general x6, matrix products, product_nt(): lax.dot_general(left, right, (((1,), (1,)), ((), ())), preferred_element_...  31.6 us
    unnamed x195, local copies, waits for them, and re-layouts  29 us
    dot_general x8, matrix products, product_tn(): lax.dot_general(left, right, (((0,), (0,)), ((), ())), preferred_element_...  27.3 us
  transfers between devices with their start and end apart: 12, of which 4 were waited for; matrix products, arithmetic and copies ran while one was open for 16% of the time, Pallas kernels for 14%

profile of v7, /device:TPU:0, one launch (start us, length us, event | category | flops | bytes accessed | tf_op | source)
XLA Modules:
  0.0 736.3 jit_solution(7411293855618417136)
XLA Ops:
  26.0 162.5 %gather_weights.1 = (f32[8,128]{1,0:T(8,128)}, bf16[4,2,2,16,4608]{4,3,2,1,0:T(8,128)(2,1)S(1)}, bf16[4,2,2,96,2304]{4,3,2,1,0:T(8,128)(2,1)}, bf16[2,2,2,96,153...) custom-call(f32[8,640]{1,0:T(8,128)S(1)} %copy-done.2, ...), custom_call_target="tpu_custom_call" | custom-call | flops 99999997952 | bytes 100000000 | tf_op jit(solution)/shard_map/gather_weights/pallas_call | solution.py:581
  203.2 6.5 fusion.48.refs_0_
  209.7 7.4 %shard_map.256 = (bf16[256,768]{1,0:T(8,128)(2,1)}, f32[256,768]{1,0:T(8,128)}, bf16[256,768]{1,0:T(8,128)(2,1)}, bf16[256,768]{1,0:T(8,128)(2,1)}, f32[256,128]{1,0:T(8,128)}, /*index=5*/f32[256,128]{1,0:T(8,128)}) custom-call(s32[1]{0:T(128)S(6)} %mul.297.live_ref, f32[256,2304]{1,0:T(8,128)} %fusion.48.refs_0_, f32[4,1536]{1,0:T(4,128)} %copy-done, ...), custom_call_target="tpu_custom_call" | custom-call | flops 201326592 | bytes 4874240 | tf_op jit(solution)/shard_map/pallas_call | solution.py:306
  226.6 4.7 pair_sum.4
  237.8 17.9 %collective-permute-done = bf16[4,2,96,768]{3,2,1,0:T(8,128)(2,1)} collective-permute-done((bf16[4,2,96,768]{3,2,1,0:T(8,128)(2,1)S(1)}, bf16[4,2,96,768]{3,2,1,0:T(8,128)(2,1)}, u32[]{:S(2)}, u32[]{:S(2)}) %collective-permute-start) | collective-permute-done | bytes 1179680 | tf_op jit(solution)/shard_map/ppermute | solution.py:1204
  258.5 22.4 %collective-permute-done.2 = bf16[4,2,96,768]{3,2,1,0:T(8,128)(2,1)} collective-permute-done((bf16[4,2,96,768]{3,2,1,0:T(8,128)(2,1)S(1)}, bf16[4,2,96,768]{3,2,1,0:T(8,128)(2,1)}, u32[]{:S(2)}, u32[]{:S(2)}) %collective-permute-start.2) | collective-permute-done | bytes 1179680 | tf_op jit(solution)/shard_map/ppermute | solution.py:1203
  292.7 8.5 %shard_map.257 = (bf16[256,768]{1,0:T(8,128)(2,1)}, f32[256,768]{1,0:T(8,128)}, bf16[256,768]{1,0:T(8,128)(2,1)}, bf16[512,768]{1,0:T(8,128)(2,1)}, f32[256,128]{1,0:T(8,128)}, /*index=5*/f32[512,128]{1,0:T(8,128)}) custom-call(s32[1]{0:T(128)} %constant.159.clone.1.live_ref, f32[256,768]{1,0:T(8,128)} %fusion.50.refs_0_, f32[512,1536]{1,0:T(8,128)} %fusion.refs_1_, ...), custom_call_target="tpu_custom_call" | custom-call | flops 402653184 | bytes 6971392 | tf_op jit(solution)/shard_map/pallas_call | solution.py:306
  304.9 4.8 pair_sum.5
  316.5 20.1 %plane_gather.1 = bf16[2,2,2,128,1536]{4,3,2,1,0:T(8,128)(2,1)} custom-call(bf16[128,1536]{1,0:T(8,128)(2,1)} %get-tuple-element.162.own_ref), custom_call_target="tpu_custom_call" | custom-call | flops 10000000000 | bytes 10000000 | tf_op jit(solution)/shard_map/plane_gather/pallas_call | solution.py:658
  336.7 7.0 fusion.52
  348.4 5.5 convolution_convert_fusion.2
  353.9 10.5 %fusion.10 = bf16[1024,1120]{0,1:T(8,128)(2,1)S(1)} fusion(f32[1024,1120]{0,1:T(8,128)} %copy-done.91, bf16[1024,1536]{1,0:T(8,128)(2,1)} %bitcast.235, bf16[1120,1536]{1,0:T(8,128)(2,1)} %all-gather.2.cloned.1.call-done), kind=kOutput, calls=%fused_computation.17 | convolution fusion | flops 3546152960 | bytes 13467648 | tf_op jit(solution)/shard_map/dot_general | solution.py:43
  364.4 6.0 convolution_convert_fusion.4
  370.4 5.1 convolution_convert_fusion.1
  377.9 10.3 %convolution_convert_fusion.5 = bf16[1024,1536]{1,0:T(8,128)(2,1)} fusion(bf16[1120,1536]{1,0:T(8,128)(2,1)} %all-gather.2.cloned.1.call-done, f32[1024,1120]{0,1:T(8,128)} %copy-done.91), kind=kOutput, calls=%fused_computation.20 | convolution fusion | flops 3535110144 | bytes 11173888 | tf_op jit(solution)/shard_map/dot_general | solution.py:35
  388.3 35.0 %plane_sum.1 = (f32[128,1536]{1,0:T(8,128)}, f32[128,1536]{1,0:T(8,128)}) custom-call(bf16[2,2,2,128,1536]{4,3,2,1,0:T(8,128)(2,1)} %bitcast.260, bf16[2,2,2,128,1536]{4,3,2,1,0:T(8,128)(2,1)} %bitcast.257), custom_call_target="tpu_custom_call" | custom-call | flops 10000000000 | bytes 10000000 | tf_op jit(solution)/shard_map/plane_sum/pallas_call | solution.py:717
  433.2 10.2 %shard_map.258 = (bf16[256,768]{1,0:T(8,128)(2,1)}, bf16[512,1536]{1,0:T(8,128)(2,1)}, f32[8,768]{1,0:T(8,128)}) custom-call(s32[1]{0:T(128)} %constant.159.clone.1.live_ref, f32[256,768]{1,0:T(8,128)} %fusion.50.refs_0_, f32[512,1536]{1,0:T(8,128)} %fusion.refs_1_, f32[4,1536]{1,0:T(4,128)} %copy-done, f32[256,128]{1,0:T(8,128)} %constant.173.clone.refs_2_.refs_3_, ...), custom_call_target="tpu_custom_call" | custom-call | flops 1006632960 | bytes 8962048 | tf_op jit(solution)/shard_map/pallas_call | solution.py:306
  456.2 5.7 copy.63
  468.4 8.2 %shard_map.259 = (bf16[256,2304]{1,0:T(8,128)(2,1)}, f32[8,768]{1,0:T(8,128)}) custom-call(s32[1]{0:T(128)S(6)} %mul.297.live_ref, f32[256,2304]{1,0:T(8,128)} %fusion.48.refs_0_, f32[4,1536]{1,0:T(4,128)} %copy-done, f32[256,128]{1,0:T(8,128)} %constant.173.clone.refs_2_.refs_3_, f32[256,128]{1,0:T(8,128)} %constant.174.clone.refs_3_.refs_4_, ...), custom_call_target="tpu_custom_call" | custom-call | flops 503316480 | bytes 6078464 | tf_op jit(solution)/shard_map/pallas_call | solution.py:306
  476.6 6.5 fusion.54.part_ref
  516.5 4.9 convolution_convert_fusion
  521.4 15.0 %collective-permute-done.7 = bf16[4,2,96,768]{3,2,1,0:T(8,128)(2,1)S(1)} collective-permute-done((bf16[4,2,96,768]{3,2,1,0:T(8,128)(2,1)S(1)}, bf16[4,2,96,768]{3,2,1,0:T(8,128)(2,1)S(1)}, u32[]{:S(2)}, u32[]{:S(2)}) %collective-permute-start.7) | collective-permute-done | bytes 1179680 | tf_op jit(solution)/shard_map/ppermute | solution.py:1280
  537.5 17.9 %collective-permute-done.8 = bf16[4,2,96,1536]{3,2,1,0:T(8,128)(2,1)} collective-permute-done((bf16[4,2,96,1536]{3,2,1,0:T(8,128)(2,1)}, bf16[4,2,96,1536]{3,2,1,0:T(8,128)(2,1)}, u32[]{:S(2)}, u32[]{:S(2)}) %collective-permute-start.8) | collective-permute-done | bytes 2359328 | tf_op jit(solution)/shard_map/ppermute | solution.py:1279
  558.8 157.2 %reduce_weights.1 = (bf16[96,1536]{1,0:T(8,128)(2,1)}, bf16[96,3072]{1,0:T(8,128)(2,1)}, bf16[96,1536]{1,0:T(8,128)(2,1)}, bf16[96,1536]{1,0:T(8,128)(2,1)}, bf1...) custom-call(bf16[4,2,96,768]{3,2,1,0:T(8,128)(2,1)} %bitcast_add_fus, ...), custom_call_target="tpu_custom_call" | custom-call | flops 99999997952 | bytes 100000000 | tf_op jit(solution)/shard_map/reduce_weights/pallas_call | solution.py:1036
  (326 shorter events, 160.5 us)
Async XLA Ops:
  7.2 346.7 %all-gather.2.cloned.1.call-start = ((), (), s32[]{:S(2)}) async-start(), calls=%async_computation.2 | async-start | bytes 4300800 | tf_op jit(solution)/shard_map/all_gather | solution.py:1117
  10.8 187.8 %copy-start.66 = (f32[128]{0:T(128)}, f32[128]{0:T(128)S(1)}, u32[]{:S(2)}) copy-start(f32[128]{0:T(128)S(1)} %fusion.35) | copy-start | bytes 1540
  26.0 166.3 %copy-start.76 = (f32[128]{0:T(128)S(1)}, f32[128]{0:T(128)}, u32[]{:S(2)}) copy-start(f32[128]{0:T(128)} %multiply_exponential_fusion) | copy-start | bytes 1540
  26.0 166.3 %copy-start.88 = (f32[4]{0:T(128)S(1)}, f32[4]{0:T(128)}, u32[]{:S(2)}) copy-start(f32[4]{0:T(128)} %get-tuple-element.182) | copy-start | bytes 52
  217.2 93.8 %collective-permute-start.5 = (bf16[128,1536]{1,0:T(8,128)(2,1)}, bf16[128,1536]{1,0:T(8,128)(2,1)}, u32[]{:S(2)}, u32[]{:S(2)}) collective-permute-start(bf16[128,1536]{1,0:T(8,128)(2,1)} %fusion.17), channel_id=1, source_target_pairs={{0,6},{2,4},{4,2},{6,0},{1,7},{3,5},{5,3},{7,1},{8,14},{10,12},{12... | collective-permute-start | bytes 1179656 | tf_op jit(solution)/shard_map/ppermute | solution.py:1217
  218.7 92.3 %collective-permute-start.4 = (bf16[128,1536]{1,0:T(8,128)(2,1)}, bf16[128,1536]{1,0:T(8,128)(2,1)}, u32[]{:S(2)}, u32[]{:S(2)}) collective-permute-start(bf16[128,1536]{1,0:T(8,128)(2,1)} %fusion.17), channel_id=1, source_target_pairs={{0,4},{4,0},{1,5},{5,1},{2,6},{6,2},{3,7},{7,3},{8,12},{12,8},{9,1... | collective-permute-start | bytes 1179656 | tf_op jit(solution)/shard_map/ppermute | solution.py:1216
  220.2 338.6 %reduce-scatter.5.cloned.1.call-start = ((), (), s32[]{:S(2)}) async-start(), calls=%async_computation.3 | async-start | bytes 4300800 | tf_op jit(solution)/shard_map/reduce_scatter | solution.py:1121
  220.3 35.4 %collective-permute-start = (bf16[4,2,96,768]{3,2,1,0:T(8,128)(2,1)S(1)}, bf16[4,2,96,768]{3,2,1,0:T(8,128)(2,1)}, u32[]{:S(2)}, u32[]{:S(2)}) collective-permute-start(bf16[4,2,96,768]{3,2,1,0:T(8,128)(2,1)S(1)} %get-tuple-element.108), channel_id=1, source_target_pairs={{0,2},{2,0},{1,3},{3,1},{4,6},{6,4},{5,7},{7,5},{8,10},{10,8},{9,1... | collective-permute-start | bytes 3538952 | tf_op jit(solution)/shard_map/ppermute | solution.py:1204
  220.9 63.7 %collective-permute-start.1 = (bf16[4,2,96,768]{3,2,1,0:T(8,128)(2,1)S(1)}, bf16[4,2,96,768]{3,2,1,0:T(8,128)(2,1)}, u32[]{:S(2)}, u32[]{:S(2)}) collective-permute-start(bf16[4,2,96,768]{3,2,1,0:T(8,128)(2,1)S(1)} %get-tuple-element.110), channel_id=1, source_target_pairs={{0,4},{4,0},{1,5},{5,1},{2,6},{6,2},{3,7},{7,3},{8,12},{12,8},{9,1... | collective-permute-start | bytes 3538952 | tf_op jit(solution)/shard_map/ppermute | solution.py:1202
  222.2 58.7 %collective-permute-start.2 = (bf16[4,2,96,768]{3,2,1,0:T(8,128)(2,1)S(1)}, bf16[4,2,96,768]{3,2,1,0:T(8,128)(2,1)}, u32[]{:S(2)}, u32[]{:S(2)}) collective-permute-start(bf16[4,2,96,768]{3,2,1,0:T(8,128)(2,1)S(1)} %get-tuple-element.111), channel_id=1, source_target_pairs={{0,2},{2,0},{1,3},{3,1},{4,6},{6,4},{5,7},{7,5},{8,10},{10,8},{9,1... | collective-permute-start | bytes 3538952 | tf_op jit(solution)/shard_map/ppermute | solution.py:1203
  232.8 25.5 %copy-start.71 = (f32[128]{0:T(128)}, f32[128]{0:T(128)S(1)}, u32[]{:S(2)}) copy-start(f32[128]{0:T(128)S(1)} %broadcast_multiply_fusion.1) | copy-start | bytes 1540
  237.8 45.1 %copy-start.29 = (bf16[256,1536]{1,0:T(8,128)(2,1)}, bf16[256,1536]{1,0:T(8,128)(2,1)S(1)}, u32[]{:S(2)}) copy-start(bf16[256,1536]{1,0:T(8,128)(2,1)S(1)} %all_gather.16) | copy-start | bytes 2359300
  255.7 55.3 %collective-permute-start.3 = (bf16[128,1536]{1,0:T(8,128)(2,1)}, bf16[128,1536]{1,0:T(8,128)(2,1)}, u32[]{:S(2)}, u32[]{:S(2)}) collective-permute-start(bf16[128,1536]{1,0:T(8,128)(2,1)} %fusion.17), channel_id=1, source_target_pairs={{0,2},{2,0},{1,3},{3,1},{4,6},{6,4},{5,7},{7,5},{8,10},{10,8},{9,1... | collective-permute-start | bytes 1179656 | tf_op jit(solution)/shard_map/ppermute | solution.py:1215
  258.5 28.5 %copy-start.19 = (bf16[4,2,2,96,768]{4,3,2,1,0:T(8,128)(2,1)}, bf16[4,2,2,96,768]{4,3,2,1,0:T(8,128)(2,1)S(1)}, u32[]{:S(2)}) copy-start(bf16[4,2,2,96,768]{4,3,2,1,0:T(8,128)(2,1)S(1)} %copy.53) | copy-start | bytes 7077892
  314.1 29.6 %collective-permute-start.6 = (bf16[4,128,1536]{2,1,0:T(8,128)(2,1)}, bf16[4,128,1536]{2,1,0:T(8,128)(2,1)}, u32[]{:S(2)}, u32[]{:S(2)}) collective-permute-start(bf16[4,128,1536]{2,1,0:T(8,128)(2,1)} %get-tuple-element.167), channel_id=1, source_target_pairs={{0,1},{1,0},{2,3},{3,2},{4,5},{5,4},{6,7},{7,6},{8,9},{9,8},{10,11... | collective-permute-start | bytes 4718600 | tf_op jit(solution)/shard_map/ppermute | solution.py:1241
  314.3 22.3 %copy-start.70 = (f32[128]{0:T(128)}, f32[128]{0:T(128)S(1)}, u32[]{:S(2)}) copy-start(f32[128]{0:T(128)S(1)} %broadcast_multiply_fusion) | copy-start | bytes 1540
  314.6 22.1 %copy-start.85 = (f32[128]{0:T(128)}, f32[128]{0:T(128)S(1)}, u32[]{:S(2)}) copy-start(f32[128]{0:T(128)S(1)} %multiply_reduce_fusion.2) | copy-start | bytes 1540
  314.6 22.1 %copy-start.73 = (f32[128]{0:T(128)}, f32[128]{0:T(128)S(1)}, u32[]{:S(2)}) copy-start(f32[128]{0:T(128)S(1)} %fusion.37) | copy-start | bytes 1540
  375.6 183.3 %reduce-scatter.7.cloned.1.call-start = ((), (), s32[]{:S(2)}) async-start(), calls=%async_computation.4 | async-start | bytes 4423680 | tf_op jit(solution)/shard_map/reduce_scatter | solution.py:1121
  388.3 35.0 %copy-start.54 = (f32[2,1536]{1,0:T(2,128)S(1)}, f32[2,1536]{1,0:T(2,128)}, u32[]{:S(2)}) copy-start(f32[2,1536]{1,0:T(2,128)} %get-tuple-element.171) | copy-start | bytes 36868
  501.8 53.7 %collective-permute-start.8 = (bf16[4,2,96,1536]{3,2,1,0:T(8,128)(2,1)}, bf16[4,2,96,1536]{3,2,1,0:T(8,128)(2,1)}, u32[]{:S(2)}, u32[]{:S(2)}) collective-permute-start(bf16[4,2,96,1536]{3,2,1,0:T(8,128)(2,1)} %dynamic-slice_bitcast_fusion), channel_id=1, source_target_pairs={{0,4},{4,0},{1,5},{5,1},{2,6},{6,2},{3,7},{7,3},{8,12},{12,8},{9,1... | collective-permute-start | bytes 7077896 | tf_op jit(solution)/shard_map/ppermute | solution.py:1279
  508.3 28.1 %collective-permute-start.7 = (bf16[4,2,96,768]{3,2,1,0:T(8,128)(2,1)S(1)}, bf16[4,2,96,768]{3,2,1,0:T(8,128)(2,1)S(1)}, u32[]{:S(2)}, u32[]{:S(2)}) collective-permute-start(bf16[4,2,96,768]{3,2,1,0:T(8,128)(2,1)S(1)} %dynamic-slice_bitcast_fusion.1), channel_id=1, source_target_pairs={{0,2},{2,0},{1,3},{3,1},{4,6},{6,4},{5,7},{7,5},{8,10},{10,8},{9,1... | collective-permute-start | bytes 3538952 | tf_op jit(solution)/shard_map/ppermute | solution.py:1280
  514.2 41.2 %slice-start = ((s8[4718592]{0:T(1024)(128)(4,1)}), s8[4194304]{0:T(1024)(128)(4,1)S(1)}, s32[]{:S(2)}) async-start(s8[4718592]{0:T(1024)(128)(4,1)} %bitcast.231), calls=%async_computation.5 | async-start | bytes 8388608
  516.5 39.0 %slice-start.1 = ((s8[4718592]{0:T(1024)(128)(4,1)}), s8[524288]{0:T(1024)(128)(4,1)S(1)}, s32[]{:S(2)}) async-start(s8[4718592]{0:T(1024)(128)(4,1)} %bitcast.231), calls=%async_computation.6 | async-start | bytes 1048576
  (82 other events, 256.4 us)
Sparse Core Ops, SparseCore 0:
  220.3 66.4 all-gather.1
  375.7 63.2 reduce-scatter.4
  468.5 64.7 reduce-scatter.6

commit v8 on v7

--- a/solution.py
+++ b/solution.py
@@ -7,6 +7,7 @@
 from jax import lax
 from jax.experimental import pallas as pl
 from jax.experimental.pallas import tpu as pltpu
+from jax.experimental.layout import Layout, with_layout_constraint
 from jax.sharding import Mesh
 from jax.sharding import PartitionSpec as P
 
@@ -605,7 +606,7 @@
             dma((nf + 1, 3)),
         ],
         compiler_params=pltpu.CompilerParams(
-            collective_id=0, has_side_effects=True, vmem_limit_bytes=40 * 1024 * 1024
+            collective_id=0, has_side_effects=True, vmem_limit_bytes=63 * 1024 * 1024
         ),
         cost_estimate=pl.CostEstimate(flops=10**11, bytes_accessed=10**8, transcendentals=0),
         name="gather_weights",
@@ -764,7 +765,7 @@
     )(partial.reshape(2, rows, width))
 
 
-AHEAD, LAG_PLANE, LAG_CHAIN = 6, 2, 4
+AHEAD, LAG_PLANE, LAG_CHAIN = 14, 4, 6
 PLAIN, SPLIT, OVER_X, OVER_Y = range(4)
 
 
@@ -1254,7 +1255,7 @@
     grad_rows = cotangent.astype(F32)
     grad_down = product_tn(activated, grad_branch_all).astype(BF)
     grad_up_low = back_gelu(product_nt(grad_branch_all, down_matrix))[0].astype(BF)
-    grad_up = product_tn(mlp_input, grad_up_low).astype(BF)
+    grad_up = with_layout_constraint(product_tn(mlp_input, grad_up_low).astype(BF), Layout(major_to_minor=(0, 1)))
     grad_mlp_part = product_nt(grad_up_low, up_matrix).astype(BF)
     grad_mlp_part, grad_up, grad_down = lax.optimization_barrier((grad_mlp_part, grad_up, grad_down))
     down_owned = scatter(grad_down, "za")

time: 750 us -> 726 us (0.968)
  local copies, waits for them, and re-layouts: 42.1 us -> 19.9 us
    unnamed x195 -> x144, local copies, waits for them, and re-layouts: 29 us -> 6.44 us
where the time goes in v8:
time: 726 us; the launch traced here: 717 us
  Pallas kernels  433 us (60%)
  matrix products  98.3 us (14%)
  waiting for transfers between devices  77.7 us (11%)
  other arithmetic  54.8 us (8%)
  local copies, waits for them, and re-layouts  19.9 us (3%)
  between operations  15.6 us (2%)
  blocking collectives  9.98 us (1%)
  starting transfers between devices  8.05 us (1%)
    pallas_call x1, Pallas kernels, gather_weights(): pl.pallas_call(functools.partial(gather_kernel, outer, kinds), out_shape=...  163 us
    pallas_call x1, Pallas kernels, reduce_weights(): pl.pallas_call(functools.partial(reduce_kernel, outer, kinds), out_shape=...  158 us
    dot_general x7, matrix products, product(): return jnp.dot(left, right, preferred_element_type=F32)  37.3 us
    pallas_call x1, Pallas kernels, plane_sum(): pl.pallas_call(plane_sum_kernel, out_shape=(shape, shape), in_specs=[VM,...  35.1 us
    pallas_call x4, Pallas kernels, attend_call(): pl.pallas_call(functools.partial(kernel, joint, rotary, 0 if rotary else...  34.8 us
    dot_general x6, matrix products, product_nt(): lax.dot_general(left, right, (((1,), (1,)), ((), ())), preferred_element_...  31.9 us
    dot_general x8, matrix products, product_tn(): lax.dot_general(left, right, (((0,), (0,)), ((), ())), preferred_element_...  29.1 us
    ppermute x1, waiting for transfers between devices, body(): v_other = lax.ppermute(v_half, 'xc', exchange)  21.6 us
  transfers between devices with their start and end apart: 12, of which 4 were waited for; matrix products, arithmetic and copies ran while one was open for 16% of the time, Pallas kernels for 14%

profile of v8, /device:TPU:0, one launch (start us, length us, event | category | flops | bytes accessed | tf_op | source)
XLA Modules:
  0.0 717.4 jit_solution(14439168876476556303)
XLA Ops:
  16.0 162.5 %gather_weights.1 = (f32[8,128]{1,0:T(8,128)}, bf16[4,2,2,16,4608]{4,3,2,1,0:T(8,128)(2,1)}, bf16[4,2,2,96,2304]{4,3,2,1,0:T(8,128)(2,1)}, bf16[2,2,2,96,1536]{4...) custom-call(f32[8,640]{1,0:T(8,128)} %copy-done.43, ...), custom_call_target="tpu_custom_call" | custom-call | flops 99999997952 | bytes 100000000 | tf_op jit(solution)/shard_map/gather_weights/pallas_call | solution.py:582
  187.7 6.6 fusion.48.refs_0_
  194.4 7.4 %shard_map.256 = (bf16[256,768]{1,0:T(8,128)(2,1)}, f32[256,768]{1,0:T(8,128)}, bf16[256,768]{1,0:T(8,128)(2,1)}, bf16[256,768]{1,0:T(8,128)(2,1)}, f32[256,128]{1,0:T(8,128)}, /*index=5*/f32[256,128]{1,0:T(8,128)}) custom-call(s32[1]{0:T(128)S(6)} %mul.297.live_ref, f32[256,2304]{1,0:T(8,128)} %fusion.48.refs_0_, ...), custom_call_target="tpu_custom_call" | custom-call | flops 201326592 | bytes 4874240 | tf_op jit(solution)/shard_map/pallas_call | solution.py:307
  211.1 4.8 pair_sum.4
  220.4 19.6 %collective-permute-done = bf16[4,2,96,768]{3,2,1,0:T(8,128)(2,1)} collective-permute-done((bf16[4,2,96,768]{3,2,1,0:T(8,128)(2,1)}, bf16[4,2,96,768]{3,2,1,0:T(8,128)(2,1)}, u32[]{:S(2)}, u32[]{:S(2)}) %collective-permute-start) | collective-permute-done | bytes 1179680 | tf_op jit(solution)/shard_map/ppermute | solution.py:1205
  243.6 21.6 %collective-permute-done.2 = bf16[4,2,96,768]{3,2,1,0:T(8,128)(2,1)} collective-permute-done((bf16[4,2,96,768]{3,2,1,0:T(8,128)(2,1)}, bf16[4,2,96,768]{3,2,1,0:T(8,128)(2,1)}, u32[]{:S(2)}, u32[]{:S(2)}) %collective-permute-start.2) | collective-permute-done | bytes 1179680 | tf_op jit(solution)/shard_map/ppermute | solution.py:1204
  278.5 8.5 %shard_map.257 = (bf16[256,768]{1,0:T(8,128)(2,1)}, f32[256,768]{1,0:T(8,128)}, bf16[256,768]{1,0:T(8,128)(2,1)}, bf16[512,768]{1,0:T(8,128)(2,1)}, f32[256,128]{1,0:T(8,128)}, /*index=5*/f32[512,128]{1,0:T(8,128)}) custom-call(s32[1]{0:T(128)} %constant.159.clone.1.live_ref, f32[256,768]{1,0:T(8,128)} %fusion.50.refs_0_, f32[512,1536]{1,0:T(8,128)} %fusion.refs_1_, ...), custom_call_target="tpu_custom_call" | custom-call | flops 402653184 | bytes 6971392 | tf_op jit(solution)/shard_map/pallas_call | solution.py:307
  290.7 4.7 pair_sum.5
  301.6 20.0 %plane_gather.1 = bf16[2,2,2,128,1536]{4,3,2,1,0:T(8,128)(2,1)} custom-call(bf16[128,1536]{1,0:T(8,128)(2,1)} %get-tuple-element.162.own_ref), custom_call_target="tpu_custom_call" | custom-call | flops 10000000000 | bytes 10000000 | tf_op jit(solution)/shard_map/plane_gather/pallas_call | solution.py:659
  321.6 7.0 fusion.52
  333.4 7.3 %convolution_convert_fusion.1 = bf16[1120,1536]{1,0:T(8,128)(2,1)} fusion(bf16[1024,1536]{1,0:T(8,128)(2,1)} %bitcast.43, f32[1024,1120]{0,1:T(8,128)S(1)} %fusion.52), kind=kOutput, calls=%fused_computation.2 | convolution fusion | flops 3535257600 | bytes 11173888 | tf_op jit(solution)/shard_map/dot_general | solution.py:40
  340.7 10.5 %fusion.10 = bf16[1024,1120]{0,1:T(8,128)(2,1)S(1)} fusion(f32[1024,1120]{0,1:T(8,128)} %copy-done.66, bf16[1024,1536]{1,0:T(8,128)(2,1)} %bitcast.43, bf16[1120,1536]{1,0:T(8,128)(2,1)} %all-gather.2.cloned.1.call-done), kind=kOutput, calls=%fused_computation.17 | convolution fusion | flops 3546152960 | bytes 13467648 | tf_op jit(solution)/shard_map/dot_general | solution.py:44
  351.2 6.0 convolution_convert_fusion.4
  357.2 5.8 convolution_convert_fusion.2
  365.4 10.3 %convolution_convert_fusion.5 = bf16[1024,1536]{1,0:T(8,128)(2,1)} fusion(bf16[1120,1536]{1,0:T(8,128)(2,1)} %all-gather.2.cloned.1.call-done, f32[1024,1120]{0,1:T(8,128)} %copy-done.66), kind=kOutput, calls=%fused_computation.20 | convolution fusion | flops 3535110144 | bytes 11173888 | tf_op jit(solution)/shard_map/dot_general | solution.py:36
  375.7 35.1 %plane_sum.1 = (f32[128,1536]{1,0:T(8,128)}, f32[128,1536]{1,0:T(8,128)}) custom-call(bf16[2,2,2,128,1536]{4,3,2,1,0:T(8,128)(2,1)} %bitcast.251, bf16[2,2,2,128,1536]{4,3,2,1,0:T(8,128)(2,1)} %bitcast.248), custom_call_target="tpu_custom_call" | custom-call | flops 10000000000 | bytes 10000000 | tf_op jit(solution)/shard_map/plane_sum/pallas_call | solution.py:718
  419.9 10.1 %shard_map.258 = (bf16[256,768]{1,0:T(8,128)(2,1)}, bf16[512,1536]{1,0:T(8,128)(2,1)}, f32[8,768]{1,0:T(8,128)}) custom-call(s32[1]{0:T(128)} %constant.159.clone.1.live_ref, f32[256,768]{1,0:T(8,128)} %fusion.50.refs_0_, f32[512,1536]{1,0:T(8,128)} %fusion.refs_1_, f32[4,1536]{1,0:T(4,128)} %get-tuple-element.104.refs_1_.refs_2_, ...), custom_call_target="tpu_custom_call" | custom-call | flops 1006632960 | bytes 8962048 | tf_op jit(solution)/shard_map/pallas_call | solution.py:307
  433.8 4.7 pair_sum.6
  448.7 8.8 %shard_map.259 = (bf16[256,2304]{1,0:T(8,128)(2,1)}, f32[8,768]{1,0:T(8,128)}) custom-call(s32[1]{0:T(128)S(6)} %mul.297.live_ref, f32[256,2304]{1,0:T(8,128)} %fusion.48.refs_0_, f32[4,1536]{1,0:T(4,128)} %get-tuple-element.104.refs_1_.refs_2_, f32[256,128]{1,0:T(8,128)} %constant.173.clone.refs_2_.refs_3_, f32[256,128]{1,0:T(8,128)} %constant.174.clone.refs_3_.refs_4_, ...), custom_call_target="tpu_custom_call" | custom-call | flops 503316480 | bytes 6078464 | tf_op jit(solution)/shard_map/pallas_call | solution.py:307
  457.4 6.6 fusion.54.part_ref
  494.1 4.9 convolution_convert_fusion
  499.0 15.1 %collective-permute-done.7 = bf16[4,2,96,768]{3,2,1,0:T(8,128)(2,1)S(1)} collective-permute-done((bf16[4,2,96,768]{3,2,1,0:T(8,128)(2,1)S(1)}, bf16[4,2,96,768]{3,2,1,0:T(8,128)(2,1)S(1)}, u32[]{:S(2)}, u32[]{:S(2)}) %collective-permute-start.7) | collective-permute-done | bytes 1179680 | tf_op jit(solution)/shard_map/ppermute | solution.py:1281
  515.3 21.2 %collective-permute-done.8 = bf16[4,2,96,1536]{3,2,1,0:T(8,128)(2,1)} collective-permute-done((bf16[4,2,96,1536]{3,2,1,0:T(8,128)(2,1)}, bf16[4,2,96,1536]{3,2,1,0:T(8,128)(2,1)}, u32[]{:S(2)}, u32[]{:S(2)}) %collective-permute-start.8) | collective-permute-done | bytes 2359328 | tf_op jit(solution)/shard_map/ppermute | solution.py:1280
  539.9 157.6 %reduce_weights.1 = (bf16[96,1536]{1,0:T(8,128)(2,1)}, bf16[96,3072]{1,0:T(8,128)(2,1)}, bf16[96,1536]{1,0:T(8,128)(2,1)}, bf16[96,1536]{1,0:T(8,128)(2,1)}, bf1...) custom-call(bf16[4,2,96,768]{3,2,1,0:T(8,128)(2,1)} %bitcast_add_fus, ...), custom_call_target="tpu_custom_call" | custom-call | flops 99999997952 | bytes 100000000 | tf_op jit(solution)/shard_map/reduce_weights/pallas_call | solution.py:1037
  (275 shorter events, 135.0 us)
Async XLA Ops:
  7.2 333.5 %all-gather.2.cloned.1.call-start = ((), (), s32[]{:S(2)}) async-start(), calls=%async_computation.2 | async-start | bytes 4300800 | tf_op jit(solution)/shard_map/all_gather | solution.py:1118
  7.2 171.3 %copy-start.53 = (f32[128]{0:T(128)}, f32[128]{0:T(128)S(1)}, u32[]{:S(2)}) copy-start(f32[128]{0:T(128)S(1)} %multiply_exponential_fusion) | copy-start | bytes 1540
  10.8 174.2 %copy-start.46 = (f32[128]{0:T(128)}, f32[128]{0:T(128)S(1)}, u32[]{:S(2)}) copy-start(f32[128]{0:T(128)S(1)} %fusion.35) | copy-start | bytes 1540
  185.0 31.0 %copy-start.34 = (f32[2,1536]{1,0:T(2,128)}, f32[2,1536]{1,0:T(2,128)S(1)}, u32[]{:S(2)}) copy-start(f32[2,1536]{1,0:T(2,128)S(1)} %get-tuple-element.173) | copy-start | bytes 36868
  201.7 95.0 %collective-permute-start.5 = (bf16[128,1536]{1,0:T(8,128)(2,1)S(1)}, bf16[128,1536]{1,0:T(8,128)(2,1)}, u32[]{:S(2)}, u32[]{:S(2)}) collective-permute-start(bf16[128,1536]{1,0:T(8,128)(2,1)S(1)} %fusion.17), channel_id=1, source_target_pairs={{0,6},{2,4},{4,2},{6,0},{1,7},{3,5},{5,3},{7,1},{8,14},{10,12},{12... | collective-permute-start | bytes 1179656 | tf_op jit(solution)/shard_map/ppermute | solution.py:1218
  203.2 93.5 %collective-permute-start.4 = (bf16[128,1536]{1,0:T(8,128)(2,1)S(1)}, bf16[128,1536]{1,0:T(8,128)(2,1)}, u32[]{:S(2)}, u32[]{:S(2)}) collective-permute-start(bf16[128,1536]{1,0:T(8,128)(2,1)S(1)} %fusion.17), channel_id=1, source_target_pairs={{0,4},{4,0},{1,5},{5,1},{2,6},{6,2},{3,7},{7,3},{8,12},{12,8},{9,1... | collective-permute-start | bytes 1179656 | tf_op jit(solution)/shard_map/ppermute | solution.py:1217
  204.8 335.2 %reduce-scatter.3.cloned.1.call-start = ((), (), s32[]{:S(2)}) async-start(), calls=%async_computation.3 | async-start | bytes 4423680 | tf_op jit(solution)/shard_map/reduce_scatter | solution.py:1122
  204.8 35.2 %collective-permute-start = (bf16[4,2,96,768]{3,2,1,0:T(8,128)(2,1)}, bf16[4,2,96,768]{3,2,1,0:T(8,128)(2,1)}, u32[]{:S(2)}, u32[]{:S(2)}) collective-permute-start(bf16[4,2,96,768]{3,2,1,0:T(8,128)(2,1)} %get-tuple-element.108), channel_id=1, source_target_pairs={{0,2},{2,0},{1,3},{3,1},{4,6},{6,4},{5,7},{7,5},{8,10},{10,8},{9,1... | collective-permute-start | bytes 3538952 | tf_op jit(solution)/shard_map/ppermute | solution.py:1205
  205.4 64.3 %collective-permute-start.1 = (bf16[4,2,96,768]{3,2,1,0:T(8,128)(2,1)}, bf16[4,2,96,768]{3,2,1,0:T(8,128)(2,1)}, u32[]{:S(2)}, u32[]{:S(2)}) collective-permute-start(bf16[4,2,96,768]{3,2,1,0:T(8,128)(2,1)} %get-tuple-element.110), channel_id=1, source_target_pairs={{0,4},{4,0},{1,5},{5,1},{2,6},{6,2},{3,7},{7,3},{8,12},{12,8},{9,1... | collective-permute-start | bytes 3538952 | tf_op jit(solution)/shard_map/ppermute | solution.py:1203
  206.8 58.5 %collective-permute-start.2 = (bf16[4,2,96,768]{3,2,1,0:T(8,128)(2,1)}, bf16[4,2,96,768]{3,2,1,0:T(8,128)(2,1)}, u32[]{:S(2)}, u32[]{:S(2)}) collective-permute-start(bf16[4,2,96,768]{3,2,1,0:T(8,128)(2,1)} %get-tuple-element.111), channel_id=1, source_target_pairs={{0,2},{2,0},{1,3},{3,1},{4,6},{6,4},{5,7},{7,5},{8,10},{10,8},{9,1... | collective-permute-start | bytes 3538952 | tf_op jit(solution)/shard_map/ppermute | solution.py:1204
  217.3 26.2 %copy-start.51 = (f32[128]{0:T(128)}, f32[128]{0:T(128)S(1)}, u32[]{:S(2)}) copy-start(f32[128]{0:T(128)S(1)} %broadcast_multiply_fusion.1) | copy-start | bytes 1540
  217.5 25.9 %copy-start.59 = (f32[128]{0:T(128)}, f32[128]{0:T(128)S(1)}, u32[]{:S(2)}) copy-start(f32[128]{0:T(128)S(1)} %multiply_reduce_fusion.3) | copy-start | bytes 1540
  217.5 25.9 %copy-start.55 = (f32[128]{0:T(128)}, f32[128]{0:T(128)S(1)}, u32[]{:S(2)}) copy-start(f32[128]{0:T(128)S(1)} %fusion.36) | copy-start | bytes 1540
  220.3 47.8 %copy-start.9 = (bf16[256,1536]{1,0:T(8,128)(2,1)}, bf16[256,1536]{1,0:T(8,128)(2,1)S(1)}, u32[]{:S(2)}) copy-start(bf16[256,1536]{1,0:T(8,128)(2,1)S(1)} %all_gather.16) | copy-start | bytes 2359300
  240.0 56.7 %collective-permute-start.3 = (bf16[128,1536]{1,0:T(8,128)(2,1)S(1)}, bf16[128,1536]{1,0:T(8,128)(2,1)}, u32[]{:S(2)}, u32[]{:S(2)}) collective-permute-start(bf16[128,1536]{1,0:T(8,128)(2,1)S(1)} %fusion.17), channel_id=1, source_target_pairs={{0,2},{2,0},{1,3},{3,1},{4,6},{6,4},{5,7},{7,5},{8,10},{10,8},{9,1... | collective-permute-start | bytes 1179656 | tf_op jit(solution)/shard_map/ppermute | solution.py:1216
  243.6 29.2 %copy-start.2 = (bf16[4,2,2,96,768]{4,3,2,1,0:T(8,128)(2,1)}, bf16[4,2,2,96,768]{4,3,2,1,0:T(8,128)(2,1)S(1)}, u32[]{:S(2)}) copy-start(bf16[4,2,2,96,768]{4,3,2,1,0:T(8,128)(2,1)S(1)} %copy.41) | copy-start | bytes 7077892
  299.9 28.7 %collective-permute-start.6 = (bf16[4,128,1536]{2,1,0:T(8,128)(2,1)}, bf16[4,128,1536]{2,1,0:T(8,128)(2,1)}, u32[]{:S(2)}, u32[]{:S(2)}) collective-permute-start(bf16[4,128,1536]{2,1,0:T(8,128)(2,1)} %get-tuple-element.167), channel_id=1, source_target_pairs={{0,1},{1,0},{2,3},{3,2},{4,5},{5,4},{6,7},{7,6},{8,9},{9,8},{10,11... | collective-permute-start | bytes 4718600 | tf_op jit(solution)/shard_map/ppermute | solution.py:1242
  363.0 177.0 %reduce-scatter.5.cloned.1.call-start = ((), (), s32[]{:S(2)}) async-start(), calls=%async_computation.4 | async-start | bytes 4300800 | tf_op jit(solution)/shard_map/reduce_scatter | solution.py:1122
  375.6 36.5 %copy-start.32 = (f32[2,1536]{1,0:T(2,128)S(1)}, f32[2,1536]{1,0:T(2,128)}, u32[]{:S(2)}) copy-start(f32[2,1536]{1,0:T(2,128)} %get-tuple-element.171) | copy-start | bytes 36868
  375.7 36.5 %copy-start.37 = (f32[2,1536]{1,0:T(2,128)S(1)}, f32[2,1536]{1,0:T(2,128)}, u32[]{:S(2)}) copy-start(f32[2,1536]{1,0:T(2,128)} %copy-done.36) | copy-start | bytes 36868
  482.8 53.7 %collective-permute-start.8 = (bf16[4,2,96,1536]{3,2,1,0:T(8,128)(2,1)}, bf16[4,2,96,1536]{3,2,1,0:T(8,128)(2,1)}, u32[]{:S(2)}, u32[]{:S(2)}) collective-permute-start(bf16[4,2,96,1536]{3,2,1,0:T(8,128)(2,1)} %dynamic-slice_bitcast_fusion), channel_id=1, source_target_pairs={{0,4},{4,0},{1,5},{5,1},{2,6},{6,2},{3,7},{7,3},{8,12},{12,8},{9,1... | collective-permute-start | bytes 7077896 | tf_op jit(solution)/shard_map/ppermute | solution.py:1280
  486.0 28.1 %collective-permute-start.7 = (bf16[4,2,96,768]{3,2,1,0:T(8,128)(2,1)S(1)}, bf16[4,2,96,768]{3,2,1,0:T(8,128)(2,1)S(1)}, u32[]{:S(2)}, u32[]{:S(2)}) collective-permute-start(bf16[4,2,96,768]{3,2,1,0:T(8,128)(2,1)S(1)} %dynamic-slice_bitcast_fusion.1), channel_id=1, source_target_pairs={{0,2},{2,0},{1,3},{3,1},{4,6},{6,4},{5,7},{7,5},{8,10},{10,8},{9,1... | collective-permute-start | bytes 3538952 | tf_op jit(solution)/shard_map/ppermute | solution.py:1281
  491.8 44.8 %slice-start = ((s8[4718592]{0:T(1024)(128)(4,1)}), s8[4194304]{0:T(1024)(128)(4,1)S(1)}, s32[]{:S(2)}) async-start(s8[4718592]{0:T(1024)(128)(4,1)} %bitcast.215), calls=%async_computation.5 | async-start | bytes 8388608
  494.1 42.4 %slice-start.1 = ((s8[4718592]{0:T(1024)(128)(4,1)}), s8[524288]{0:T(1024)(128)(4,1)S(1)}, s32[]{:S(2)}) async-start(s8[4718592]{0:T(1024)(128)(4,1)} %bitcast.215), calls=%async_computation.6 | async-start | bytes 1048576
  (57 other events, 201.7 us)
Sparse Core Ops, SparseCore 0:
  204.9 66.4 all-gather.1
  363.1 64.8 reduce-scatter.2
  445.3 63.2 reduce-scatter.4
